TPU v7x, 256 devices: a whole 4x4x8 slice. The times are simulated.
256 devices in a mesh: gx: 16 (over x_lo, z), gy: 2 (over core), gz: 8 (over y, x_hi).
Axes of the slice: x: 4 (x_hi: 2, x_lo: 2; x = x_hi * 2 + x_lo), y: 4, z: 8, core: 2. Of those that a mesh axis runs over, the one named last changes fastest.
Arguments:
- features: bfloat16 [16, 2, 8, 128, 512], P('gx', 'gy', 'gz'), may hold values from -6 to 6
- fraction: bfloat16 [16, 2, 8, 3, 128], P('gx', 'gy', 'gz'), may hold values from 0 to 0.98828125
- cell_index: int32 [16, 2, 8, 3, 128], P('gx', 'gy', 'gz'), may hold values from 0 to 127, as said below
- species: int32 [16, 2, 8, 128], P('gx', 'gy', 'gz'), may hold values from 0 to 1
- octant_rows: int32 [16, 2, 8, 8, 14], P('gx', 'gy', 'gz'), may hold values from 0 to 127, as said below
- neighbours: int32 [16, 2, 8, 16, 128], P('gx', 'gy', 'gz'), may hold values from 0 to 912, as said below
- radial_in: bfloat16 [2, 8, 64], replicated, may hold values from -2 to 2
- radial_out: bfloat16 [2, 64, 512], replicated, may hold values from -1.5 to 1.5
- mix_weight: bfloat16 [2, 2, 128, 128], replicated, may hold values from -0.5 to 0.5
- readout: bfloat16 [128, 2], replicated, may hold values from -0.125 to 0.125
- species_table: float32 [2, 2], replicated, may hold values from -4 to 4
Outputs:
- new_features: bfloat16 [16, 2, 8, 128, 512], P('gx', 'gy', 'gz')
- site_energy: float32 [16, 2, 8, 128], P('gx', 'gy', 'gz')
- recip_force: float32 [16, 2, 8, 3, 128], P('gx', 'gy', 'gz')
Inputs may be any that keep to these rules, and one draw needn't show every extreme that they name: `cell_index`: component x lies below 16, component y below 128, component z below 32. `octant_rows`: each octant's list holds 14 different atoms of the domain. `neighbours`: entries are rows of the domain's table; 912 is an empty slot; an atom never lists itself, and the other entries of a column are different; the cell of a listed row (cell_index plus its shift) lies within 8 cells of the atom's cell.
All inputs are finite; a program needn't handle non-finite values.
Results may differ from a plain program's by a relative error of at most 0.0051.
Values may be sent and summed in bfloat16 or wider, within the bound.
No kernel may reach another device: no remote copies, remote signals or barrier semaphores. Data moves between devices by JAX's collectives and lax.ppermute only.
A program may use at most 64 MiB of HBM per device.

v0:
```python
import math

import jax
import jax.numpy as jnp
import numpy as np
from jax import lax
from jax.sharding import PartitionSpec as P

C = 128
NB = 8
LAYERS = 2
NEIGH = 16
ENV = 7
MESH = 256


COULOMB = 4.0
EWALD = 0.7
HIGHEST_PRECISION = lax.Precision.HIGHEST


def extended_2(shard, sides, width):
    for axis, dim in sides:
        count, length = (lax.axis_size(axis), shard.shape[dim])
        up = [(i, (i + 1) % count) for i in range(count)]
        down = [(j, i) for i, j in up]
        last = lax.slice_in_dim(shard, length - width, length, axis=dim)
        leading = lax.slice_in_dim(shard, 0, width, axis=dim)
        before = lax.ppermute(last, axis, up)
        after = lax.ppermute(leading, axis, down)
        shard = jnp.concatenate([before, shard, after], axis=dim)
    return shard


def in_blocks(shard, dim, count):
    lengths = shard.shape
    pieces = shard.reshape(*lengths[:dim], count, lengths[dim] // count, *lengths[dim + 1 :])
    return jnp.moveaxis(pieces, dim, 0)


def summed_on_arrival(shard, axis, dim):
    pieces = in_blocks(shard, dim, lax.axis_size(axis))
    arrived = lax.all_to_all(pieces, axis, split_axis=0, concat_axis=0, tiled=True)
    return arrived.sum(axis=0)


def from_partner(block, axis, bit):
    count = lax.axis_size(axis)
    route = []
    for low in range(count):
        high = low | 1 << bit
        if high != low and high < count:
            route += [(low, high), (high, low)]
    return lax.ppermute(block, axis, route)


def outer_cells():
    found = []
    for first in range(4):
        for second in range(4):
            for third in range(4):
                if 0 < first < 3 and 0 < second < 3 and (0 < third < 3):
                    continue
                found.append((first, second, third))
    return found


def offset_of(coord):
    return -1 if coord == 0 else 1 if coord == 3 else 0


def spline(fraction_in):
    lower_t = 1.0 - fraction_in
    weights = jnp.stack(
        [
            lower_t * lower_t * lower_t / 6.0,
            (3.0 * fraction_in * fraction_in * fraction_in - 6.0 * fraction_in * fraction_in + 4.0)
            / 6.0,
            (
                -3.0 * fraction_in * fraction_in * fraction_in
                + 3.0 * fraction_in * fraction_in
                + 3.0 * fraction_in
                + 1.0
            )
            / 6.0,
            fraction_in * fraction_in * fraction_in / 6.0,
        ]
    )
    slopes = jnp.stack(
        [
            -0.5 * lower_t * lower_t,
            0.5 * (3.0 * fraction_in * fraction_in - 4.0 * fraction_in),
            0.5 * (-3.0 * fraction_in * fraction_in + 2.0 * fraction_in + 1.0),
            0.5 * fraction_in * fraction_in,
        ]
    )
    return (weights, slopes)


def frequency(waves):
    signed = jnp.where(waves <= MESH // 2, waves, waves - MESH).astype(jnp.float32) / MESH
    modulus = 9.0 / jnp.square(2.0 + jnp.cos(waves.astype(jnp.float32) * (2.0 * math.pi / MESH)))
    return (signed, modulus)


def influence(wave_y, wave_z, wave_x):
    freq_y, modul_y = frequency(wave_y)
    freq_z, modul_z = frequency(wave_z)
    freq_x, modul_x = frequency(wave_x)
    wave_square = (
        jnp.square(freq_x)[None, None, :]
        + jnp.square(freq_y)[:, None, None]
        + jnp.square(freq_z)[None, :, None]
    )
    positive = wave_square > 0.0
    gaussian = jnp.exp(-(math.pi * math.pi / (EWALD * EWALD)) * wave_square)
    kernel = jnp.where(positive, gaussian / jnp.where(positive, wave_square, 1.0), 0.0)
    moduli = modul_x[None, None, :] * modul_y[:, None, None] * modul_z[None, :, None]
    return kernel * moduli * (COULOMB / (math.pi * MESH**3))


def interact(current, lookup, places, located, links, radial_in, radial_out, mix_weight):
    atom_count = current.shape[0]
    gathered = lookup[links].astype(jnp.float32)
    displace = places[links] - located[None]
    length_sq = jnp.sum(displace * displace, axis=-1)
    distance = jnp.sqrt(length_sq)
    direction = displace / jnp.sqrt(length_sq + 1.0)[..., None]
    spacing = ENV / (NB - 1)
    centres = jnp.arange(NB, dtype=jnp.float32) * spacing
    envelope = jnp.square(jnp.maximum(1.0 - length_sq / (ENV * ENV), 0.0))
    basis_set = (
        jnp.exp(-jnp.square((distance[..., None] - centres) / spacing)) * envelope[..., None]
    )
    edge_count = NEIGH * atom_count
    hidden = jax.nn.silu(
        jnp.dot(
            basis_set.reshape(edge_count, NB).astype(jnp.bfloat16),
            radial_in,
            preferred_element_type=jnp.float32,
        )
    ).astype(jnp.bfloat16)
    radial = jnp.dot(hidden, radial_out, preferred_element_type=jnp.float32).reshape(
        NEIGH, atom_count, 4 * C
    )
    scalars = gathered[..., :C]
    vectors = gathered[..., C:].reshape(NEIGH, atom_count, 3, C)
    first_path = radial[..., :C]
    second_path = radial[..., C : 2 * C]
    third_path = radial[..., 2 * C : 3 * C]
    fourth_path = radial[..., 3 * C :]
    projected = jnp.sum(direction[..., None] * vectors, axis=2)
    inverse_root = 1.0 / math.sqrt(NEIGH)
    scalar_message = jnp.sum(first_path * scalars + second_path * projected, axis=0) * inverse_root
    scaled_path = third_path * scalars
    vector_message = (
        jnp.einsum("kad,kac->adc", direction, scaled_path, precision=HIGHEST_PRECISION)
        + jnp.sum(fourth_path[:, :, None, :] * vectors, axis=0)
    ) * inverse_root
    previous = current.astype(jnp.float32)
    scalar_new = previous[:, :C] + jax.nn.silu(
        jnp.dot(
            scalar_message.astype(jnp.bfloat16), mix_weight[0], preferred_element_type=jnp.float32
        )
    )
    vector_new = previous[:, C:] + jnp.dot(
        vector_message.reshape(atom_count * 3, C).astype(jnp.bfloat16),
        mix_weight[1],
        preferred_element_type=jnp.float32,
    ).reshape(atom_count, 3 * C)
    return jnp.concatenate([scalar_new, vector_new], axis=1).astype(jnp.bfloat16)


def ghost_rows(buffer):
    return extended_2(buffer, (("gx", 0), ("gy", 1), ("gz", 2)), 1)


def mesh_rim(mesh_block):
    return extended_2(mesh_block, (("gx", 1), ("gy", 0), ("gz", 2)), 2)


def along_gy(term, row_count):
    return summed_on_arrival(term(jnp.int32(0), row_count * lax.axis_size("gy")), "gy", 0)


def across_gz(blocks):
    return lax.all_to_all(blocks, "gz", split_axis=0, concat_axis=0, tiled=True)


def across_gx(blocks):
    return lax.all_to_all(blocks, "gx", split_axis=0, concat_axis=0, tiled=True)


def outer_pick(extended):
    flattened = extended.reshape(64, -1)
    chosen = np.array(
        [16 * corner[0] + 4 * corner[1] + corner[2] for corner in outer_cells()], np.int32
    )
    return flattened[chosen]


def fold_rim(bordered, axis_dim):
    inner = bordered.shape[axis_dim] - 8
    middle = lax.slice_in_dim(bordered, 4, inner + 4, axis=axis_dim)
    lower = lax.slice_in_dim(bordered, 0, 2, axis=axis_dim)
    higher = lax.slice_in_dim(bordered, inner + 6, inner + 8, axis=axis_dim)
    shape_pad = list(lower.shape)
    shape_pad[axis_dim] = inner - 2
    padding = jnp.zeros(shape_pad, bordered.dtype)
    return (
        middle
        + jnp.concatenate([lower, padding], axis=axis_dim)
        + jnp.concatenate([padding, higher], axis=axis_dim)
    )


def product(left, right):
    return jnp.dot(left, right, precision=HIGHEST_PRECISION, preferred_element_type=jnp.float32)


def phases(left, right):
    turns = left[:, None] * right[None, :] % MESH
    angle = turns.astype(jnp.float32) * (2.0 * math.pi / MESH)
    return (jnp.cos(angle), jnp.sin(angle))


def along_last(data, cosine_table, sine_table, inverse):
    flattened = data.reshape(-1, data.shape[-1])
    with_cosine = product(flattened, cosine_table).reshape(data.shape)
    with_sine = product(flattened, sine_table).reshape(data.shape)
    if inverse:
        real_part = with_cosine[:, 0] - with_sine[:, 1]
        imag_part = with_cosine[:, 1] + with_sine[:, 0]
    else:
        real_part = with_cosine[:, 0] + with_sine[:, 1]
        imag_part = with_cosine[:, 1] - with_sine[:, 0]
    return jnp.stack([real_part, imag_part], axis=1)


def spline_rows(coefficient, cell_row, span):
    slot_index = jnp.arange(span + 4, dtype=jnp.int32)
    summed = jnp.zeros((cell_row.shape[0], span + 4), jnp.float32)
    for offset in range(4):
        summed = summed + coefficient[offset][:, None] * (
            slot_index[None, :] == (cell_row + 1 + offset)[:, None]
        ).astype(jnp.float32)
    return summed


def per_device(
    features,
    fraction,
    cell_index,
    species,
    octant_rows,
    neighbours,
    radial_in,
    radial_out,
    mix_weight,
    readout,
    species_table,
):
    current = features[0, 0, 0]
    fraction_here = fraction[0, 0, 0]
    cells_here = cell_index[0, 0, 0]
    kinds = species[0, 0, 0]
    chosen_rows = octant_rows[0, 0, 0].reshape(-1)
    links = neighbours[0, 0, 0]
    atom_count, feat_width = current.shape
    ghost_count = chosen_rows.shape[0] // 8
    count_x = lax.axis_size("gx")
    count_y = lax.axis_size("gy")
    count_z = lax.axis_size("gz")
    span_x = MESH // count_x
    span_y = MESH // count_y
    span_z = MESH // count_z
    located = jnp.transpose(cells_here.astype(jnp.float32)) + jnp.transpose(
        fraction_here.astype(jnp.float32)
    )
    geometry = jnp.concatenate([fraction_here, cells_here.astype(jnp.bfloat16)], axis=0)[
        :, chosen_rows
    ]
    geometry = jnp.transpose(geometry.reshape(6, 8, ghost_count), (1, 0, 2)).reshape(
        8, 6 * ghost_count
    )
    outgoing = current[chosen_rows].reshape(8, ghost_count * feat_width)
    arrived = outer_pick(
        ghost_rows(jnp.concatenate([outgoing, geometry], axis=1).reshape(2, 2, 2, -1))
    )
    split_at = ghost_count * feat_width
    ghost_feats = arrived[:, :split_at].reshape(56 * ghost_count, feat_width)
    ghost_geometry = arrived[:, split_at:].reshape(56, 6, ghost_count).astype(jnp.float32)
    shift_table = np.array(
        [[offset_of(coord) for coord in corner] for corner in outer_cells()], np.float32
    )
    shifts = jnp.asarray(shift_table) * jnp.array([span_x, span_y, span_z], jnp.float32)
    ghost_places = ghost_geometry[:, 3:6] + shifts[:, :, None] + ghost_geometry[:, 0:3]
    places = jnp.concatenate(
        [
            located,
            jnp.transpose(ghost_places, (0, 2, 1)).reshape(-1, 3),
            jnp.zeros((1, 3), jnp.float32),
        ],
        axis=0,
    )
    block_rows = min(64, atom_count)
    block_count = atom_count // block_rows
    for layer_index in range(LAYERS):
        if layer_index > 0:
            outgoing = current[chosen_rows].reshape(2, 2, 2, ghost_count * feat_width)
            ghost_feats = outer_pick(ghost_rows(outgoing)).reshape(56 * ghost_count, feat_width)
        lookup = jnp.concatenate(
            [current, ghost_feats, jnp.zeros((1, feat_width), jnp.bfloat16)], axis=0
        )

        def one_block(block_index, lookup=lookup, layer_index=layer_index, current=current):
            start = block_index * block_rows
            return interact(
                lax.dynamic_slice_in_dim(current, start, block_rows, 0),
                lookup,
                places,
                lax.dynamic_slice_in_dim(located, start, block_rows, 0),
                lax.dynamic_slice_in_dim(links, start, block_rows, 1),
                radial_in[layer_index],
                radial_out[layer_index],
                mix_weight[layer_index],
            )

        current = lax.map(one_block, jnp.arange(block_count, dtype=jnp.int32)).reshape(
            atom_count, feat_width
        )
    head_out = jnp.dot(current[:, :C], readout, preferred_element_type=jnp.float32)
    one_hot = (
        kinds[:, None] == jnp.arange(species_table.shape[0], dtype=jnp.int32)[None, :]
    ).astype(jnp.float32)
    species_term = jnp.dot(
        one_hot, species_table, precision=HIGHEST_PRECISION, preferred_element_type=jnp.float32
    )
    base_energy = head_out[:, 0] + species_term[:, 0]
    charge = head_out[:, 1] + species_term[:, 1]
    weights, slopes = spline(fraction_here.astype(jnp.float32))
    weight_x = spline_rows(weights[:, 0], cells_here[0], span_x)
    weight_y = spline_rows(weights[:, 1], cells_here[1], span_y)
    weight_z = spline_rows(weights[:, 2], cells_here[2], span_z)
    plane_xz = (weight_x[:, :, None] * weight_z[:, None, :]).reshape(atom_count, -1)
    spread = product(jnp.transpose(weight_y * charge[:, None]), plane_xz).reshape(
        span_y + 4, span_x + 4, span_z + 4
    )
    charge_mesh = fold_rim(fold_rim(fold_rim(mesh_rim(spread), 0), 1), 2)
    index_x = lax.axis_index("gx")
    index_y = lax.axis_index("gy")
    index_z = lax.axis_index("gz")
    flattened = charge_mesh.reshape(span_y, span_x * span_z)
    own_rows = index_y * span_y + jnp.arange(span_y, dtype=jnp.int32)
    partner = from_partner(flattened, "gy", 0)
    partner_rows = (1 - index_y) * span_y + jnp.arange(span_y, dtype=jnp.int32)
    cosine_own, sine_own = phases(own_rows, own_rows)
    cosine_other, sine_other = phases(own_rows, partner_rows)
    real_part = product(cosine_own, flattened) + product(cosine_other, partner)
    imag_part = -(product(sine_own, flattened) + product(sine_other, partner))
    spectrum = jnp.stack([real_part, imag_part], axis=1)
    wave_rows = span_y // count_z
    full_waves = jnp.arange(MESH, dtype=jnp.int32)
    cosine_full, sine_full = phases(full_waves, full_waves)
    received = across_gz(spectrum.reshape(count_z, wave_rows, 2, span_x, span_z))
    lines_z = jnp.transpose(received, (1, 2, 3, 0, 4)).reshape(wave_rows, 2, span_x, MESH)
    lines_z = along_last(lines_z, cosine_full, sine_full, False)
    sending = jnp.transpose(lines_z.reshape(wave_rows, 2, span_x, count_x, span_x), (3, 0, 1, 2, 4))
    received = across_gx(sending)
    lines_x = jnp.transpose(received, (1, 2, 4, 0, 3)).reshape(wave_rows, 2, span_x, MESH)
    lines_x = along_last(lines_x, cosine_full, sine_full, False)
    wave_y = index_y * span_y + index_z * wave_rows + jnp.arange(wave_rows, dtype=jnp.int32)
    wave_z = index_x * span_x + jnp.arange(span_x, dtype=jnp.int32)
    kernel = influence(wave_y, wave_z, full_waves)
    scaled = lines_x * kernel[:, None]
    lines_x = along_last(scaled, cosine_full, sine_full, True)
    sending = jnp.transpose(lines_x.reshape(wave_rows, 2, span_x, count_x, span_x), (3, 0, 1, 2, 4))
    received = across_gx(sending)
    lines_z = jnp.transpose(received, (1, 2, 4, 0, 3)).reshape(wave_rows, 2, span_x, MESH)
    lines_z = along_last(lines_z, cosine_full, sine_full, True)
    sending = jnp.transpose(lines_z.reshape(wave_rows, 2, span_x, count_z, span_z), (3, 0, 1, 2, 4))
    returned = across_gz(sending).reshape(span_y, 2, span_x * span_z)

    def backward_rows(start, row_count):
        spots = jnp.arange(row_count, dtype=jnp.int32)
        cosine_table, sine_table = phases(spots, own_rows)
        return product(cosine_table, returned[:, 0]) - product(sine_table, returned[:, 1])

    potential = along_gy(backward_rows, span_y).reshape(span_y, span_x, span_z)
    bordered = mesh_rim(potential).reshape(span_y + 4, -1)
    slope_x = spline_rows(slopes[:, 0], cells_here[0], span_x)
    slope_y = spline_rows(slopes[:, 1], cells_here[1], span_y)
    slope_z = spline_rows(slopes[:, 2], cells_here[2], span_z)
    level_y = product(weight_y, bordered)
    level_slope = product(slope_y, bordered)
    potential_at = jnp.sum(level_y * plane_xz, axis=1)
    field_x = -jnp.sum(
        level_y * (slope_x[:, :, None] * weight_z[:, None, :]).reshape(atom_count, -1), axis=1
    )
    field_y = -jnp.sum(level_slope * plane_xz, axis=1)
    field_z = -jnp.sum(
        level_y * (weight_x[:, :, None] * slope_z[:, None, :]).reshape(atom_count, -1), axis=1
    )
    recip_force = charge[None, :] * jnp.stack([field_x, field_y, field_z])
    site_energy = base_energy + 0.5 * charge * potential_at
    return (current[None, None, None], site_energy[None, None, None], recip_force[None, None, None])


def solution(mesh):
    in_specs = (
        P("gx", "gy", "gz", None, None),
        P("gx", "gy", "gz", None, None),
        P("gx", "gy", "gz", None, None),
        P("gx", "gy", "gz", None),
        P("gx", "gy", "gz", None, None),
        P("gx", "gy", "gz", None, None),
        P(),
        P(),
        P(),
        P(),
        P(),
    )
    out_specs = (
        P("gx", "gy", "gz", None, None),
        P("gx", "gy", "gz", None),
        P("gx", "gy", "gz", None, None),
    )
    return jax.shard_map(
        per_device, mesh=mesh, in_specs=in_specs, out_specs=out_specs, check_vma=False
    )
```

profile of v0, /device:TPU:1, one launch (start us, length us, event | category | flops | bytes accessed | tf_op | source)
XLA Modules:
  0.0 535.0 jit_solution(12342076762261325509)
XLA Ops:
  6.1 7.4 %collective-permute-start.1 = (bf16[1,2,2,7252]{3,2,1,0:T(2,128)(2,1)S(1)}, bf16[1,2,2,7252]{3,2,1,0:T(2,128)(2,1)S(1)}, u32[]{:S(2)}, u32[]{:S(2)}) collective-permute-start(bf16[1,2,2,7252]{3,2,1,0:T(2,128)(2,1)S(1)} %slice.445), channel_id=1, source_target_pairs={{16,0},{32,16},{48,32},{64,48},{80,64},{96,80},{112,96},{128,112},... | collective-permute-start | bytes 174056 | tf_op jit(solution)/shard_map/ppermute | solution.py:30
  23.8 5.0 collective-permute-start.5
  30.5 8.2 %collective-permute-done.5 = bf16[4,4,1,7252]{3,2,1,0:T(2,128)(2,1)S(1)} collective-permute-done((bf16[4,4,1,7252]{3,2,1,0:T(2,128)(2,1)S(1)}, bf16[4,4,1,7252]{3,2,1,0:T(2,128)(2,1)S(1)}, u32[]{:S(2)}, u32[]{:S(2)}) %collective-permute-start.5) | collective-permute-done | bytes 232096 | tf_op jit(solution)/shard_map/ppermute | solution.py:30
  38.6 11.3 %collective-permute-done.4 = bf16[4,4,1,7252]{3,2,1,0:T(2,128)(2,1)S(1)} collective-permute-done((bf16[4,4,1,7252]{3,2,1,0:T(2,128)(2,1)S(1)}, bf16[4,4,1,7252]{3,2,1,0:T(2,128)(2,1)S(1)}, u32[]{:S(2)}, u32[]{:S(2)}) %collective-permute-start.4) | collective-permute-done | bytes 232096 | tf_op jit(solution)/shard_map/ppermute | solution.py:29
  58.3 106.5 %while.20 = (s32[]{:T(128)}, bf16[2,64,512]{2,1,0:T(8,128)(2,1)}, s32[2]{0:T(128)}, bf16[128,512]{1,0:T(8,128)(2,1)}, s32[16,128]{1,0:T(8,128)S(1)}, /*index=5*/...) while((s32[]{:T(128)}, bf16[2,64,512]{2,1,0:T(8,128)(2,1)}, ...), condition=%wide.region_5.6_spmd, body=%wide.region_0.5_spmd.sunk | while | flops 84597768 | bytes 34620808 | solution.py:329
  60.3 5.1 gather_fusion
  68.2 3.6 reshape.1590
  71.8 4.0 gather_fusion.1
  88.5 3.6 multiply_reduce_fusion.16
  99.0 3.8 mul.1854
  113.6 5.1 gather_fusion
  121.5 3.6 reshape.1590
  125.1 4.0 gather_fusion.1
  141.7 3.6 multiply_reduce_fusion.16
  152.2 3.8 mul.1854
  167.7 3.6 collective-permute-start.7
  184.5 6.7 %collective-permute-done.11 = bf16[4,4,1,7168]{3,2,1,0:T(2,128)(2,1)S(1)} collective-permute-done((bf16[4,4,1,7168]{3,2,1,0:T(2,128)(2,1)S(1)}, bf16[4,4,1,7168]{3,2,1,0:T(2,128)(2,1)S(1)}, u32[]{:S(2)}, u32[]{:S(2)}) %collective-permute-start.11) | collective-permute-done | bytes 229408 | tf_op jit(solution)/shard_map/ppermute | solution.py:30
  191.2 10.0 %collective-permute-done.10 = bf16[4,4,1,7168]{3,2,1,0:T(2,128)(2,1)S(1)} collective-permute-done((bf16[4,4,1,7168]{3,2,1,0:T(2,128)(2,1)S(1)}, bf16[4,4,1,7168]{3,2,1,0:T(2,128)(2,1)S(1)}, u32[]{:S(2)}, u32[]{:S(2)}) %collective-permute-start.10) | collective-permute-done | bytes 229408 | tf_op jit(solution)/shard_map/ppermute | solution.py:29
  206.3 106.4 %while.21 = (s32[]{:T(128)}, bf16[2,64,512]{2,1,0:T(8,128)(2,1)}, s32[2]{0:T(128)S(1)}, bf16[128,512]{1,0:T(8,128)(2,1)S(1)}, s32[16,128]{1,0:T(8,128)S(1)}, /*i...) while((s32[]{:T(128)}, bf16[2,64,512]{2,1,0:T(8,128)(2,1)}, ...), condition=%wide.region_11.12_spmd, body=%wide.region_6.11_spmd.sunk | while | flops 84597768 | bytes 35137028 | solution.py:329
  207.6 5.1 gather_fusion.2
  215.5 3.6 reshape.1597
  219.1 4.0 gather_fusion.3
  235.8 3.6 multiply_reduce_fusion.19
  246.9 3.8 mul.1869
  260.8 5.1 gather_fusion.2
  268.7 3.6 reshape.1597
  272.3 4.0 gather_fusion.3
  289.0 3.6 multiply_reduce_fusion.19
  300.1 3.8 mul.1869
  316.2 4.3 collective-permute-start.13
  321.9 4.1 collective-permute-done.12
  335.7 4.4 collective-permute-done.16
  351.0 3.7 all-to-all-start
  354.7 11.4 %all-to-all-done = f32[8,1,16384]{2,1,0:T(1,128)S(1)} async-done(((f32[8,1,16384]{2,1,0:T(1,128)}), f32[8,1,16384]{2,1,0:T(1,128)S(1)}, u32[]{:S(2)}, u32[]{:S(2)}) %all-to-all-start) | async-done | bytes 524320 | tf_op jit(solution)/shard_map/all_to_all | solution.py:187
  381.6 4.2 reshape.1565
  385.8 4.0 all-to-all-start.1
  390.2 12.9 %all-to-all-done.1 = f32[16,1,8192]{2,1,0:T(1,128)S(1)} async-done(((f32[16,1,8192]{2,1,0:T(1,128)}), f32[16,1,8192]{2,1,0:T(1,128)S(1)}, u32[]{:S(2)}, u32[]{:S(2)}) %all-to-all-start.1) | async-done | bytes 524320 | tf_op jit(solution)/shard_map/all_to_all | solution.py:191
  408.0 4.7 bitcast_bitcast_fusion.1
  412.6 5.6 %copy.136 = f32[16,2,16,16,16]{4,3,2,1,0:T(8,128)} copy(f32[16,2,16,16,16]{2,4,0,1,3:T(8,128)} %bitcast_bitcast_fusion.1) | data formatting | bytes 1048576 | tf_op jit(solution)/shard_map/transpose | solution.py:370
  418.2 3.5 dot_general.113
  435.3 3.5 reshape.1567
  438.8 19.1 %all_to_all.25 = f32[16,1,8192]{2,1,0:T(1,128)S(1)} all-to-all(f32[16,1,8192]{2,1,0:T(1,128)S(1)} %reshape.1567), channel_id=1, replica_groups=mesh['gx'=16,'gy'=2,'gz'=8] {'gx'}, dimensions={0} | all-to-all | bytes 1048576 | tf_op jit(solution)/shard_map/all_to_all | solution.py:191
  462.7 4.7 bitcast_bitcast_fusion
  467.4 5.6 %copy.139 = f32[16,2,16,16,16]{4,3,2,1,0:T(8,128)} copy(f32[16,2,16,16,16]{2,4,0,1,3:T(8,128)} %bitcast_bitcast_fusion) | data formatting | bytes 1048576 | tf_op jit(solution)/shard_map/transpose | solution.py:379
  481.7 13.2 %all_to_all.26 = f32[8,1,16384]{2,1,0:T(1,128)S(1)} all-to-all(f32[8,1,16384]{2,1,0:T(1,128)S(1)} %reshape.1569), channel_id=1, replica_groups=mesh['gx'=16,'gy'=2,'gz'=8] {'gz'}, dimensions={0} | all-to-all | bytes 1048576 | tf_op jit(solution)/shard_map/all_to_all | solution.py:187
  503.5 8.2 %all_to_all.27 = f32[2,128,512]{2,1,0:T(8,128)S(1)} all-to-all(f32[2,128,512]{2,1,0:T(8,128)S(1)} %bitcast.377), channel_id=1, replica_groups=mesh['gx'=16,'gy'=2,'gz'=8] {'gy'}, dimensions={0} | all-to-all | bytes 1048576 | tf_op jit(solution)/shard_map/all_to_all | solution.py:43
  515.2 3.9 collective-permute-done.19
  527.5 3.9 collective-permute-done.23
  (478 shorter events, 273.0 us)
Async XLA Ops:
  0.6 182.4 %copy-start = (f32[2,2]{1,0:T(2,128)S(1)}, f32[2,2]{1,0:T(2,128)}, u32[]{:S(2)}) copy-start(f32[2,2]{1,0:T(2,128)} %param.31) | copy-start | bytes 52
  0.6 14.9 %copy-start.23 = (s32[1,1,1,3,128]{4,2,3,1,0:T(1,128)S(1)}, s32[1,1,1,3,128]{4,2,3,1,0:T(1,128)}, u32[]{:S(2)}) copy-start(s32[1,1,1,3,128]{4,2,3,1,0:T(1,128)} %param.23) | copy-start | bytes 4612
  0.7 13.0 %copy-start.24 = (bf16[1,1,1,3,128]{4,3,2,1,0:T(4,128)(2,1)S(1)}, bf16[1,1,1,3,128]{4,3,2,1,0:T(4,128)(2,1)}, u32[]{:S(2)}) copy-start(bf16[1,1,1,3,128]{4,3,2,1,0:T(4,128)(2,1)} %param.22) | copy-start | bytes 2308
  6.1 22.8 %copy-start.55 = (s32[56]{0:T(128)S(1)}, s32[56]{0:T(128)}, u32[]{:S(2)}) copy-start(s32[56]{0:T(128)} %constant.255) | copy-start | bytes 676
  6.1 10.2 %collective-permute-start.1 = (bf16[1,2,2,7252]{3,2,1,0:T(2,128)(2,1)S(1)}, bf16[1,2,2,7252]{3,2,1,0:T(2,128)(2,1)S(1)}, u32[]{:S(2)}, u32[]{:S(2)}) collective-permute-start(bf16[1,2,2,7252]{3,2,1,0:T(2,128)(2,1)S(1)} %slice.445), channel_id=1, source_target_pairs={{16,0},{32,16},{48,32},{64,48},{80,64},{96,80},{112,96},{128,112},... | collective-permute-start | bytes 174056 | tf_op jit(solution)/shard_map/ppermute | solution.py:30
  13.6 5.2 collective-permute-start
  19.2 3.2 collective-permute-start.3
  21.4 1.3 collective-permute-start.2
  23.8 14.9 %collective-permute-start.5 = (bf16[4,4,1,7252]{3,2,1,0:T(2,128)(2,1)S(1)}, bf16[4,4,1,7252]{3,2,1,0:T(2,128)(2,1)S(1)}, u32[]{:S(2)}, u32[]{:S(2)}) collective-permute-start(bf16[4,4,1,7252]{3,2,1,0:T(2,128)(2,1)S(1)} %get-tuple-element.273), channel_id=1, source_target_pairs={{1,0},{2,1},{3,2},{4,3},{5,4},{6,5},{7,6},{0,7},{9,8},{10,9},{11,1... | collective-permute-start | bytes 696200 | tf_op jit(solution)/shard_map/ppermute | solution.py:30
  28.7 21.1 %collective-permute-start.4 = (bf16[4,4,1,7252]{3,2,1,0:T(2,128)(2,1)S(1)}, bf16[4,4,1,7252]{3,2,1,0:T(2,128)(2,1)S(1)}, u32[]{:S(2)}, u32[]{:S(2)}) collective-permute-start(bf16[4,4,1,7252]{3,2,1,0:T(2,128)(2,1)S(1)} %get-tuple-element.272), channel_id=1, source_target_pairs={{0,1},{1,2},{2,3},{3,4},{4,5},{5,6},{6,7},{7,0},{8,9},{9,10},{10,1... | collective-permute-start | bytes 696200 | tf_op jit(solution)/shard_map/ppermute | solution.py:29
  28.9 24.1 %copy-start.30 = (s32[1024]{0:T(1024)}, s32[1024]{0:T(1024)S(1)}, u32[]{:S(2)}) copy-start(s32[1024]{0:T(1024)S(1)} %pad_clamp_fusion) | copy-start | bytes 12292
  29.9 26.0 %copy-start.21 = (bf16[913]{0:T(1024)(128)(2,1)}, bf16[913]{0:T(1024)(128)(2,1)S(1)}, u32[]{:S(2)}) copy-start(bf16[913]{0:T(1024)(128)(2,1)S(1)} %pad.66.clone) | copy-start | bytes 5482
  164.7 10.4 %copy-start.39 = (f32[128]{0:T(128)S(1)}, f32[128]{0:T(128)}, u32[]{:S(2)}) copy-start(f32[128]{0:T(128)} %get-tuple-element.302) | copy-start | bytes 1540
  164.8 10.4 %copy-start.40 = (f32[128]{0:T(128)S(1)}, f32[128]{0:T(128)}, u32[]{:S(2)}) copy-start(f32[128]{0:T(128)} %get-tuple-element.339) | copy-start | bytes 1540
  164.8 10.4 %copy-start.41 = (f32[128]{0:T(128)S(1)}, f32[128]{0:T(128)}, u32[]{:S(2)}) copy-start(f32[128]{0:T(128)} %get-tuple-element.296) | copy-start | bytes 1540
  164.8 10.4 %copy-start.42 = (f32[128]{0:T(128)S(1)}, f32[128]{0:T(128)}, u32[]{:S(2)}) copy-start(f32[128]{0:T(128)} %get-tuple-element.342) | copy-start | bytes 1540
  164.8 10.4 %copy-start.43 = (f32[128]{0:T(128)S(1)}, f32[128]{0:T(128)}, u32[]{:S(2)}) copy-start(f32[128]{0:T(128)} %get-tuple-element.318) | copy-start | bytes 1540
  164.8 10.4 %copy-start.44 = (f32[128]{0:T(128)S(1)}, f32[128]{0:T(128)}, u32[]{:S(2)}) copy-start(f32[128]{0:T(128)} %get-tuple-element.345) | copy-start | bytes 1540
  164.8 10.4 %copy-start.45 = (f32[128]{0:T(128)S(1)}, f32[128]{0:T(128)}, u32[]{:S(2)}) copy-start(f32[128]{0:T(128)} %get-tuple-element.312) | copy-start | bytes 1540
  164.8 10.4 %copy-start.46 = (f32[128]{0:T(128)S(1)}, f32[128]{0:T(128)}, u32[]{:S(2)}) copy-start(f32[128]{0:T(128)} %get-tuple-element.348) | copy-start | bytes 1540
  164.8 10.4 %copy-start.47 = (s32[128]{0:T(128)S(1)}, s32[128]{0:T(128)}, u32[]{:S(2)}) copy-start(s32[128]{0:T(128)} %get-tuple-element.323) | copy-start | bytes 1540
  164.8 10.4 %copy-start.48 = (s32[128]{0:T(128)S(1)}, s32[128]{0:T(128)}, u32[]{:S(2)}) copy-start(s32[128]{0:T(128)} %get-tuple-element.324) | copy-start | bytes 1540
  164.8 10.4 %copy-start.49 = (s32[128]{0:T(128)S(1)}, s32[128]{0:T(128)}, u32[]{:S(2)}) copy-start(s32[128]{0:T(128)} %get-tuple-element.325) | copy-start | bytes 1540
  164.8 10.4 %copy-start.50 = (s32[128]{0:T(128)S(1)}, s32[128]{0:T(128)}, u32[]{:S(2)}) copy-start(s32[128]{0:T(128)} %get-tuple-element.330) | copy-start | bytes 1540
  166.8 5.2 collective-permute-start.6
  167.7 4.9 collective-permute-start.7
  172.8 3.2 collective-permute-start.9
  175.1 1.3 collective-permute-start.8
  177.7 13.5 %collective-permute-start.11 = (bf16[4,4,1,7168]{3,2,1,0:T(2,128)(2,1)S(1)}, bf16[4,4,1,7168]{3,2,1,0:T(2,128)(2,1)S(1)}, u32[]{:S(2)}, u32[]{:S(2)}) collective-permute-start(bf16[4,4,1,7168]{3,2,1,0:T(2,128)(2,1)S(1)} %get-tuple-element.275), channel_id=1, source_target_pairs={{1,0},{2,1},{3,2},{4,3},{5,4},{6,5},{7,6},{0,7},{9,8},{10,9},{11,1... | collective-permute-start | bytes 688136 | tf_op jit(solution)/shard_map/ppermute | solution.py:30
  180.4 20.8 %collective-permute-start.10 = (bf16[4,4,1,7168]{3,2,1,0:T(2,128)(2,1)S(1)}, bf16[4,4,1,7168]{3,2,1,0:T(2,128)(2,1)S(1)}, u32[]{:S(2)}, u32[]{:S(2)}) collective-permute-start(bf16[4,4,1,7168]{3,2,1,0:T(2,128)(2,1)S(1)} %get-tuple-element.274), channel_id=1, source_target_pairs={{0,1},{1,2},{2,3},{3,4},{4,5},{5,6},{6,7},{7,0},{8,9},{9,10},{10,1... | collective-permute-start | bytes 688136 | tf_op jit(solution)/shard_map/ppermute | solution.py:29
  182.1 19.1 %copy-start.10 = (f32[128,720]{0,1:T(8,128)}, f32[128,720]{0,1:T(8,128)S(1)}, u32[]{:S(2)}) copy-start(f32[128,720]{0,1:T(8,128)S(1)} %mul.1016) | copy-start | bytes 1105924
  316.2 5.7 %collective-permute-start.13 = (f32[132,2,36]{0,2,1:T(8,128)S(1)}, f32[132,2,36]{0,2,1:T(8,128)S(1)}, u32[]{:S(2)}, u32[]{:S(2)}) collective-permute-start(f32[132,2,36]{0,2,1:T(8,128)S(1)} %get-tuple-element.271), channel_id=1, source_target_pairs={{16,0},{32,16},{48,32},{64,48},{80,64},{96,80},{112,96},{128,112},... | collective-permute-start | bytes 114056 | tf_op jit(solution)/shard_map/ppermute | solution.py:30
  320.4 5.6 %collective-permute-start.12 = (f32[132,2,36]{0,2,1:T(8,128)S(1)}, f32[132,2,36]{0,2,1:T(8,128)S(1)}, u32[]{:S(2)}, u32[]{:S(2)}) collective-permute-start(f32[132,2,36]{0,2,1:T(8,128)S(1)} %get-tuple-element.270), channel_id=1, source_target_pairs={{0,16},{16,32},{32,48},{48,64},{64,80},{80,96},{96,112},{112,128},... | collective-permute-start | bytes 114056 | tf_op jit(solution)/shard_map/ppermute | solution.py:29
  326.3 4.0 collective-permute-start.15
  328.8 2.2 collective-permute-start.14
  331.2 4.5 collective-permute-start.17
  333.6 6.6 %collective-permute-start.16 = (f32[136,24,2]{0,2,1:T(2,128)S(1)}, f32[136,24,2]{0,2,1:T(2,128)S(1)}, u32[]{:S(2)}, u32[]{:S(2)}) collective-permute-start(f32[136,24,2]{0,2,1:T(2,128)S(1)} %get-tuple-element.256), channel_id=1, source_target_pairs={{0,1},{1,2},{2,3},{3,4},{4,5},{5,6},{6,7},{7,0},{8,9},{9,10},{10,1... | collective-permute-start | bytes 78344 | tf_op jit(solution)/shard_map/ppermute | solution.py:29
  341.6 3.2 collective-permute-start.18
  351.0 15.1 %all-to-all-start = ((f32[8,1,16384]{2,1,0:T(1,128)}), f32[8,1,16384]{2,1,0:T(1,128)S(1)}, u32[]{:S(2)}, u32[]{:S(2)}) async-start(f32[8,1,16384]{2,1,0:T(1,128)} %reshape.1563), calls=%async_computation | async-start | bytes 1048576 | tf_op jit(solution)/shard_map/all_to_all | solution.py:187
  385.8 17.4 %all-to-all-start.1 = ((f32[16,1,8192]{2,1,0:T(1,128)}), f32[16,1,8192]{2,1,0:T(1,128)S(1)}, u32[]{:S(2)}, u32[]{:S(2)}) async-start(f32[16,1,8192]{2,1,0:T(1,128)} %reshape.1565), calls=%async_computation.1 | async-start | bytes 1048576 | tf_op jit(solution)/shard_map/all_to_all | solution.py:191
  511.7 14.4 %copy-start.13 = (f32[128,20,36]{0,2,1:T(8,128)S(1)}, f32[128,20,36]{0,2,1:T(8,128)}, u32[]{:S(2)}) copy-start(f32[128,20,36]{0,2,1:T(8,128)} %get-tuple-element.288) | copy-start | bytes 1105924
  511.9 14.2 %copy-start.12 = (f32[128,20,36]{0,2,1:T(8,128)S(1)}, f32[128,20,36]{0,2,1:T(8,128)}, u32[]{:S(2)}) copy-start(f32[128,20,36]{0,2,1:T(8,128)} %get-tuple-element.290) | copy-start | bytes 1105924
  511.9 3.3 collective-permute-start.20
  514.2 4.9 collective-permute-start.19
  519.3 3.1 collective-permute-start.22
  521.1 1.7 collective-permute-start.21
  523.1 4.4 collective-permute-start.24
  524.9 6.5 %collective-permute-start.23 = (f32[132,20,2]{0,2,1:T(2,128)S(1)}, f32[132,20,2]{0,2,1:T(2,128)S(1)}, u32[]{:S(2)}, u32[]{:S(2)}) collective-permute-start(f32[132,20,2]{0,2,1:T(2,128)S(1)} %get-tuple-element.266), channel_id=1, source_target_pairs={{0,1},{1,2},{2,3},{3,4},{4,5},{5,6},{6,7},{7,0},{8,9},{9,10},{10,1... | collective-permute-start | bytes 63368 | tf_op jit(solution)/shard_map/ppermute | solution.py:29
  (53 other events, 213.8 us)
where the time goes:
time: 545 us; the launch traced here: 535 us
  local copies, waits for them, and re-layouts  213 us (39%)
  waiting for transfers between devices  91.4 us (17%)
  other arithmetic  84.9 us (16%)
  starting transfers between devices  51.4 us (9%)
  matrix products  48.8 us (9%)
  blocking collectives  40.6 us (7%)
    ppermute x12, waiting for transfers between devices, extended_2(): before = lax.ppermute(last, axis, up)  42.6 us
    ppermute x12, starting transfers between devices, extended_2(): after = lax.ppermute(leading, axis, down)  38.3 us
    gather x8, local copies, waits for them, and re-layouts, interact(): displace = places[links] - located[None]  24.6 us
    ppermute x12, waiting for transfers between devices, extended_2(): after = lax.ppermute(leading, axis, down)  24.5 us
    mul x8, local copies, waits for them, and re-layouts, interact(): fourth_path[:, :, None, :] * vectors  22 us
    dot_general x17, matrix products, product(): jnp.dot(left, right, precision=HIGHEST_PRECISION, preferred_element_type=...  20.7 us
    transpose x4, local copies, waits for them, and re-layouts, per_device(): jnp.transpose(received, (1, 2, 4, 0, 3)).reshape(wave_rows, 2, span_x, MESH)  20.4 us
    gather x4, local copies, waits for them, and re-layouts, interact(): gathered = lookup[links].astype(jnp.float32)  20.3 us
  transfers between devices with their start and end apart: 27, of which 25 were waited for; matrix products, arithmetic and copies ran while one was open for 2% of the time, Pallas kernels for 0%

commit v1 on v0

v1 whole, which is shorter than its diff:
```python
import math

import jax
import jax.numpy as jnp
import numpy as np
from jax import lax
from jax.experimental import pallas as pl
from jax.experimental.pallas import tpu as pltpu
from jax.sharding import PartitionSpec as P

C = 128
NB = 8
HID = 64
NEIGH = 16
ENV = 7
MESH = 256
ATOMS = 128
COULOMB = 4.0
EWALD = 0.7
BX, BY, BZ = 16, 128, 32
ZPAD = 40

F32 = jnp.float32
BF16 = jnp.bfloat16
NN = (((1,), (0,)), ((), ()))
NT = (((1,), (1,)), ((), ()))
TN = (((0,), (0,)), ((), ()))


def dot(a, b, dims=NN):
    return lax.dot_general(a, b, dims, preferred_element_type=F32)


def halves(x):
    high = x.astype(BF16)
    return high, (x - high.astype(F32)).astype(BF16)


def dot3(a, b, dims=NN):
    return dot(a[0], b[0], dims) + (dot(a[0], b[1], dims) + dot(a[1], b[0], dims))


def np_halves(x):
    x = np.asarray(x, np.float32)
    high = x.astype(BF16)
    return high, (x - high.astype(np.float32)).astype(BF16)


def real_basis():
    rows = np.arange(MESH)
    wave = np.where(rows <= MESH // 2, rows, rows - MESH // 2)
    angle = 2.0 * np.pi * ((wave[:, None] * np.arange(MESH)[None, :]) % MESH) / MESH
    table = np.where((rows <= MESH // 2)[:, None], np.cos(angle), np.sin(angle))
    return wave, table


def constants():
    wave, table = real_basis()
    freq = wave / MESH
    modulus = 9.0 / np.square(2.0 + np.cos(2.0 * np.pi * wave / MESH))
    weight = np.where((wave == 0) | (wave == MESH // 2), 1.0, 2.0)
    factor = np.exp(-(np.pi**2 / EWALD**2) * freq**2) * modulus * weight
    out = {"basis_y": np_halves(table)}
    zed = np.zeros((8, 128, MESH))
    for part in range(8):
        for point in range(35):
            zed[part, point] = table[:, (part * BZ + point - 1) % MESH]
    out["basis_z"] = np_halves(zed.reshape(1024, MESH))
    exx = np.zeros((3, MESH, 16, 8))
    for third in range(3):
        for part in range(16):
            for group in range(7):
                point = 3 * group + third
                if point < 19:
                    exx[third, :, part, group] = table[:, (part * BX + point - 1) % MESH]
    exx = exx.reshape(3, MESH, 128)
    out["basis_x"] = np_halves(exx)
    out["basis_xt"] = np_halves(np.swapaxes(exx, 1, 2))
    out["col"] = np.stack([freq**2, factor], axis=1).astype(np.float32)
    row = np.zeros((8, MESH), np.float32)
    row[0], row[1] = freq**2, factor
    out["row"] = row
    out["scale_y"] = (factor * (COULOMB / (math.pi * MESH**3))).astype(np.float32)
    return out


def select_rows(octants):
    wanted = jnp.transpose(jnp.broadcast_to(octants.astype(F32), (128, 128)))
    lane = lax.broadcasted_iota(jnp.int32, (128, 128), 1).astype(F32)
    return jnp.where(wanted == lane, 1.0, 0.0).astype(BF16)


def geometry_rows(cells, fraction):
    return jnp.concatenate(
        [cells.astype(F32), fraction.astype(F32), jnp.zeros((122, ATOMS), F32)], axis=0
    )


def prep_kernel(feats, fraction, cells, octants, out):
    chosen = select_rows(octants[...])
    out[:, :512] = dot(chosen, feats[...]).astype(BF16)
    geometry = jnp.transpose(geometry_rows(cells[...], fraction[...])).astype(BF16)
    out[:, 512:] = dot(chosen, geometry).astype(BF16)


def table_rows(neighbours):
    ghost = neighbours - ATOMS
    outer = (ghost * 4682) >> 16
    spot = ghost - outer * 14
    code = outer
    for bound in (21, 21, 23, 23, 33, 33, 35, 35):
        code = code + (outer >= bound).astype(jnp.int32)
    ex, ey, ez = code >> 4, (code >> 2) & 3, code & 3
    is_ghost = (neighbours >= ATOMS) & (neighbours < 912)
    near = (ey == 1) | (ey == 2)
    half = jnp.where(near, ey - 1, jnp.where(ey == 0, 1, 0))
    base = jnp.where(near, 128, 640)
    row = base + ((ex * 2 + half) * 4 + ez) * 16 + spot
    row = jnp.where(is_ghost, row, jnp.where(neighbours < ATOMS, neighbours, -1))

    def offset(coord, span):
        moved = jnp.where(coord == 3, span, jnp.where(coord == 0, -span, 0))
        return jnp.where(is_ghost, moved, 0).astype(F32)

    return row, (offset(ex, BX), offset(ey, BY), offset(ez, BZ))


def transposed(x):
    return jnp.transpose(x.astype(F32)).astype(BF16)


def gather_slots(rows, table, gathered, geometry=None):
    for pair in range(NEIGH // 2):
        wanted = jnp.concatenate(
            [rows[2 * pair : 2 * pair + 1, :], rows[2 * pair + 1 : 2 * pair + 2, :]], axis=1
        )
        spots = lax.broadcasted_iota(jnp.int32, (1152, 256), 0)
        one_hot = jnp.where(spots == wanted, 1.0, 0.0).astype(BF16)
        found = dot(table[...], one_hot)
        lanes = slice(pair * 256, pair * 256 + 256)
        gathered[:, lanes] = found[:512].astype(BF16)
        if geometry is not None:
            geometry[:, lanes] = found[512:520]


def silu(x):
    return x * (1.0 / (1.0 + jnp.exp(-x)))


def messages(hidden, radial_out, radial, gathered, unit, message):
    for pair in range(NEIGH // 2):
        lanes = slice(pair * 256, pair * 256 + 256)
        radial[:, lanes] = dot(radial_out, hidden[:, lanes], TN)

    def one_chunk(chunk, carry):
        start = pl.multiple_of(chunk * 32, 32)
        sums = [jnp.zeros((32, 128), F32) for _ in range(4)]
        for slot in range(NEIGH):
            lanes = slice(slot * 128, slot * 128 + 128)
            r = [radial[pl.ds(start + 128 * p, 32), lanes] for p in range(4)]
            s, vx, vy, vz = [
                gathered[pl.ds(start + 128 * p, 32), lanes].astype(F32) for p in range(4)
            ]
            ux = unit[slot : slot + 1, :]
            uy = unit[16 + slot : 17 + slot, :]
            uz = unit[32 + slot : 33 + slot, :]
            sums[0] += r[0] * s + r[1] * (ux * vx + uy * vy + uz * vz)
            scaled = r[2] * s
            sums[1] += ux * scaled + r[3] * vx
            sums[2] += uy * scaled + r[3] * vy
            sums[3] += uz * scaled + r[3] * vz
        for p in range(4):
            message[pl.ds(start + 128 * p, 32), :] = (sums[p] * 0.25).astype(BF16)
        return carry

    lax.fori_loop(0, 4, one_chunk, 0)


def mixed(feats, message, mix_weight, layer, out):
    previous = feats[...].astype(F32)
    scalar = dot(message[0:128, :], mix_weight[layer, 0], TN)
    out[:, 0:128] = (previous[:, 0:128] + silu(scalar)).astype(BF16)
    for d in range(1, 4):
        rows = slice(128 * d, 128 * d + 128)
        moved = dot(message[rows, :], mix_weight[layer, 1], TN)
        out[:, rows] = (previous[:, rows] + moved).astype(BF16)


def first_kernel(
    feats, near, far, fraction, cells, octants, neighbours, radial_in, radial_out, mix_weight,
    new, outgoing, unit, hidden_next, rows_out,
    table, gathered, geometry, radial, message,
):
    table[:512, 0:128] = transposed(feats[...])
    table[512:528, 0:128] = geometry_rows(cells[...], fraction[...])[:16].astype(BF16)
    for start, piece in ((128, near), (640, far)):
        for q in range(4):
            lanes = slice(start + 128 * q, start + 128 * q + 128)
            flipped = transposed(piece[128 * q : 128 * q + 128, :])
            table[:, lanes] = flipped[:528]
    rows, shifts = table_rows(neighbours[...])
    rows_out[...] = rows
    gather_slots(rows, table, gathered, geometry)
    located = cells[...].astype(F32) + fraction[...].astype(F32)
    delta = []
    for d in range(3):
        cell = jnp.concatenate(
            [geometry[d : d + 1, k * 128 : k * 128 + 128] for k in range(NEIGH)], axis=0
        )
        part = jnp.concatenate(
            [geometry[3 + d : 4 + d, k * 128 : k * 128 + 128] for k in range(NEIGH)], axis=0
        )
        delta.append(((cell + shifts[d]) + part) - located[d : d + 1, :])
    length_sq = delta[0] * delta[0] + delta[1] * delta[1] + delta[2] * delta[2]
    distance = jnp.sqrt(length_sq)
    divisor = jnp.sqrt(length_sq + 1.0)
    for d in range(3):
        unit[16 * d : 16 * d + 16, :] = delta[d] / divisor
    envelope = jnp.square(jnp.maximum(1.0 - length_sq / (ENV * ENV), 0.0))
    centres = lax.broadcasted_iota(jnp.int32, (NB, 128), 0).astype(F32)
    basis = []
    for k in range(NEIGH):
        away = distance[k : k + 1, :] - centres
        basis.append(jnp.exp(-(away * away)) * envelope[k : k + 1, :])
    basis = jnp.concatenate(basis, axis=1).astype(BF16)
    hidden = silu(dot(radial_in[0], basis, TN)).astype(BF16)
    hidden_next[...] = silu(dot(radial_in[1], basis, TN)).astype(BF16)
    messages(hidden, radial_out[0], radial, gathered, unit, message)
    mixed(feats, message, mix_weight, 0, new)
    outgoing[...] = dot(select_rows(octants[...]), new[...]).astype(BF16)


def second_kernel(
    feats, near, far, rows, unit, hidden, radial_out, mix_weight, readout, kinds, species_table,
    fraction, cells,
    new, packed, base,
    table, gathered, radial, message,
):
    table[:, 0:128] = transposed(feats[...])
    for start, piece in ((128, near), (640, far)):
        for q in range(4):
            lanes = slice(start + 128 * q, start + 128 * q + 128)
            table[:, lanes] = transposed(piece[128 * q : 128 * q + 128, :])
    gather_slots(rows[...], table, gathered)
    messages(hidden[...], radial_out[1], radial, gathered, unit, message)
    mixed(feats, message, mix_weight, 1, new)
    heads = dot(readout[...], new[:, 0:128], NT)
    second = kinds[...] == 1
    energy = jnp.where(second, species_table[1, 0], species_table[0, 0])
    offset = jnp.where(second, species_table[1, 1], species_table[0, 1])
    base[...] = heads[0:1, :] + energy
    packed[...] = jnp.concatenate(
        [
            heads[1:2, :] + offset,
            fraction[...].astype(F32),
            cells[...].astype(F32),
            jnp.zeros((1, ATOMS), F32),
        ],
        axis=0,
    )


def spline(t):
    s = 1.0 - t
    weights = [
        s * s * s / 6.0,
        (3.0 * t * t * t - 6.0 * t * t + 4.0) / 6.0,
        (-3.0 * t * t * t + 3.0 * t * t + 3.0 * t + 1.0) / 6.0,
        t * t * t / 6.0,
    ]
    slopes = [
        -0.5 * s * s,
        0.5 * (3.0 * t * t - 4.0 * t),
        0.5 * (-3.0 * t * t + 2.0 * t + 1.0),
        0.5 * t * t,
    ]
    return weights, slopes


def spread(coefficients, spots, count):
    row = lax.broadcasted_iota(jnp.int32, (count, spots[0].shape[1]), 0)
    total = jnp.zeros(row.shape, F32)
    for coefficient, spot in zip(coefficients, spots):
        total = jnp.where(row == spot, coefficient, total)
    return total


def planes_of(along_x, along_z):
    tail = jnp.zeros((8, along_z.shape[1]), F32)
    tiles = []
    for group in range(7):
        parts = [along_z * along_x[3 * group + c : 3 * group + c + 1, :] for c in range(3)]
        tiles.append(jnp.concatenate(parts + [tail], axis=0))
    return tiles


def both_atoms(own, other):
    both = jnp.concatenate([own[...], other[...]], axis=1)
    return both, [both[4 + d : 5 + d, :].astype(jnp.int32) for d in range(3)]


def charges_kernel(own, other, high, low, out, weight_y, slope_y):
    both, cells = both_atoms(own, other)
    half = lax.axis_index("gy")
    lane = lax.broadcasted_iota(jnp.int32, (1, 256), 1)
    domain = jnp.where(lane < 128, half, 1 - half)
    rows = pl.ds(pl.multiple_of(half * 128, 128), 128)
    table = (high[rows, :], low[rows, :])
    weights, slopes = spline(both[2:3, :])
    spots = [(cells[1] + domain * BY + (m - 1)) & (MESH - 1) for m in range(4)]
    along_y = dot3(table, halves(spread(weights, spots, MESH)))
    weight_y[...] = along_y
    slope_y[...] = dot3(table, halves(spread(slopes, spots, MESH)))
    charged = halves(along_y * both[0:1, :])
    along_x = spread(spline(both[1:2, :])[0], [cells[0] + m for m in range(4)], 24)
    along_z = spread(spline(both[3:4, :])[0], [cells[2] + m for m in range(4)], ZPAD)
    for group, tile in enumerate(planes_of(along_x, along_z)):
        out[:, group, :] = dot3(charged, halves(tile), NT)
    out[:, 7, :] = jnp.zeros((128, 128), F32)


def waves_kernel(
    scale_y, received, zh, zl, xh, xl, th, tl, col, row, out, lhs,
):
    for part in range(8):
        lanes = slice(part * 128, part * 128 + 128)
        block = received[part]
        for third in range(3):
            moved = block if third == 0 else pltpu.roll(block, 128 - ZPAD * third, 1)
            lhs[third * 128 : third * 128 + 128, lanes] = moved
    zed = (zh[...], zl[...])
    lines = dot3(halves(lhs[...]), zed)
    total = jnp.zeros((MESH, MESH), F32)
    for third in range(3):
        total += dot3(
            (xh[third], xl[third]), halves(lines[third * 128 : third * 128 + 128, :])
        )
    number = lax.axis_index("gy") * 128 + lax.axis_index("gz") * 16 + lax.axis_index("gx")
    wave = jnp.where(number <= 128, number, number - 128)
    freq_y = wave.astype(F32) / MESH
    square = (col[:, 0:1] + row[0:1, :]) + freq_y * freq_y
    kernel = (col[:, 1:2] * scale_y[number]) * row[1:2, :]
    positive = square > 0.0
    kernel = jnp.where(positive, kernel / jnp.where(positive, square, 1.0), 0.0)
    scaled = halves(total * kernel)
    for third in range(3):
        lhs[third * 128 : third * 128 + 128, :] = dot3(
            halves(dot3((th[third], tl[third]), scaled)), zed, NT
        )
    for part in range(8):
        lanes = slice(part * 128, part * 128 + 128)
        block = lhs[0:128, lanes]
        for third in range(1, 3):
            block += pltpu.roll(lhs[third * 128 : third * 128 + 128, lanes], ZPAD * third, 1)
        out[part] = block


def forces_kernel(own, other, weight_y, slope_y, returned, out_own, out_other):
    both, cells = both_atoms(own, other)
    flat = halves(jnp.concatenate([returned[:, group, :] for group in range(7)], axis=1))
    weights_x, slopes_x = spline(both[1:2, :])
    weights_z, slopes_z = spline(both[3:4, :])
    spots_x = [cells[0] + m for m in range(4)]
    spots_z = [cells[2] + m for m in range(4)]
    along_x = spread(weights_x, spots_x, 24)
    along_z = spread(weights_z, spots_z, ZPAD)
    down_x = spread(slopes_x, spots_x, 24)
    down_z = spread(slopes_z, spots_z, ZPAD)

    def level(ax, az):
        return dot3(flat, halves(jnp.concatenate(planes_of(ax, az), axis=0)))

    level_0 = level(along_x, along_z)
    wy = weight_y[...]
    rows = [
        jnp.sum(wy * level_0, axis=0, keepdims=True),
        jnp.sum(wy * level(down_x, along_z), axis=0, keepdims=True),
        jnp.sum(slope_y[...] * level_0, axis=0, keepdims=True),
        jnp.sum(wy * level(along_x, down_z), axis=0, keepdims=True),
        jnp.zeros((4, 256), F32),
    ]
    total = jnp.concatenate(rows, axis=0)
    out_own[...] = total[:, 0:128]
    out_other[...] = total[:, 128:256]


VMEM = pl.BlockSpec(memory_space=pltpu.VMEM)
SMEM = pl.BlockSpec(memory_space=pltpu.SMEM)


def call(kernel, outs, *args, scratch=(), scalars=()):
    specs = [SMEM if i in scalars else VMEM for i in range(len(args))]
    return pl.pallas_call(
        kernel,
        out_shape=[jax.ShapeDtypeStruct(s, d) for s, d in outs],
        in_specs=specs,
        out_specs=[VMEM] * len(outs),
        scratch_shapes=[pltpu.VMEM(s, d) for s, d in scratch],
    )(*args)


def ring(axis, step):
    count = lax.axis_size(axis)
    return [(i, (i + step) % count) for i in range(count)]


def partner(block):
    return lax.ppermute(block, "gy", [(0, 1), (1, 0)])


def ghosts(blocks):
    width = blocks.shape[1]
    x = blocks.reshape(2, 2, 2, 16, width)
    before = lax.ppermute(x[:, :, 1:], "gz", ring("gz", 1))
    after = lax.ppermute(x[:, :, :1], "gz", ring("gz", -1))
    x = jnp.concatenate([before, x, after], axis=2)
    before = lax.ppermute(x[1:], "gx", ring("gx", 1))
    after = lax.ppermute(x[:1], "gx", ring("gx", -1))
    x = jnp.concatenate([before, x, after], axis=0)
    return x.reshape(512, width), partner(x).reshape(512, width)


def across(blocks):
    return lax.all_to_all(blocks, ("gz", "gx"), split_axis=0, concat_axis=0, tiled=True)


def per_device(
    features, fraction, cell_index, species, octant_rows, neighbours,
    radial_in, radial_out, mix_weight, readout, species_table,
):
    table = constants()
    feats = features[0, 0, 0]
    part = fraction[0, 0, 0]
    cells = cell_index[0, 0, 0]
    kinds = species.reshape(1, ATOMS)
    octants = jnp.pad(octant_rows[0, 0, 0], ((0, 0), (0, 2)), constant_values=-1).reshape(1, 128)
    links = neighbours[0, 0, 0]
    heads = jnp.pad(jnp.transpose(readout), ((0, 6), (0, 0)))

    (outgoing,) = call(prep_kernel, [((128, 640), BF16)], feats, part, cells, octants)
    near, far = ghosts(outgoing)
    feats, outgoing, unit, hidden, rows = call(
        first_kernel,
        [
            ((128, 512), BF16),
            ((128, 512), BF16),
            ((48, 128), F32),
            ((HID, 2048), BF16),
            ((NEIGH, 128), jnp.int32),
        ],
        feats, near, far, part, cells, octants, links, radial_in, radial_out, mix_weight,
        scratch=[
            ((528, 1152), BF16),
            ((512, 2048), BF16),
            ((8, 2048), F32),
            ((512, 2048), F32),
            ((512, 128), BF16),
        ],
    )
    near, far = ghosts(outgoing)
    feats, packed, base = call(
        second_kernel,
        [((128, 512), BF16), ((8, 128), F32), ((1, 128), F32)],
        feats, near, far, rows, unit, hidden, radial_out, mix_weight, heads, kinds, species_table,
        part, cells,
        scalars=(10,),
        scratch=[
            ((512, 1152), BF16),
            ((512, 2048), BF16),
            ((512, 2048), F32),
            ((512, 128), BF16),
        ],
    )
    other = partner(packed)
    lines, weight_y, slope_y = call(
        charges_kernel,
        [((128, 8, 128), F32), ((128, 256), F32), ((128, 256), F32)],
        packed, other, *table["basis_y"],
    )
    received = across(lines).reshape(8, 128, 128)
    (waves,) = call(
        waves_kernel,
        [((8, 128, 128), F32)],
        table["scale_y"], received, *table["basis_z"], *table["basis_x"], *table["basis_xt"],
        table["col"], table["row"],
        scalars=(0,),
        scratch=[((384, 1024), F32)],
    )
    returned = across(waves.reshape(128, 8, 128))
    here, there = call(
        forces_kernel,
        [((8, 128), F32), ((8, 128), F32)],
        packed, other, weight_y, slope_y, returned,
    )
    total = here + partner(there)
    charge = packed[0:1]
    force = -charge * total[1:4]
    energy = base + 0.5 * charge * total[0:1]
    return feats[None, None, None], energy.reshape(1, 1, 1, ATOMS), force[None, None, None]


def solution(mesh):
    domain = P("gx", "gy", "gz", None, None)
    atoms = P("gx", "gy", "gz", None)
    return jax.shard_map(
        per_device,
        mesh=mesh,
        in_specs=(domain, domain, domain, atoms, domain, domain, P(), P(), P(), P(), P()),
        out_specs=(domain, atoms, domain),
        check_vma=False,
    )
```

time: 545 us -> 142 us (0.26); the launches traced: 535 us -> 142 us
  local copies, waits for them, and re-layouts: 213 us -> 7.95 us
  other arithmetic: 84.9 us -> 2.13 us
  waiting for transfers between devices: 91.4 us -> 15.1 us
  matrix products: 48.8 us -> 0 us
  Pallas kernels: 0 us -> 28.8 us
  starting transfers between devices: 51.4 us -> 30.9 us
  blocking collectives: 40.6 us -> 56 us
    ppermute x25 -> x12, waiting for transfers between devices: 67.1 us -> 15.1 us  [the longest x2 5.31 us: ghosts(): before = lax.ppermute(x[1:], 'gx', ring('gx', 1))]
    gather x18 -> x0, local copies, waits for them, and re-layouts: 51.7 us -> none  [the longest x8 24.6 us: interact(): displace = places[links] - located[None]]
    dot_general x39 -> x0, matrix products: 48.8 us -> none  [the longest x17 20.7 us: product(): jnp.dot(left, right, precision=HIGHEST_PRECISION, preferred_element_type=...]
    reduce_sum x17 -> x0, other arithmetic: 34.2 us -> none  [the longest x4 14.2 us: interact(): projected = jnp.sum(direction[..., None] * vectors, axis=2)]
    pallas_call x0 -> x6, Pallas kernels: none -> 28.8 us  [call(): pl.pallas_call(kernel, out_shape=[jax.ShapeDtypeStruct(s, d) for s, d in...]
    mul x15 -> x0, local copies, waits for them, and re-layouts: 24.5 us -> none  [the longest x8 22 us: interact(): fourth_path[:, :, None, :] * vectors]
    all_to_all x2 -> x0, waiting for transfers between devices: 24.3 us -> none  [the longest x1 12.9 us: across_gx(): return lax.all_to_all(blocks, 'gx', split_axis=0, concat_axis=0, tiled=True)]
    transpose x8 -> x0, local copies, waits for them, and re-layouts: 21.9 us -> none  [the longest x4 20.4 us: per_device(): jnp.transpose(received, (1, 2, 4, 0, 3)).reshape(wave_rows, 2, span_x, MESH)]
  transfers between devices with their start and end apart: 27 -> 12, of which waited for: 25 -> 10; matrix products, arithmetic and copies ran while one was open for 2% -> 0% of each run, Pallas kernels for 0% -> 0%
where the time goes in v1:
time: 142 us
  blocking collectives  56 us (39%)
  starting transfers between devices  30.9 us (22%)
  Pallas kernels  28.8 us (20%)
  waiting for transfers between devices  15.1 us (11%)
  local copies, waits for them, and re-layouts  7.95 us (6%)
  other arithmetic  2.13 us (2%)
    all_to_all x2, blocking collectives, across(): lax.all_to_all(blocks, ('gz', 'gx'), split_axis=0, concat_axis=0, tiled=T...  56 us
    pallas_call x6, Pallas kernels, call(): pl.pallas_call(kernel, out_shape=[jax.ShapeDtypeStruct(s, d) for s, d in...  28.8 us
    ppermute x4, starting transfers between devices, partner(): return lax.ppermute(block, 'gy', [(0, 1), (1, 0)])  8.98 us
    ppermute x2, starting transfers between devices, ghosts(): after = lax.ppermute(x[:1], 'gx', ring('gx', -1))  8 us
    ppermute x2, starting transfers between devices, ghosts(): before = lax.ppermute(x[:, :, 1:], 'gz', ring('gz', 1))  6.93 us
    ppermute x2, waiting for transfers between devices, ghosts(): before = lax.ppermute(x[1:], 'gx', ring('gx', 1))  5.31 us
    ppermute x2, starting transfers between devices, ghosts(): after = lax.ppermute(x[:, :, :1], 'gz', ring('gz', -1))  4.93 us
    unnamed x22, local copies, waits for them, and re-layouts  4.81 us
  transfers between devices with their start and end apart: 12, of which 10 were waited for; matrix products, arithmetic and copies ran while one was open for 0% of the time, Pallas kernels for 0%

profile of v1, /device:TPU:1, one launch (start us, length us, event | category | flops | bytes accessed | tf_op | source)
XLA Modules:
  0.0 141.6 jit_solution(2001826760919673573)
XLA Ops:
  0.6 1.3 copy.28
  1.9 0.6 reshape.39.octants
  2.5 1.8 %shard_map.229 = bf16[128,640]{1,0:T(8,128)(2,1)} custom-call(bf16[128,512]{1,0:T(8,128)(2,1)} %bitcast.36, bf16[3,128]{1,0:T(4,128)(2,1)} %bitcast.41, s32[3,128]{1,0:T(4,128)} %bitcast.38, s32[1,128]{1,0:T(1,128)} %reshape.39.octants), custom_call_target="tpu_custom_call" | custom-call | tf_op jit(solution)/shard_map/pallas_call | solution.py:393
  4.4 1.0 fusion.2
  5.3 3.6 %collective-permute-start = (bf16[2,2,1,16,640]{4,3,2,1,0:T(8,128)(2,1)S(1)}, bf16[2,2,1,16,640]{4,3,2,1,0:T(8,128)(2,1)S(1)}, u32[]{:S(2)}, u32[]{:S(2)}) collective-permute-start(bf16[2,2,1,16,640]{4,3,2,1,0:T(8,128)(2,1)S(1)} %get-tuple-element.36), channel_id=1, source_target_pairs={{0,1},{1,2},{2,3},{3,4},{4,5},{5,6},{6,7},{7,0},{8,9},{9,10},{10,1... | collective-permute-start | bytes 245768 | tf_op jit(solution)/shard_map/ppermute | solution.py:414
  9.0 2.5 %collective-permute-start.1 = (bf16[2,2,1,16,640]{4,3,2,1,0:T(8,128)(2,1)S(1)}, bf16[2,2,1,16,640]{4,3,2,1,0:T(8,128)(2,1)S(1)}, u32[]{:S(2)}, u32[]{:S(2)}) collective-permute-start(bf16[2,2,1,16,640]{4,3,2,1,0:T(8,128)(2,1)S(1)} %get-tuple-element.37), channel_id=1, source_target_pairs={{0,7},{1,0},{2,1},{3,2},{4,3},{5,4},{6,5},{7,6},{8,15},{9,8},{10,9... | collective-permute-start | bytes 245768 | tf_op jit(solution)/shard_map/ppermute | solution.py:415
  11.5 1.7 %collective-permute-done = bf16[2,2,1,16,640]{4,3,2,1,0:T(8,128)(2,1)S(1)} collective-permute-done((bf16[2,2,1,16,640]{4,3,2,1,0:T(8,128)(2,1)S(1)}, bf16[2,2,1,16,640]{4,3,2,1,0:T(8,128)(2,1)S(1)}, u32[]{:S(2)}, u32[]{:S(2)}) %collective-permute-start) | collective-permute-done | bytes 81952 | tf_op jit(solution)/shard_map/ppermute | solution.py:414
  13.3 0.8 collective-permute-done.1
  14.1 0.0 copy-done
  14.2 2.0 %collective-permute-start.2 = (bf16[1,2,4,16,640]{4,3,2,1,0:T(8,128)(2,1)S(1)}, bf16[1,2,4,16,640]{4,3,2,1,0:T(8,128)(2,1)S(1)}, u32[]{:S(2)}, u32[]{:S(2)}) collective-permute-start(bf16[1,2,4,16,640]{4,3,2,1,0:T(8,128)(2,1)S(1)} %get-tuple-element.32), channel_id=1, source_target_pairs={{0,16},{16,32},{32,48},{48,64},{64,80},{80,96},{96,112},{112,128},... | collective-permute-start | bytes 491528 | tf_op jit(solution)/shard_map/ppermute | solution.py:417
  16.2 4.4 %collective-permute-start.3 = (bf16[1,2,4,16,640]{4,3,2,1,0:T(8,128)(2,1)S(1)}, bf16[1,2,4,16,640]{4,3,2,1,0:T(8,128)(2,1)S(1)}, u32[]{:S(2)}, u32[]{:S(2)}) collective-permute-start(bf16[1,2,4,16,640]{4,3,2,1,0:T(8,128)(2,1)S(1)} %get-tuple-element.33), channel_id=1, source_target_pairs={{0,240},{16,0},{32,16},{48,32},{64,48},{80,64},{96,80},{112,96},{1... | collective-permute-start | bytes 491528 | tf_op jit(solution)/shard_map/ppermute | solution.py:418
  20.6 3.0 %collective-permute-done.2 = bf16[1,2,4,16,640]{4,3,2,1,0:T(8,128)(2,1)S(1)} collective-permute-done((bf16[1,2,4,16,640]{4,3,2,1,0:T(8,128)(2,1)S(1)}, bf16[1,2,4,16,640]{4,3,2,1,0:T(8,128)(2,1)S(1)}, u32[]{:S(2)}, u32[]{:S(2)}) %collective-permute-start.2) | collective-permute-done | bytes 163872 | tf_op jit(solution)/shard_map/ppermute | solution.py:417
  23.6 0.0 collective-permute-done.3
  23.6 0.1 pad_maximum_fusion
  23.7 2.2 %collective-permute-start.4 = (bf16[4,2,4,16,640]{4,3,2,1,0:T(8,128)(2,1)S(1)}, bf16[4,2,4,16,640]{4,3,2,1,0:T(8,128)(2,1)S(1)}, u32[]{:S(2)}, u32[]{:S(2)}) collective-permute-start(bf16[4,2,4,16,640]{4,3,2,1,0:T(8,128)(2,1)S(1)} %pad_maximum_fusion), channel_id=1, source_target_pairs={{0,8},{8,0},{1,9},{9,1},{2,10},{10,2},{3,11},{11,3},{4,12},{12,4},... | collective-permute-start | bytes 1966088 | tf_op jit(solution)/shard_map/ppermute | solution.py:408
  25.9 1.7 %collective-permute-done.4 = bf16[4,2,4,16,640]{4,3,2,1,0:T(8,128)(2,1)S(1)} collective-permute-done((bf16[4,2,4,16,640]{4,3,2,1,0:T(8,128)(2,1)S(1)}, bf16[4,2,4,16,640]{4,3,2,1,0:T(8,128)(2,1)S(1)}, u32[]{:S(2)}, u32[]{:S(2)}) %collective-permute-start.4) | collective-permute-done | bytes 655392 | tf_op jit(solution)/shard_map/ppermute | solution.py:408
  27.6 0.9 copy-done.4
  28.5 7.6 %shard_map.230 = (bf16[128,512]{1,0:T(8,128)(2,1)}, bf16[128,512]{1,0:T(8,128)(2,1)}, f32[48,128]{1,0:T(8,128)}, bf16[64,2048]{1,0:T(8,128)(2,1)}, s32[16,128]{1,0:T(8,128)}) custom-call(bf16[128,512]{1,0:T(8,128)(2,1)} %bitcast.37, bf16[512,640]{1,0:T(8,128)(2,1)} %bitcast.27, bf16[512,640]{1,0:T(8,128)(2,1)} %bitcast.34, bf16[3,128]{1,0:T(4,128)(2,1)} %bitcast.42, ...), custom_call_target="tpu_custom_call" | custom-call | tf_op jit(solution)/shard_map/pallas_call | solution.py:393
  36.1 0.9 fusion.3
  37.0 3.3 %collective-permute-start.5 = (bf16[2,2,1,16,512]{4,3,2,1,0:T(8,128)(2,1)S(1)}, bf16[2,2,1,16,512]{4,3,2,1,0:T(8,128)(2,1)S(1)}, u32[]{:S(2)}, u32[]{:S(2)}) collective-permute-start(bf16[2,2,1,16,512]{4,3,2,1,0:T(8,128)(2,1)S(1)} %get-tuple-element.38), channel_id=1, source_target_pairs={{0,1},{1,2},{2,3},{3,4},{4,5},{5,6},{6,7},{7,0},{8,9},{9,10},{10,1... | collective-permute-start | bytes 196616 | tf_op jit(solution)/shard_map/ppermute | solution.py:414
  40.3 2.4 %collective-permute-start.6 = (bf16[2,2,1,16,512]{4,3,2,1,0:T(8,128)(2,1)S(1)}, bf16[2,2,1,16,512]{4,3,2,1,0:T(8,128)(2,1)S(1)}, u32[]{:S(2)}, u32[]{:S(2)}) collective-permute-start(bf16[2,2,1,16,512]{4,3,2,1,0:T(8,128)(2,1)S(1)} %get-tuple-element.39), channel_id=1, source_target_pairs={{0,7},{1,0},{2,1},{3,2},{4,3},{5,4},{6,5},{7,6},{8,15},{9,8},{10,9... | collective-permute-start | bytes 196616 | tf_op jit(solution)/shard_map/ppermute | solution.py:415
  42.7 2.0 %collective-permute-done.5 = bf16[2,2,1,16,512]{4,3,2,1,0:T(8,128)(2,1)S(1)} collective-permute-done((bf16[2,2,1,16,512]{4,3,2,1,0:T(8,128)(2,1)S(1)}, bf16[2,2,1,16,512]{4,3,2,1,0:T(8,128)(2,1)S(1)}, u32[]{:S(2)}, u32[]{:S(2)}) %collective-permute-start.5) | collective-permute-done | bytes 65568 | tf_op jit(solution)/shard_map/ppermute | solution.py:414
  44.7 0.5 collective-permute-done.6
  45.3 0.1 collective-permute-start.7
  45.4 3.6 %collective-permute-start.8 = (bf16[1,2,4,16,512]{4,3,2,1,0:T(8,128)(2,1)S(1)}, bf16[1,2,4,16,512]{4,3,2,1,0:T(8,128)(2,1)S(1)}, u32[]{:S(2)}, u32[]{:S(2)}) collective-permute-start(bf16[1,2,4,16,512]{4,3,2,1,0:T(8,128)(2,1)S(1)} %get-tuple-element.35), channel_id=1, source_target_pairs={{0,240},{16,0},{32,16},{48,32},{64,48},{80,64},{96,80},{112,96},{1... | collective-permute-start | bytes 393224 | tf_op jit(solution)/shard_map/ppermute | solution.py:418
  48.9 2.4 %collective-permute-done.7 = bf16[1,2,4,16,512]{4,3,2,1,0:T(8,128)(2,1)S(1)} collective-permute-done((bf16[1,2,4,16,512]{4,3,2,1,0:T(8,128)(2,1)S(1)}, bf16[1,2,4,16,512]{4,3,2,1,0:T(8,128)(2,1)S(1)}, u32[]{:S(2)}, u32[]{:S(2)}) %collective-permute-start.7) | collective-permute-done | bytes 131104 | tf_op jit(solution)/shard_map/ppermute | solution.py:417
  51.3 0.0 collective-permute-done.8
  51.3 0.1 pad_maximum_fusion.1
  51.4 0.0 copy-start.9
  51.4 2.9 %collective-permute-start.9 = (bf16[4,2,4,16,512]{4,3,2,1,0:T(8,128)(2,1)S(1)}, bf16[4,2,4,16,512]{4,3,2,1,0:T(8,128)(2,1)S(1)}, u32[]{:S(2)}, u32[]{:S(2)}) collective-permute-start(bf16[4,2,4,16,512]{4,3,2,1,0:T(8,128)(2,1)S(1)} %pad_maximum_fusion.1), channel_id=1, source_target_pairs={{0,8},{8,0},{1,9},{9,1},{2,10},{10,2},{3,11},{11,3},{4,12},{12,4},... | collective-permute-start | bytes 1572872 | tf_op jit(solution)/shard_map/ppermute | solution.py:408
  54.3 0.6 pad.9.readout
  54.9 0.9 collective-permute-done.9
  55.9 0.8 copy-done.5
  56.7 6.9 %shard_map.231 = (bf16[128,512]{1,0:T(8,128)(2,1)}, f32[8,128]{1,0:T(8,128)}, f32[1,128]{1,0:T(1,128)}) custom-call(bf16[128,512]{1,0:T(8,128)(2,1)} %get-tuple-element.16.feats, bf16[512,512]{1,0:T(8,128)(2,1)} %bitcast.28, bf16[512,512]{1,0:T(8,128)(2,1)} %bitcast.35, s32[16,128]{1,0:T(8,128)} %get-tuple-element.18.rows, ...), custom_call_target="tpu_custom_call" | custom-call | tf_op jit(solution)/shard_map/pallas_call | solution.py:393
  63.5 0.4 collective-permute-start.10
  63.9 1.0 collective-permute-done.10.other
  64.9 0.6 copy-done.6
  65.5 2.8 %shard_map.232 = (f32[128,8,128]{2,1,0:T(8,128)}, f32[128,256]{1,0:T(8,128)}, f32[128,256]{1,0:T(8,128)}) custom-call(f32[8,128]{1,0:T(8,128)} %get-tuple-element.23.own, f32[8,128]{1,0:T(8,128)} %copy-done.6, bf16[256,256]{1,0:T(8,128)(2,1)} %constant.29.clone.high, bf16[256,256]{1,0:T(8,128)(2,1)} %constant.30.clone.low), custom_call_target="tpu_custom_call" | custom-call | tf_op jit(solution)/shard_map/pallas_call | solution.py:393
  68.3 30.8 %all_to_all.10 = f32[128,8,128]{2,1,0:T(8,128)} all-to-all(f32[128,8,128]{2,1,0:T(8,128)} %get-tuple-element.26), channel_id=1, replica_groups=mesh['gx'=16,'gy'=2,'gz'=8] {'gz','gx'}, dimensions={0} | all-to-all | bytes 1048576 | tf_op jit(solution)/shard_map/all_to_all | solution.py:424
  99.1 6.7 %shard_map.233 = f32[8,128,128]{2,1,0:T(8,128)} custom-call(f32[256]{0:T(256)} %constant.31.clone.scale_y, f32[8,128,128]{2,1,0:T(8,128)} %bitcast.29, bf16[1024,256]{1,0:T(8,128)(2,1)} %constant.32.clone.zh, bf16[1024,256]{1,0:T(8,128)(2,1)} %constant.33.clone.zl, bf16[3,256,128]{2,1,0:T(8,128)(2,1)} %constant.34.clone.xh, ...), custom_call_target="tpu_custom_call" | custom-call | tf_op jit(solution)/shard_map/pallas_call | solution.py:393
  105.8 25.2 %all_to_all.11.returned = f32[128,8,128]{2,1,0:T(8,128)} all-to-all(f32[128,8,128]{2,1,0:T(8,128)} %bitcast.30), channel_id=1, replica_groups=mesh['gx'=16,'gy'=2,'gz'=8] {'gz','gx'}, dimensions={0} | all-to-all | bytes 1048576 | tf_op jit(solution)/shard_map/all_to_all | solution.py:424
  131.1 3.0 %shard_map.234 = (f32[8,128]{1,0:T(8,128)}, f32[8,128]{1,0:T(8,128)}) custom-call(f32[8,128]{1,0:T(8,128)} %get-tuple-element.23.own, f32[8,128]{1,0:T(8,128)} %copy-done.6, f32[128,256]{1,0:T(8,128)} %get-tuple-element.24.weight_y, f32[128,256]{1,0:T(8,128)} %get-tuple-element.25.slope_y, f32[128,8,128]{2,1,0:T(8,128)} %all_to_all.11.returned), custom_call_target="tpu_custom_call" | custom-call | tf_op jit(solution)/shard_map/pallas_call | solution.py:393
  134.0 3.5 %collective-permute-start.11 = (f32[8,128]{1,0:T(8,128)}, f32[8,128]{1,0:T(8,128)S(1)}, u32[]{:S(2)}, u32[]{:S(2)}) collective-permute-start(f32[8,128]{1,0:T(8,128)} %get-tuple-element.28), channel_id=1, source_target_pairs={{0,8},{8,0},{1,9},{9,1},{2,10},{10,2},{3,11},{11,3},{4,12},{12,4},... | collective-permute-start | bytes 12296 | tf_op jit(solution)/shard_map/ppermute | solution.py:408
  137.5 1.0 collective-permute-done.11
  138.6 0.7 add.10
  139.2 0.7 copy-done.8
  139.9 1.2 negate_bitcast_fusion
  141.1 0.6 copy.25
  (20 shorter events, 0.2 us)
Async XLA Ops:
  0.6 1.3 copy-start.7
  4.4 9.7 %copy-start = (bf16[128,640]{1,0:T(8,128)(2,1)S(1)}, bf16[128,640]{1,0:T(8,128)(2,1)}, u32[]{:S(2)}) copy-start(bf16[128,640]{1,0:T(8,128)(2,1)} %shard_map.229) | copy-start | bytes 491524
  5.3 7.9 %collective-permute-start = (bf16[2,2,1,16,640]{4,3,2,1,0:T(8,128)(2,1)S(1)}, bf16[2,2,1,16,640]{4,3,2,1,0:T(8,128)(2,1)S(1)}, u32[]{:S(2)}, u32[]{:S(2)}) collective-permute-start(bf16[2,2,1,16,640]{4,3,2,1,0:T(8,128)(2,1)S(1)} %get-tuple-element.36), channel_id=1, source_target_pairs={{0,1},{1,2},{2,3},{3,4},{4,5},{5,6},{6,7},{7,0},{8,9},{9,10},{10,1... | collective-permute-start | bytes 245768 | tf_op jit(solution)/shard_map/ppermute | solution.py:414
  9.0 5.1 %collective-permute-start.1 = (bf16[2,2,1,16,640]{4,3,2,1,0:T(8,128)(2,1)S(1)}, bf16[2,2,1,16,640]{4,3,2,1,0:T(8,128)(2,1)S(1)}, u32[]{:S(2)}, u32[]{:S(2)}) collective-permute-start(bf16[2,2,1,16,640]{4,3,2,1,0:T(8,128)(2,1)S(1)} %get-tuple-element.37), channel_id=1, source_target_pairs={{0,7},{1,0},{2,1},{3,2},{4,3},{5,4},{6,5},{7,6},{8,15},{9,8},{10,9... | collective-permute-start | bytes 245768 | tf_op jit(solution)/shard_map/ppermute | solution.py:415
  14.2 9.4 %collective-permute-start.2 = (bf16[1,2,4,16,640]{4,3,2,1,0:T(8,128)(2,1)S(1)}, bf16[1,2,4,16,640]{4,3,2,1,0:T(8,128)(2,1)S(1)}, u32[]{:S(2)}, u32[]{:S(2)}) collective-permute-start(bf16[1,2,4,16,640]{4,3,2,1,0:T(8,128)(2,1)S(1)} %get-tuple-element.32), channel_id=1, source_target_pairs={{0,16},{16,32},{32,48},{48,64},{64,80},{80,96},{96,112},{112,128},... | collective-permute-start | bytes 491528 | tf_op jit(solution)/shard_map/ppermute | solution.py:417
  16.2 7.4 %collective-permute-start.3 = (bf16[1,2,4,16,640]{4,3,2,1,0:T(8,128)(2,1)S(1)}, bf16[1,2,4,16,640]{4,3,2,1,0:T(8,128)(2,1)S(1)}, u32[]{:S(2)}, u32[]{:S(2)}) collective-permute-start(bf16[1,2,4,16,640]{4,3,2,1,0:T(8,128)(2,1)S(1)} %get-tuple-element.33), channel_id=1, source_target_pairs={{0,240},{16,0},{32,16},{48,32},{64,48},{80,64},{96,80},{112,96},{1... | collective-permute-start | bytes 491528 | tf_op jit(solution)/shard_map/ppermute | solution.py:418
  23.7 3.9 %copy-start.1 = (bf16[4,2,4,16,640]{4,3,2,1,0:T(8,128)(2,1)}, bf16[4,2,4,16,640]{4,3,2,1,0:T(8,128)(2,1)S(1)}, u32[]{:S(2)}) copy-start(bf16[4,2,4,16,640]{4,3,2,1,0:T(8,128)(2,1)S(1)} %pad_maximum_fusion) | copy-start | bytes 1966084
  23.7 3.9 %collective-permute-start.4 = (bf16[4,2,4,16,640]{4,3,2,1,0:T(8,128)(2,1)S(1)}, bf16[4,2,4,16,640]{4,3,2,1,0:T(8,128)(2,1)S(1)}, u32[]{:S(2)}, u32[]{:S(2)}) collective-permute-start(bf16[4,2,4,16,640]{4,3,2,1,0:T(8,128)(2,1)S(1)} %pad_maximum_fusion), channel_id=1, source_target_pairs={{0,8},{8,0},{1,9},{9,1},{2,10},{10,2},{3,11},{11,3},{4,12},{12,4},... | collective-permute-start | bytes 1966088 | tf_op jit(solution)/shard_map/ppermute | solution.py:408
  27.6 0.9 copy-start.4
  36.1 9.1 %copy-start.3 = (bf16[128,512]{1,0:T(8,128)(2,1)S(1)}, bf16[128,512]{1,0:T(8,128)(2,1)}, u32[]{:S(2)}) copy-start(bf16[128,512]{1,0:T(8,128)(2,1)} %get-tuple-element.17) | copy-start | bytes 393220
  37.0 7.7 %collective-permute-start.5 = (bf16[2,2,1,16,512]{4,3,2,1,0:T(8,128)(2,1)S(1)}, bf16[2,2,1,16,512]{4,3,2,1,0:T(8,128)(2,1)S(1)}, u32[]{:S(2)}, u32[]{:S(2)}) collective-permute-start(bf16[2,2,1,16,512]{4,3,2,1,0:T(8,128)(2,1)S(1)} %get-tuple-element.38), channel_id=1, source_target_pairs={{0,1},{1,2},{2,3},{3,4},{4,5},{5,6},{6,7},{7,0},{8,9},{9,10},{10,1... | collective-permute-start | bytes 196616 | tf_op jit(solution)/shard_map/ppermute | solution.py:414
  40.3 4.9 %collective-permute-start.6 = (bf16[2,2,1,16,512]{4,3,2,1,0:T(8,128)(2,1)S(1)}, bf16[2,2,1,16,512]{4,3,2,1,0:T(8,128)(2,1)S(1)}, u32[]{:S(2)}, u32[]{:S(2)}) collective-permute-start(bf16[2,2,1,16,512]{4,3,2,1,0:T(8,128)(2,1)S(1)} %get-tuple-element.39), channel_id=1, source_target_pairs={{0,7},{1,0},{2,1},{3,2},{4,3},{5,4},{6,5},{7,6},{8,15},{9,8},{10,9... | collective-permute-start | bytes 196616 | tf_op jit(solution)/shard_map/ppermute | solution.py:415
  45.3 6.0 %collective-permute-start.7 = (bf16[1,2,4,16,512]{4,3,2,1,0:T(8,128)(2,1)S(1)}, bf16[1,2,4,16,512]{4,3,2,1,0:T(8,128)(2,1)S(1)}, u32[]{:S(2)}, u32[]{:S(2)}) collective-permute-start(bf16[1,2,4,16,512]{4,3,2,1,0:T(8,128)(2,1)S(1)} %get-tuple-element.34), channel_id=1, source_target_pairs={{0,16},{16,32},{32,48},{48,64},{64,80},{80,96},{96,112},{112,128},... | collective-permute-start | bytes 393224 | tf_op jit(solution)/shard_map/ppermute | solution.py:417
  45.4 5.9 %collective-permute-start.8 = (bf16[1,2,4,16,512]{4,3,2,1,0:T(8,128)(2,1)S(1)}, bf16[1,2,4,16,512]{4,3,2,1,0:T(8,128)(2,1)S(1)}, u32[]{:S(2)}, u32[]{:S(2)}) collective-permute-start(bf16[1,2,4,16,512]{4,3,2,1,0:T(8,128)(2,1)S(1)} %get-tuple-element.35), channel_id=1, source_target_pairs={{0,240},{16,0},{32,16},{48,32},{64,48},{80,64},{96,80},{112,96},{1... | collective-permute-start | bytes 393224 | tf_op jit(solution)/shard_map/ppermute | solution.py:418
  51.4 4.5 %copy-start.2 = (bf16[4,2,4,16,512]{4,3,2,1,0:T(8,128)(2,1)}, bf16[4,2,4,16,512]{4,3,2,1,0:T(8,128)(2,1)S(1)}, u32[]{:S(2)}) copy-start(bf16[4,2,4,16,512]{4,3,2,1,0:T(8,128)(2,1)S(1)} %pad_maximum_fusion.1) | copy-start | bytes 1572868
  51.4 2.9 %copy-start.9 = (bf16[128,2]{0,1:T(2,128)(2,1)S(1)}, bf16[128,2]{0,1:T(2,128)(2,1)}, u32[]{:S(2)}) copy-start(bf16[128,2]{0,1:T(2,128)(2,1)} %param.31) | copy-start | bytes 1540
  51.4 4.5 %collective-permute-start.9 = (bf16[4,2,4,16,512]{4,3,2,1,0:T(8,128)(2,1)S(1)}, bf16[4,2,4,16,512]{4,3,2,1,0:T(8,128)(2,1)S(1)}, u32[]{:S(2)}, u32[]{:S(2)}) collective-permute-start(bf16[4,2,4,16,512]{4,3,2,1,0:T(8,128)(2,1)S(1)} %pad_maximum_fusion.1), channel_id=1, source_target_pairs={{0,8},{8,0},{1,9},{9,1},{2,10},{10,2},{3,11},{11,3},{4,12},{12,4},... | collective-permute-start | bytes 1572872 | tf_op jit(solution)/shard_map/ppermute | solution.py:408
  55.9 0.8 copy-start.5
  63.5 1.4 collective-permute-start.10
  64.9 0.6 copy-start.6
  134.0 4.5 %collective-permute-start.11 = (f32[8,128]{1,0:T(8,128)}, f32[8,128]{1,0:T(8,128)S(1)}, u32[]{:S(2)}, u32[]{:S(2)}) collective-permute-start(f32[8,128]{1,0:T(8,128)} %get-tuple-element.28), channel_id=1, source_target_pairs={{0,8},{8,0},{1,9},{9,1},{2,10},{10,2},{3,11},{11,3},{4,12},{12,4},... | collective-permute-start | bytes 12296 | tf_op jit(solution)/shard_map/ppermute | solution.py:408
  139.2 0.7 copy-start.8

commit v2 on v1

--- a/solution.py
+++ b/solution.py
@@ -20,6 +20,8 @@
 BX, BY, BZ = 16, 128, 32
 ZPAD = 40
 
+NODES = (1, 9, 17, 25, 33)
+
 F32 = jnp.float32
 BF16 = jnp.bfloat16
 NN = (((1,), (0,)), ((), ()))
@@ -65,6 +67,17 @@
     for part in range(8):
         for point in range(35):
             zed[part, point] = table[:, (part * BZ + point - 1) % MESH]
+        for spare, node in enumerate(NODES):
+            zed[part, 35 + spare] = table[:, (part * BZ + node - 1) % MESH]
+    carry = np.zeros((128, 128), np.float32)
+    for point in range(35):
+        left = min(max((point - 1) // 8, 0), 3)
+        share = (point - NODES[left]) / 8.0
+        for third in range(3):
+            row = ZPAD * third + point
+            carry[row, ZPAD * third + 35 + left] = 1.0 - share
+            carry[row, ZPAD * third + 36 + left] = share
+    out["carry"] = carry.astype(BF16)
     out["basis_z"] = np_halves(zed.reshape(1024, MESH))
     exx = np.zeros((3, MESH, 16, 8))
     for third in range(3):
@@ -85,22 +98,33 @@
 
 
 def select_rows(octants):
-    wanted = jnp.transpose(jnp.broadcast_to(octants.astype(F32), (128, 128)))
+    slot = lax.broadcasted_iota(jnp.int32, (128, 8), 0)
+    group = lax.broadcasted_iota(jnp.int32, (128, 8), 1)
+    picker = jnp.where((slot >> 4) == group, 1.0, 0.0).astype(BF16)
+    listed = dot(picker, octants[...].astype(F32).astype(BF16))
+    spot = lax.broadcasted_iota(jnp.int32, listed.shape, 0) & 15
+    entry = lax.broadcasted_iota(jnp.int32, listed.shape, 1)
+    wanted = jnp.sum(jnp.where(spot == entry, listed, 0.0), axis=1, keepdims=True)
     lane = lax.broadcasted_iota(jnp.int32, (128, 128), 1).astype(F32)
     return jnp.where(wanted == lane, 1.0, 0.0).astype(BF16)
 
 
+def cell_rows(cells):
+    return [cells[:, 128 * d : 128 * d + 128].astype(F32) for d in range(3)]
+
+
 def geometry_rows(cells, fraction):
     return jnp.concatenate(
-        [cells.astype(F32), fraction.astype(F32), jnp.zeros((122, ATOMS), F32)], axis=0
-    )
-
-
-def prep_kernel(feats, fraction, cells, octants, out):
-    chosen = select_rows(octants[...])
+        cell_rows(cells) + [fraction[...].astype(F32), jnp.zeros((122, ATOMS), F32)], axis=0
+    )
+
+
+def prep_kernel(feats, fraction, cells, octants, out, geometry_out):
+    chosen = select_rows(octants)
     out[:, :512] = dot(chosen, feats[...]).astype(BF16)
-    geometry = jnp.transpose(geometry_rows(cells[...], fraction[...])).astype(BF16)
-    out[:, 512:] = dot(chosen, geometry).astype(BF16)
+    geometry = geometry_rows(cells, fraction)
+    out[:, 512:] = dot(chosen, jnp.transpose(geometry).astype(BF16)).astype(BF16)
+    geometry_out[...] = geometry[0:8]
 
 
 def table_rows(neighbours):
@@ -114,9 +138,10 @@
     is_ghost = (neighbours >= ATOMS) & (neighbours < 912)
     near = (ey == 1) | (ey == 2)
     half = jnp.where(near, ey - 1, jnp.where(ey == 0, 1, 0))
-    base = jnp.where(near, 128, 640)
+    base = jnp.where(near, 0, 512)
     row = base + ((ex * 2 + half) * 4 + ez) * 16 + spot
-    row = jnp.where(is_ghost, row, jnp.where(neighbours < ATOMS, neighbours, -1))
+    own = 144 + ((neighbours >> 5) << 6) + (neighbours & 31)
+    row = jnp.where(is_ghost, row, jnp.where(neighbours < ATOMS, own, -1))
 
     def offset(coord, span):
         moved = jnp.where(coord == 3, span, jnp.where(coord == 0, -span, 0))
@@ -127,6 +152,26 @@
 
 def transposed(x):
     return jnp.transpose(x.astype(F32)).astype(BF16)
+
+
+def fill_table(table, feats, near, far, count, geometry=None):
+    own = feats[...]
+    if geometry is not None:
+        own = jnp.concatenate([own, geometry], axis=1)
+    for q in range(4):
+        piece = near[128 * q : 128 * q + 128, :]
+        if q in (1, 2):
+            at = 64 * (q - 1)
+            piece = jnp.concatenate(
+                [
+                    piece[0:16], own[at : at + 32], piece[48:80], own[at + 32 : at + 64],
+                    piece[112:128],
+                ],
+                axis=0,
+            )
+        table[:, 128 * q : 128 * q + 128] = transposed(piece)[:count]
+        piece = far[128 * q : 128 * q + 128, :]
+        table[:, 512 + 128 * q : 640 + 128 * q] = transposed(piece)[:count]
 
 
 def gather_slots(rows, table, gathered, geometry=None):
@@ -134,7 +179,7 @@
         wanted = jnp.concatenate(
             [rows[2 * pair : 2 * pair + 1, :], rows[2 * pair + 1 : 2 * pair + 2, :]], axis=1
         )
-        spots = lax.broadcasted_iota(jnp.int32, (1152, 256), 0)
+        spots = lax.broadcasted_iota(jnp.int32, (1024, 256), 0)
         one_hot = jnp.where(spots == wanted, 1.0, 0.0).astype(BF16)
         found = dot(table[...], one_hot)
         lanes = slice(pair * 256, pair * 256 + 256)
@@ -191,17 +236,12 @@
     new, outgoing, unit, hidden_next, rows_out,
     table, gathered, geometry, radial, message,
 ):
-    table[:512, 0:128] = transposed(feats[...])
-    table[512:528, 0:128] = geometry_rows(cells[...], fraction[...])[:16].astype(BF16)
-    for start, piece in ((128, near), (640, far)):
-        for q in range(4):
-            lanes = slice(start + 128 * q, start + 128 * q + 128)
-            flipped = transposed(piece[128 * q : 128 * q + 128, :])
-            table[:, lanes] = flipped[:528]
+    own = jnp.transpose(geometry_rows(cells, fraction)).astype(BF16)
+    fill_table(table, feats, near, far, 528, own)
     rows, shifts = table_rows(neighbours[...])
     rows_out[...] = rows
     gather_slots(rows, table, gathered, geometry)
-    located = cells[...].astype(F32) + fraction[...].astype(F32)
+    located = jnp.concatenate(cell_rows(cells), axis=0) + fraction[...].astype(F32)
     delta = []
     for d in range(3):
         cell = jnp.concatenate(
@@ -227,20 +267,15 @@
     hidden_next[...] = silu(dot(radial_in[1], basis, TN)).astype(BF16)
     messages(hidden, radial_out[0], radial, gathered, unit, message)
     mixed(feats, message, mix_weight, 0, new)
-    outgoing[...] = dot(select_rows(octants[...]), new[...]).astype(BF16)
+    outgoing[...] = dot(select_rows(octants), new[...]).astype(BF16)
 
 
 def second_kernel(
     feats, near, far, rows, unit, hidden, radial_out, mix_weight, readout, kinds, species_table,
-    fraction, cells,
-    new, packed, base,
+    new, charge, base,
     table, gathered, radial, message,
 ):
-    table[:, 0:128] = transposed(feats[...])
-    for start, piece in ((128, near), (640, far)):
-        for q in range(4):
-            lanes = slice(start + 128 * q, start + 128 * q + 128)
-            table[:, lanes] = transposed(piece[128 * q : 128 * q + 128, :])
+    fill_table(table, feats, near, far, 512)
     gather_slots(rows[...], table, gathered)
     messages(hidden[...], radial_out[1], radial, gathered, unit, message)
     mixed(feats, message, mix_weight, 1, new)
@@ -249,15 +284,7 @@
     energy = jnp.where(second, species_table[1, 0], species_table[0, 0])
     offset = jnp.where(second, species_table[1, 1], species_table[0, 1])
     base[...] = heads[0:1, :] + energy
-    packed[...] = jnp.concatenate(
-        [
-            heads[1:2, :] + offset,
-            fraction[...].astype(F32),
-            cells[...].astype(F32),
-            jnp.zeros((1, ATOMS), F32),
-        ],
-        axis=0,
-    )
+    charge[...] = heads[1:2, :] + offset
 
 
 def spline(t):
@@ -294,42 +321,58 @@
     return tiles
 
 
-def both_atoms(own, other):
+def static_kernel(own, other, high, low, weight_y, slope_y, planes):
     both = jnp.concatenate([own[...], other[...]], axis=1)
-    return both, [both[4 + d : 5 + d, :].astype(jnp.int32) for d in range(3)]
-
-
-def charges_kernel(own, other, high, low, out, weight_y, slope_y):
-    both, cells = both_atoms(own, other)
+    cells = [both[d : d + 1, :].astype(jnp.int32) for d in range(3)]
     half = lax.axis_index("gy")
     lane = lax.broadcasted_iota(jnp.int32, (1, 256), 1)
     domain = jnp.where(lane < 128, half, 1 - half)
     rows = pl.ds(pl.multiple_of(half * 128, 128), 128)
     table = (high[rows, :], low[rows, :])
-    weights, slopes = spline(both[2:3, :])
+    weights, slopes = spline(both[4:5, :])
     spots = [(cells[1] + domain * BY + (m - 1)) & (MESH - 1) for m in range(4)]
-    along_y = dot3(table, halves(spread(weights, spots, MESH)))
-    weight_y[...] = along_y
+    weight_y[...] = dot3(table, halves(spread(weights, spots, MESH)))
     slope_y[...] = dot3(table, halves(spread(slopes, spots, MESH)))
-    charged = halves(along_y * both[0:1, :])
-    along_x = spread(spline(both[1:2, :])[0], [cells[0] + m for m in range(4)], 24)
-    along_z = spread(spline(both[3:4, :])[0], [cells[2] + m for m in range(4)], ZPAD)
-    for group, tile in enumerate(planes_of(along_x, along_z)):
-        out[:, group, :] = dot3(charged, halves(tile), NT)
-    out[:, 7, :] = jnp.zeros((128, 128), F32)
+    weights_x, slopes_x = spline(both[3:4, :])
+    weights_z, slopes_z = spline(both[5:6, :])
+    spots_x = [cells[0] + m for m in range(4)]
+    spots_z = [cells[2] + m for m in range(4)]
+    along_x = spread(weights_x, spots_x, 24)
+    along_z = spread(weights_z, spots_z, ZPAD)
+    down_x = spread(slopes_x, spots_x, 24)
+    down_z = spread(slopes_z, spots_z, ZPAD)
+    for kind, (ax, az) in enumerate(
+        ((along_x, along_z), (down_x, along_z), (along_x, down_z))
+    ):
+        for group, tile in enumerate(planes_of(ax, az)):
+            tile_high, tile_low = halves(tile)
+            planes[2 * kind, 128 * group : 128 * group + 128, :] = tile_high
+            planes[2 * kind + 1, 128 * group : 128 * group + 128, :] = tile_low
+
+
+def charges_kernel(own, other, weight_y, planes, carry, out, lines):
+    charge = jnp.concatenate([own[...], other[...]], axis=1)
+    charged = halves(weight_y[...] * charge)
+    for group in range(7):
+        rows = slice(128 * group, 128 * group + 128)
+        line = dot3(charged, (planes[0, rows, :], planes[1, rows, :]), NT)
+        kept = line.astype(BF16).astype(F32)
+        lines[:, group, :] = kept + dot((line - kept).astype(BF16), carry[...])
+    lines[:, 7, :] = jnp.zeros((128, 128), F32)
+    out[...] = lines[...].astype(BF16)
 
 
 def waves_kernel(
-    scale_y, received, zh, zl, xh, xl, th, tl, col, row, out, lhs,
+    scale_y, received, zh, zl, xh, xl, th, tl, col, row, out, coming, lhs,
 ):
     for part in range(8):
         lanes = slice(part * 128, part * 128 + 128)
-        block = received[part]
+        block = received[part].astype(F32)
         for third in range(3):
             moved = block if third == 0 else pltpu.roll(block, 128 - ZPAD * third, 1)
-            lhs[third * 128 : third * 128 + 128, lanes] = moved
+            coming[third * 128 : third * 128 + 128, lanes] = moved.astype(BF16)
     zed = (zh[...], zl[...])
-    lines = dot3(halves(lhs[...]), zed)
+    lines = dot(coming[...], zed[0]) + dot(coming[...], zed[1])
     total = jnp.zeros((MESH, MESH), F32)
     for third in range(3):
         total += dot3(
@@ -355,28 +398,19 @@
         out[part] = block
 
 
-def forces_kernel(own, other, weight_y, slope_y, returned, out_own, out_other):
-    both, cells = both_atoms(own, other)
+def forces_kernel(weight_y, slope_y, planes, returned, out_own, out_other):
     flat = halves(jnp.concatenate([returned[:, group, :] for group in range(7)], axis=1))
-    weights_x, slopes_x = spline(both[1:2, :])
-    weights_z, slopes_z = spline(both[3:4, :])
-    spots_x = [cells[0] + m for m in range(4)]
-    spots_z = [cells[2] + m for m in range(4)]
-    along_x = spread(weights_x, spots_x, 24)
-    along_z = spread(weights_z, spots_z, ZPAD)
-    down_x = spread(slopes_x, spots_x, 24)
-    down_z = spread(slopes_z, spots_z, ZPAD)
-
-    def level(ax, az):
-        return dot3(flat, halves(jnp.concatenate(planes_of(ax, az), axis=0)))
-
-    level_0 = level(along_x, along_z)
-    wy = weight_y[...]
+
+    def level(kind):
+        return dot3(flat, (planes[2 * kind], planes[2 * kind + 1]))
+
+    level_0 = level(0)
+    along_y = weight_y[...]
     rows = [
-        jnp.sum(wy * level_0, axis=0, keepdims=True),
-        jnp.sum(wy * level(down_x, along_z), axis=0, keepdims=True),
+        jnp.sum(along_y * level_0, axis=0, keepdims=True),
+        jnp.sum(along_y * level(1), axis=0, keepdims=True),
         jnp.sum(slope_y[...] * level_0, axis=0, keepdims=True),
-        jnp.sum(wy * level(along_x, down_z), axis=0, keepdims=True),
+        jnp.sum(along_y * level(2), axis=0, keepdims=True),
         jnp.zeros((4, 256), F32),
     ]
     total = jnp.concatenate(rows, axis=0)
@@ -384,17 +418,25 @@
     out_other[...] = total[:, 128:256]
 
 
+def final_kernel(here, there, charge, base, energy, force):
+    total = here[...] + there[...]
+    energy[...] = base[...] + 0.5 * charge[...] * total[0:1, :]
+    for d in range(3):
+        force[:, 128 * d : 128 * d + 128] = -charge[...] * total[1 + d : 2 + d, :]
+
+
 VMEM = pl.BlockSpec(memory_space=pltpu.VMEM)
 SMEM = pl.BlockSpec(memory_space=pltpu.SMEM)
 
 
-def call(kernel, outs, *args, scratch=(), scalars=()):
+def call(kernel, outs, *args, scratch=(), scalars=(), limit=16):
     specs = [SMEM if i in scalars else VMEM for i in range(len(args))]
     return pl.pallas_call(
         kernel,
         out_shape=[jax.ShapeDtypeStruct(s, d) for s, d in outs],
         in_specs=specs,
         out_specs=[VMEM] * len(outs),
+        compiler_params=pltpu.CompilerParams(vmem_limit_bytes=limit << 20),
         scratch_shapes=[pltpu.VMEM(s, d) for s, d in scratch],
     )(*args)
 
@@ -431,14 +473,21 @@
     table = constants()
     feats = features[0, 0, 0]
     part = fraction[0, 0, 0]
-    cells = cell_index[0, 0, 0]
+    cells = cell_index.reshape(1, 3 * ATOMS)
     kinds = species.reshape(1, ATOMS)
-    octants = jnp.pad(octant_rows[0, 0, 0], ((0, 0), (0, 2)), constant_values=-1).reshape(1, 128)
+    octants = octant_rows[0, 0, 0]
     links = neighbours[0, 0, 0]
     heads = jnp.pad(jnp.transpose(readout), ((0, 6), (0, 0)))
 
-    (outgoing,) = call(prep_kernel, [((128, 640), BF16)], feats, part, cells, octants)
+    outgoing, places = call(
+        prep_kernel, [((128, 640), BF16), ((8, 128), F32)], feats, part, cells, octants
+    )
     near, far = ghosts(outgoing)
+    weight_y, slope_y, planes = call(
+        static_kernel,
+        [((128, 256), F32), ((128, 256), F32), ((6, 896, 256), BF16)],
+        places, partner(places), *table["basis_y"],
+    )
     feats, outgoing, unit, hidden, rows = call(
         first_kernel,
         [
@@ -450,32 +499,33 @@
         ],
         feats, near, far, part, cells, octants, links, radial_in, radial_out, mix_weight,
         scratch=[
-            ((528, 1152), BF16),
+            ((528, 1024), BF16),
             ((512, 2048), BF16),
             ((8, 2048), F32),
             ((512, 2048), F32),
             ((512, 128), BF16),
         ],
+        limit=24,
     )
     near, far = ghosts(outgoing)
-    feats, packed, base = call(
+    feats, charge, base = call(
         second_kernel,
-        [((128, 512), BF16), ((8, 128), F32), ((1, 128), F32)],
+        [((128, 512), BF16), ((1, 128), F32), ((1, 128), F32)],
         feats, near, far, rows, unit, hidden, radial_out, mix_weight, heads, kinds, species_table,
-        part, cells,
         scalars=(10,),
         scratch=[
-            ((512, 1152), BF16),
+            ((512, 1024), BF16),
             ((512, 2048), BF16),
             ((512, 2048), F32),
             ((512, 128), BF16),
         ],
-    )
-    other = partner(packed)
-    lines, weight_y, slope_y = call(
+        limit=24,
+    )
+    (lines,) = call(
         charges_kernel,
-        [((128, 8, 128), F32), ((128, 256), F32), ((128, 256), F32)],
-        packed, other, *table["basis_y"],
+        [((128, 8, 128), BF16)],
+        charge, partner(charge), weight_y, planes, table["carry"],
+        scratch=[((128, 8, 128), F32)],
     )
     received = across(lines).reshape(8, 128, 128)
     (waves,) = call(
@@ -484,19 +534,22 @@
         table["scale_y"], received, *table["basis_z"], *table["basis_x"], *table["basis_xt"],
         table["col"], table["row"],
         scalars=(0,),
-        scratch=[((384, 1024), F32)],
+        scratch=[((384, 1024), BF16), ((384, 1024), F32)],
     )
     returned = across(waves.reshape(128, 8, 128))
     here, there = call(
         forces_kernel,
         [((8, 128), F32), ((8, 128), F32)],
-        packed, other, weight_y, slope_y, returned,
-    )
-    total = here + partner(there)
-    charge = packed[0:1]
-    force = -charge * total[1:4]
-    energy = base + 0.5 * charge * total[0:1]
-    return feats[None, None, None], energy.reshape(1, 1, 1, ATOMS), force[None, None, None]
+        weight_y, slope_y, planes, returned,
+    )
+    energy, force = call(
+        final_kernel, [((1, 128), F32), ((1, 384), F32)], here, partner(there), charge, base
+    )
+    return (
+        feats[None, None, None],
+        energy.reshape(1, 1, 1, ATOMS),
+        force.reshape(1, 1, 1, 3, ATOMS),
+    )
 
 
 def solution(mesh):

time: 142 us -> 119 us (0.84)
  Pallas kernels: 28.8 us -> 19.6 us
  blocking collectives: 56 us -> 50.2 us
  local copies, waits for them, and re-layouts: 7.95 us -> 3.19 us
  other arithmetic: 2.13 us -> 0.26 us
    pallas_call x6 -> x8, Pallas kernels: 28.8 us -> 19.6 us  [call(): pl.pallas_call(kernel, out_shape=[jax.ShapeDtypeStruct(s, d) for s, d in...]
    all_to_all x2, blocking collectives: 56 us -> 50.2 us  [across(): lax.all_to_all(blocks, ('gz', 'gx'), split_axis=0, concat_axis=0, tiled=T...]
    slice x2, local copies, waits for them, and re-layouts: 1.9 us -> 0.03 us  [ghosts(): before = lax.ppermute(x[:, :, 1:], 'gz', ring('gz', 1))]
    unnamed x22 -> x54, local copies, waits for them, and re-layouts: 4.81 us -> 3.11 us
    ppermute x4 -> x5, waiting for transfers between devices: 4.73 us -> 3.8 us  [partner(): return lax.ppermute(block, 'gy', [(0, 1), (1, 0)])]
    ppermute x4 -> x5, starting transfers between devices: 8.98 us -> 8.42 us  [partner(): return lax.ppermute(block, 'gy', [(0, 1), (1, 0)])]
  transfers between devices with their start and end apart: 12 -> 13, of which waited for: 10 -> 9; matrix products, arithmetic and copies ran while one was open for 0% -> 0% of each run, Pallas kernels for 0% -> 6%
where the time goes in v2:
time: 119 us
  blocking collectives  50.2 us (42%)
  starting transfers between devices  30.4 us (26%)
  Pallas kernels  19.6 us (16%)
  waiting for transfers between devices  14.2 us (12%)
  local copies, waits for them, and re-layouts  3.19 us (3%)
    all_to_all x2, blocking collectives, across(): lax.all_to_all(blocks, ('gz', 'gx'), split_axis=0, concat_axis=0, tiled=T...  50.2 us
    pallas_call x8, Pallas kernels, call(): pl.pallas_call(kernel, out_shape=[jax.ShapeDtypeStruct(s, d) for s, d in...  19.6 us
    ppermute x5, starting transfers between devices, partner(): return lax.ppermute(block, 'gy', [(0, 1), (1, 0)])  8.42 us
    ppermute x2, starting transfers between devices, ghosts(): after = lax.ppermute(x[:1], 'gx', ring('gx', -1))  8 us
    ppermute x2, starting transfers between devices, ghosts(): before = lax.ppermute(x[:, :, 1:], 'gz', ring('gz', 1))  6.92 us
    ppermute x2, waiting for transfers between devices, ghosts(): before = lax.ppermute(x[1:], 'gx', ring('gx', 1))  5.31 us
    ppermute x2, starting transfers between devices, ghosts(): after = lax.ppermute(x[:, :, :1], 'gz', ring('gz', -1))  4.93 us
    ppermute x5, waiting for transfers between devices, partner(): return lax.ppermute(block, 'gy', [(0, 1), (1, 0)])  3.8 us
  transfers between devices with their start and end apart: 13, of which 9 were waited for; matrix products, arithmetic and copies ran while one was open for 0% of the time, Pallas kernels for 6%

profile of v2, /device:TPU:1, one launch (start us, length us, event | category | flops | bytes accessed | tf_op | source)
XLA Modules:
  0.0 118.8 jit_solution(15311411583074172108)
XLA Ops:
  0.7 0.9 copy-done.4
  1.6 0.7 copy-done.14
  2.3 0.7 copy-done.18
  3.0 0.7 copy-done.21
  3.7 0.4 shard_map.238
  4.1 3.6 %collective-permute-start = (bf16[2,2,1,16,640]{4,3,2,1,0:T(8,128)(2,1)S(1)}, bf16[2,2,1,16,640]{4,3,2,1,0:T(8,128)(2,1)S(1)}, u32[]{:S(2)}, u32[]{:S(2)}) collective-permute-start(bf16[2,2,1,16,640]{4,3,2,1,0:T(8,128)(2,1)S(1)} %get-tuple-element.47), channel_id=1, source_target_pairs={{0,1},{1,2},{2,3},{3,4},{4,5},{5,6},{6,7},{7,0},{8,9},{9,10},{10,1... | collective-permute-start | bytes 245768 | tf_op jit(solution)/shard_map/ppermute | solution.py:456
  7.8 2.5 %collective-permute-start.1 = (bf16[2,2,1,16,640]{4,3,2,1,0:T(8,128)(2,1)S(1)}, bf16[2,2,1,16,640]{4,3,2,1,0:T(8,128)(2,1)S(1)}, u32[]{:S(2)}, u32[]{:S(2)}) collective-permute-start(bf16[2,2,1,16,640]{4,3,2,1,0:T(8,128)(2,1)S(1)} %get-tuple-element.48), channel_id=1, source_target_pairs={{0,7},{1,0},{2,1},{3,2},{4,3},{5,4},{6,5},{7,6},{8,15},{9,8},{10,9... | collective-permute-start | bytes 245768 | tf_op jit(solution)/shard_map/ppermute | solution.py:457
  10.3 1.7 %collective-permute-done = bf16[2,2,1,16,640]{4,3,2,1,0:T(8,128)(2,1)S(1)} collective-permute-done((bf16[2,2,1,16,640]{4,3,2,1,0:T(8,128)(2,1)S(1)}, bf16[2,2,1,16,640]{4,3,2,1,0:T(8,128)(2,1)S(1)}, u32[]{:S(2)}, u32[]{:S(2)}) %collective-permute-start) | collective-permute-done | bytes 81952 | tf_op jit(solution)/shard_map/ppermute | solution.py:456
  12.0 0.8 collective-permute-done.1
  13.0 2.0 %collective-permute-start.2 = (bf16[1,2,4,16,640]{4,3,2,1,0:T(8,128)(2,1)S(1)}, bf16[1,2,4,16,640]{4,3,2,1,0:T(8,128)(2,1)S(1)}, u32[]{:S(2)}, u32[]{:S(2)}) collective-permute-start(bf16[1,2,4,16,640]{4,3,2,1,0:T(8,128)(2,1)S(1)} %get-tuple-element.43), channel_id=1, source_target_pairs={{0,16},{16,32},{32,48},{48,64},{64,80},{80,96},{96,112},{112,128},... | collective-permute-start | bytes 491528 | tf_op jit(solution)/shard_map/ppermute | solution.py:459
  15.0 4.4 %collective-permute-start.3 = (bf16[1,2,4,16,640]{4,3,2,1,0:T(8,128)(2,1)S(1)}, bf16[1,2,4,16,640]{4,3,2,1,0:T(8,128)(2,1)S(1)}, u32[]{:S(2)}, u32[]{:S(2)}) collective-permute-start(bf16[1,2,4,16,640]{4,3,2,1,0:T(8,128)(2,1)S(1)} %get-tuple-element.44), channel_id=1, source_target_pairs={{0,240},{16,0},{32,16},{48,32},{64,48},{80,64},{96,80},{112,96},{1... | collective-permute-start | bytes 491528 | tf_op jit(solution)/shard_map/ppermute | solution.py:460
  19.4 3.0 %collective-permute-done.2 = bf16[1,2,4,16,640]{4,3,2,1,0:T(8,128)(2,1)S(1)} collective-permute-done((bf16[1,2,4,16,640]{4,3,2,1,0:T(8,128)(2,1)S(1)}, bf16[1,2,4,16,640]{4,3,2,1,0:T(8,128)(2,1)S(1)}, u32[]{:S(2)}, u32[]{:S(2)}) %collective-permute-start.2) | collective-permute-done | bytes 163872 | tf_op jit(solution)/shard_map/ppermute | solution.py:459
  22.4 0.1 pad_maximum_fusion
  22.5 2.2 %collective-permute-start.4 = (bf16[4,2,4,16,640]{4,3,2,1,0:T(8,128)(2,1)S(1)}, bf16[4,2,4,16,640]{4,3,2,1,0:T(8,128)(2,1)S(1)}, u32[]{:S(2)}, u32[]{:S(2)}) collective-permute-start(bf16[4,2,4,16,640]{4,3,2,1,0:T(8,128)(2,1)S(1)} %pad_maximum_fusion), channel_id=1, source_target_pairs={{0,8},{8,0},{1,9},{9,1},{2,10},{10,2},{3,11},{11,3},{4,12},{12,4},... | collective-permute-start | bytes 1966088 | tf_op jit(solution)/shard_map/ppermute | solution.py:450
  24.7 1.7 %collective-permute-done.4 = bf16[4,2,4,16,640]{4,3,2,1,0:T(8,128)(2,1)S(1)} collective-permute-done((bf16[4,2,4,16,640]{4,3,2,1,0:T(8,128)(2,1)S(1)}, bf16[4,2,4,16,640]{4,3,2,1,0:T(8,128)(2,1)S(1)}, u32[]{:S(2)}, u32[]{:S(2)}) %collective-permute-start.4) | collective-permute-done | bytes 655392 | tf_op jit(solution)/shard_map/ppermute | solution.py:450
  26.5 0.0 copy-start.11
  26.5 0.0 copy-start.12
  26.5 0.0 copy-start.13
  26.5 5.1 %shard_map.239 = (bf16[128,512]{1,0:T(8,128)(2,1)S(1)}, bf16[128,512]{1,0:T(8,128)(2,1)S(1)}, f32[48,128]{1,0:T(8,128)S(1)}, bf16[64,2048]{1,0:T(8,128)(2,1)S(1)}, s32[16,128]{1,0:T(8,128)S(1)}) custom-call(bf16[128,512]{1,0:T(8,128)(2,1)S(1)} %bitcast.30, bf16[512,640]{1,0:T(8,128)(2,1)S(1)} %bitcast.18, bf16[512,640]{1,0:T(8,128)(2,1)S(1)} %bitcast.28, ...), custom_call_target="tpu_custom_call" | custom-call | tf_op jit(solution)/shard_map/pallas_call | solution.py:434
  31.6 3.3 %collective-permute-start.5 = (bf16[2,2,1,16,512]{4,3,2,1,0:T(8,128)(2,1)S(1)}, bf16[2,2,1,16,512]{4,3,2,1,0:T(8,128)(2,1)S(1)}, u32[]{:S(2)}, u32[]{:S(2)}) collective-permute-start(bf16[2,2,1,16,512]{4,3,2,1,0:T(8,128)(2,1)S(1)} %get-tuple-element.49), channel_id=1, source_target_pairs={{0,1},{1,2},{2,3},{3,4},{4,5},{5,6},{6,7},{7,0},{8,9},{9,10},{10,1... | collective-permute-start | bytes 196616 | tf_op jit(solution)/shard_map/ppermute | solution.py:456
  34.9 2.4 %collective-permute-start.6 = (bf16[2,2,1,16,512]{4,3,2,1,0:T(8,128)(2,1)S(1)}, bf16[2,2,1,16,512]{4,3,2,1,0:T(8,128)(2,1)S(1)}, u32[]{:S(2)}, u32[]{:S(2)}) collective-permute-start(bf16[2,2,1,16,512]{4,3,2,1,0:T(8,128)(2,1)S(1)} %get-tuple-element.50), channel_id=1, source_target_pairs={{0,7},{1,0},{2,1},{3,2},{4,3},{5,4},{6,5},{7,6},{8,15},{9,8},{10,9... | collective-permute-start | bytes 196616 | tf_op jit(solution)/shard_map/ppermute | solution.py:457
  37.3 2.0 %collective-permute-done.5 = bf16[2,2,1,16,512]{4,3,2,1,0:T(8,128)(2,1)S(1)} collective-permute-done((bf16[2,2,1,16,512]{4,3,2,1,0:T(8,128)(2,1)S(1)}, bf16[2,2,1,16,512]{4,3,2,1,0:T(8,128)(2,1)S(1)}, u32[]{:S(2)}, u32[]{:S(2)}) %collective-permute-start.5) | collective-permute-done | bytes 65568 | tf_op jit(solution)/shard_map/ppermute | solution.py:456
  39.3 0.5 collective-permute-done.6
  39.9 0.1 collective-permute-start.7
  40.0 3.6 %collective-permute-start.8 = (bf16[1,2,4,16,512]{4,3,2,1,0:T(8,128)(2,1)S(1)}, bf16[1,2,4,16,512]{4,3,2,1,0:T(8,128)(2,1)S(1)}, u32[]{:S(2)}, u32[]{:S(2)}) collective-permute-start(bf16[1,2,4,16,512]{4,3,2,1,0:T(8,128)(2,1)S(1)} %get-tuple-element.46), channel_id=1, source_target_pairs={{0,240},{16,0},{32,16},{48,32},{64,48},{80,64},{96,80},{112,96},{1... | collective-permute-start | bytes 393224 | tf_op jit(solution)/shard_map/ppermute | solution.py:460
  43.5 2.4 %collective-permute-done.7 = bf16[1,2,4,16,512]{4,3,2,1,0:T(8,128)(2,1)S(1)} collective-permute-done((bf16[1,2,4,16,512]{4,3,2,1,0:T(8,128)(2,1)S(1)}, bf16[1,2,4,16,512]{4,3,2,1,0:T(8,128)(2,1)S(1)}, u32[]{:S(2)}, u32[]{:S(2)}) %collective-permute-start.7) | collective-permute-done | bytes 131104 | tf_op jit(solution)/shard_map/ppermute | solution.py:459
  45.9 0.1 pad_maximum_fusion.1
  46.0 2.7 %collective-permute-start.9 = (bf16[4,2,4,16,512]{4,3,2,1,0:T(8,128)(2,1)S(1)}, bf16[4,2,4,16,512]{4,3,2,1,0:T(8,128)(2,1)S(1)}, u32[]{:S(2)}, u32[]{:S(2)}) collective-permute-start(bf16[4,2,4,16,512]{4,3,2,1,0:T(8,128)(2,1)S(1)} %pad_maximum_fusion.1), channel_id=1, source_target_pairs={{0,8},{8,0},{1,9},{9,1},{2,10},{10,2},{3,11},{11,3},{4,12},{12,4},... | collective-permute-start | bytes 1572872 | tf_op jit(solution)/shard_map/ppermute | solution.py:450
  48.7 0.3 collective-permute-start.10
  49.0 1.2 %collective-permute-done.9 = bf16[4,2,4,16,512]{4,3,2,1,0:T(8,128)(2,1)S(1)} collective-permute-done((bf16[4,2,4,16,512]{4,3,2,1,0:T(8,128)(2,1)S(1)}, bf16[4,2,4,16,512]{4,3,2,1,0:T(8,128)(2,1)S(1)}, u32[]{:S(2)}, u32[]{:S(2)}) %collective-permute-start.9) | collective-permute-done | bytes 524320 | tf_op jit(solution)/shard_map/ppermute | solution.py:450
  50.2 0.0 copy-start.6
  50.3 0.0 copy-start.7
  50.3 0.0 copy-start.8
  50.3 0.0 copy-start.9
  50.3 0.0 copy-start.10
  50.3 0.0 copy-start.17
  50.3 0.0 copy-start.23
  50.3 5.6 %shard_map.240 = (bf16[128,512]{1,0:T(8,128)(2,1)}, f32[1,128]{1,0:T(1,128)S(1)}, f32[1,128]{1,0:T(1,128)S(1)}) custom-call(bf16[128,512]{1,0:T(8,128)(2,1)S(1)} %get-tuple-element.21.feats, bf16[512,512]{1,0:T(8,128)(2,1)S(1)} %bitcast.20, bf16[512,512]{1,0:T(8,128)(2,1)S(1)} %bitcast.31, s32[16,128]{1,0:T(8,128)S(1)} %get-tuple-element.23.rows, ...), custom_call_target="tpu_custom_call" | custom-call | tf_op jit(solution)/shard_map/pallas_call | solution.py:434
  55.9 0.4 collective-permute-start.11
  56.3 0.9 shard_map.241
  57.3 1.4 %shard_map.242 = bf16[128,8,128]{2,1,0:T(8,128)(2,1)S(1)} custom-call(f32[1,128]{1,0:T(1,128)S(1)} %get-tuple-element.31.own.charge, f32[1,128]{1,0:T(1,128)S(1)} %collective-permute-done.11.other, f32[128,256]{1,0:T(8,128)S(1)} %get-tuple-element.28.weight_y, bf16[6,896,256]{2,1,0:T(8,128)(2,1)S(1)} %get-tuple-element.30.planes, bf16[128,128]{1,0:T(8,128)(2,1)S(1)} %copy-done.13), custom_call_target="tpu_custom_call" | custom-call | tf_op jit(solution)/shard_map/pallas_call | solution.py:434
  58.7 25.4 %all_to_all.10 = bf16[128,8,128]{2,1,0:T(8,128)(2,1)S(1)} all-to-all(bf16[128,8,128]{2,1,0:T(8,128)(2,1)S(1)} %shard_map.242), channel_id=1, replica_groups=mesh['gx'=16,'gy'=2,'gz'=8] {'gz','gx'}, dimensions={0} | all-to-all | bytes 524288 | tf_op jit(solution)/shard_map/all_to_all | solution.py:466
  84.2 4.6 %shard_map.243 = f32[8,128,128]{2,1,0:T(8,128)S(1)} custom-call(f32[256]{0:T(256)S(1)} %copy-done.23, bf16[8,128,128]{2,1,0:T(8,128)(2,1)S(1)} %bitcast.27, bf16[1024,256]{1,0:T(8,128)(2,1)S(1)} %copy-done.1, bf16[1024,256]{1,0:T(8,128)(2,1)S(1)} %copy-done, bf16[3,256,128]{2,1,0:T(8,128)(2,1)S(1)} %copy-done.9, bf16[3,256,128]{2,1,0:T(8,128)(2,1)S(1)} %copy-done.8, ...), custom_call_target="tpu_custom_call" | custom-call | tf_op jit(solution)/shard_map/pallas_call | solution.py:434
  88.8 24.8 %all_to_all.11.returned = f32[128,8,128]{2,1,0:T(8,128)S(1)} all-to-all(f32[128,8,128]{2,1,0:T(8,128)S(1)} %bitcast.19), channel_id=1, replica_groups=mesh['gx'=16,'gy'=2,'gz'=8] {'gz','gx'}, dimensions={0} | all-to-all | bytes 1048576 | tf_op jit(solution)/shard_map/all_to_all | solution.py:466
  113.6 1.0 shard_map.244
  114.6 2.8 %collective-permute-start.12 = (f32[8,128]{1,0:T(8,128)S(1)}, f32[8,128]{1,0:T(8,128)S(1)}, u32[]{:S(2)}, u32[]{:S(2)}) collective-permute-start(f32[8,128]{1,0:T(8,128)S(1)} %get-tuple-element.33), channel_id=1, source_target_pairs={{0,8},{8,0},{1,9},{9,1},{2,10},{10,2},{3,11},{11,3},{4,12},{12,4},... | collective-permute-start | bytes 12296 | tf_op jit(solution)/shard_map/ppermute | solution.py:450
  117.4 0.8 collective-permute-done.12.there
  118.2 0.6 shard_map.245
  (51 shorter events, 0.3 us)
Async XLA Ops:
  0.6 25.8 %copy-start.3 = (bf16[2,2,128,128]{3,2,1,0:T(8,128)(2,1)S(1)}, bf16[2,2,128,128]{3,2,1,0:T(8,128)(2,1)}, u32[]{:S(2)}) copy-start(bf16[2,2,128,128]{3,2,1,0:T(8,128)(2,1)} %mix_weight.3) | copy-start | bytes 393220
  0.6 25.8 %copy-start.2 = (bf16[2,64,512]{2,1,0:T(8,128)(2,1)S(1)}, bf16[2,64,512]{2,1,0:T(8,128)(2,1)}, u32[]{:S(2)}) copy-start(bf16[2,64,512]{2,1,0:T(8,128)(2,1)} %radial_out.3) | copy-start | bytes 393220
  0.7 0.9 copy-start.4
  1.6 0.7 copy-start.14
  2.3 0.7 copy-start.18
  3.0 0.7 copy-start.21
  3.6 22.8 %copy-start.5 = (bf16[1,1,1,128,512]{4,3,2,1,0:T(8,128)(2,1)S(1)}, bf16[1,1,1,128,512]{4,3,2,1,0:T(8,128)(2,1)}, u32[]{:S(2)}) copy-start(bf16[1,1,1,128,512]{4,3,2,1,0:T(8,128)(2,1)} %param.23) | copy-start | bytes 393220
  3.6 22.8 %copy-start.15 = (s32[1,1,1,8,14]{4,3,2,1,0:T(8,128)S(1)}, s32[1,1,1,8,14]{4,3,2,1,0:T(8,128)}, u32[]{:S(2)}) copy-start(s32[1,1,1,8,14]{4,3,2,1,0:T(8,128)} %param.27) | copy-start | bytes 1348
  3.7 22.8 %copy-start.16 = (s32[1,1,1,16,128]{4,3,2,1,0:T(8,128)S(1)}, s32[1,1,1,16,128]{4,3,2,1,0:T(8,128)}, u32[]{:S(2)}) copy-start(s32[1,1,1,16,128]{4,3,2,1,0:T(8,128)} %param.28) | copy-start | bytes 24580
  3.7 22.8 %copy-start.19 = (s32[1,1,1,3,128]{4,2,3,1,0:T(1,128)S(1)}, s32[1,1,1,3,128]{4,2,3,1,0:T(1,128)}, u32[]{:S(2)}) copy-start(s32[1,1,1,3,128]{4,2,3,1,0:T(1,128)} %param.25) | copy-start | bytes 4612
  3.7 22.8 %copy-start.20 = (bf16[2,8,64]{2,1,0:T(8,128)(2,1)S(1)}, bf16[2,8,64]{2,1,0:T(8,128)(2,1)}, u32[]{:S(2)}) copy-start(bf16[2,8,64]{2,1,0:T(8,128)(2,1)} %radial_in.1) | copy-start | bytes 6148
  3.7 22.8 %copy-start.22 = (bf16[1,1,1,3,128]{4,3,2,1,0:T(4,128)(2,1)S(1)}, bf16[1,1,1,3,128]{4,3,2,1,0:T(4,128)(2,1)}, u32[]{:S(2)}) copy-start(bf16[1,1,1,3,128]{4,3,2,1,0:T(4,128)(2,1)} %param.24) | copy-start | bytes 2308
  4.1 7.9 %collective-permute-start = (bf16[2,2,1,16,640]{4,3,2,1,0:T(8,128)(2,1)S(1)}, bf16[2,2,1,16,640]{4,3,2,1,0:T(8,128)(2,1)S(1)}, u32[]{:S(2)}, u32[]{:S(2)}) collective-permute-start(bf16[2,2,1,16,640]{4,3,2,1,0:T(8,128)(2,1)S(1)} %get-tuple-element.47), channel_id=1, source_target_pairs={{0,1},{1,2},{2,3},{3,4},{4,5},{5,6},{6,7},{7,0},{8,9},{9,10},{10,1... | collective-permute-start | bytes 245768 | tf_op jit(solution)/shard_map/ppermute | solution.py:456
  7.8 5.1 %collective-permute-start.1 = (bf16[2,2,1,16,640]{4,3,2,1,0:T(8,128)(2,1)S(1)}, bf16[2,2,1,16,640]{4,3,2,1,0:T(8,128)(2,1)S(1)}, u32[]{:S(2)}, u32[]{:S(2)}) collective-permute-start(bf16[2,2,1,16,640]{4,3,2,1,0:T(8,128)(2,1)S(1)} %get-tuple-element.48), channel_id=1, source_target_pairs={{0,7},{1,0},{2,1},{3,2},{4,3},{5,4},{6,5},{7,6},{8,15},{9,8},{10,9... | collective-permute-start | bytes 245768 | tf_op jit(solution)/shard_map/ppermute | solution.py:457
  12.9 36.1 %copy-start.26 = (bf16[128,2]{0,1:T(2,128)(2,1)S(1)}, bf16[128,2]{0,1:T(2,128)(2,1)}, u32[]{:S(2)}) copy-start(bf16[128,2]{0,1:T(2,128)(2,1)} %param.32) | copy-start | bytes 1540
  12.9 37.3 %copy-start.24 = (f32[2,2]{1,0:T(2,128)S(1)}, f32[2,2]{1,0:T(2,128)}, u32[]{:S(2)}) copy-start(f32[2,2]{1,0:T(2,128)} %species_table.1) | copy-start | bytes 52
  12.9 37.3 %copy-start.25 = (s32[1,1,1,128]{3,2,1,0:T(1,128)S(1)}, s32[1,1,1,128]{3,2,1,0:T(1,128)}, u32[]{:S(2)}) copy-start(s32[1,1,1,128]{3,2,1,0:T(1,128)} %param.26) | copy-start | bytes 1540
  13.0 9.4 %collective-permute-start.2 = (bf16[1,2,4,16,640]{4,3,2,1,0:T(8,128)(2,1)S(1)}, bf16[1,2,4,16,640]{4,3,2,1,0:T(8,128)(2,1)S(1)}, u32[]{:S(2)}, u32[]{:S(2)}) collective-permute-start(bf16[1,2,4,16,640]{4,3,2,1,0:T(8,128)(2,1)S(1)} %get-tuple-element.43), channel_id=1, source_target_pairs={{0,16},{16,32},{32,48},{48,64},{64,80},{80,96},{96,112},{112,128},... | collective-permute-start | bytes 491528 | tf_op jit(solution)/shard_map/ppermute | solution.py:459
  15.0 7.4 %collective-permute-start.3 = (bf16[1,2,4,16,640]{4,3,2,1,0:T(8,128)(2,1)S(1)}, bf16[1,2,4,16,640]{4,3,2,1,0:T(8,128)(2,1)S(1)}, u32[]{:S(2)}, u32[]{:S(2)}) collective-permute-start(bf16[1,2,4,16,640]{4,3,2,1,0:T(8,128)(2,1)S(1)} %get-tuple-element.44), channel_id=1, source_target_pairs={{0,240},{16,0},{32,16},{48,32},{64,48},{80,64},{96,80},{112,96},{1... | collective-permute-start | bytes 491528 | tf_op jit(solution)/shard_map/ppermute | solution.py:460
  22.5 3.9 %collective-permute-start.4 = (bf16[4,2,4,16,640]{4,3,2,1,0:T(8,128)(2,1)S(1)}, bf16[4,2,4,16,640]{4,3,2,1,0:T(8,128)(2,1)S(1)}, u32[]{:S(2)}, u32[]{:S(2)}) collective-permute-start(bf16[4,2,4,16,640]{4,3,2,1,0:T(8,128)(2,1)S(1)} %pad_maximum_fusion), channel_id=1, source_target_pairs={{0,8},{8,0},{1,9},{9,1},{2,10},{10,2},{3,11},{11,3},{4,12},{12,4},... | collective-permute-start | bytes 1966088 | tf_op jit(solution)/shard_map/ppermute | solution.py:450
  26.5 29.9 %copy-start.11 = (bf16[256,256]{1,0:T(8,128)(2,1)S(1)}, bf16[256,256]{1,0:T(8,128)(2,1)}, u32[]{:S(2)}) copy-start(bf16[256,256]{1,0:T(8,128)(2,1)} %constant.28.clone.low) | copy-start | bytes 393220
  26.5 29.9 %copy-start.12 = (bf16[256,256]{1,0:T(8,128)(2,1)S(1)}, bf16[256,256]{1,0:T(8,128)(2,1)}, u32[]{:S(2)}) copy-start(bf16[256,256]{1,0:T(8,128)(2,1)} %constant.27.clone.high) | copy-start | bytes 393220
  26.5 30.8 %copy-start.13 = (bf16[128,128]{1,0:T(8,128)(2,1)S(1)}, bf16[128,128]{1,0:T(8,128)(2,1)}, u32[]{:S(2)}) copy-start(bf16[128,128]{1,0:T(8,128)(2,1)} %constant.29.clone.carry) | copy-start | bytes 98308
  31.6 7.7 %collective-permute-start.5 = (bf16[2,2,1,16,512]{4,3,2,1,0:T(8,128)(2,1)S(1)}, bf16[2,2,1,16,512]{4,3,2,1,0:T(8,128)(2,1)S(1)}, u32[]{:S(2)}, u32[]{:S(2)}) collective-permute-start(bf16[2,2,1,16,512]{4,3,2,1,0:T(8,128)(2,1)S(1)} %get-tuple-element.49), channel_id=1, source_target_pairs={{0,1},{1,2},{2,3},{3,4},{4,5},{5,6},{6,7},{7,0},{8,9},{9,10},{10,1... | collective-permute-start | bytes 196616 | tf_op jit(solution)/shard_map/ppermute | solution.py:456
  34.9 4.9 %collective-permute-start.6 = (bf16[2,2,1,16,512]{4,3,2,1,0:T(8,128)(2,1)S(1)}, bf16[2,2,1,16,512]{4,3,2,1,0:T(8,128)(2,1)S(1)}, u32[]{:S(2)}, u32[]{:S(2)}) collective-permute-start(bf16[2,2,1,16,512]{4,3,2,1,0:T(8,128)(2,1)S(1)} %get-tuple-element.50), channel_id=1, source_target_pairs={{0,7},{1,0},{2,1},{3,2},{4,3},{5,4},{6,5},{7,6},{8,15},{9,8},{10,9... | collective-permute-start | bytes 196616 | tf_op jit(solution)/shard_map/ppermute | solution.py:457
  39.9 6.0 %collective-permute-start.7 = (bf16[1,2,4,16,512]{4,3,2,1,0:T(8,128)(2,1)S(1)}, bf16[1,2,4,16,512]{4,3,2,1,0:T(8,128)(2,1)S(1)}, u32[]{:S(2)}, u32[]{:S(2)}) collective-permute-start(bf16[1,2,4,16,512]{4,3,2,1,0:T(8,128)(2,1)S(1)} %get-tuple-element.45), channel_id=1, source_target_pairs={{0,16},{16,32},{32,48},{48,64},{64,80},{80,96},{96,112},{112,128},... | collective-permute-start | bytes 393224 | tf_op jit(solution)/shard_map/ppermute | solution.py:459
  40.0 5.9 %collective-permute-start.8 = (bf16[1,2,4,16,512]{4,3,2,1,0:T(8,128)(2,1)S(1)}, bf16[1,2,4,16,512]{4,3,2,1,0:T(8,128)(2,1)S(1)}, u32[]{:S(2)}, u32[]{:S(2)}) collective-permute-start(bf16[1,2,4,16,512]{4,3,2,1,0:T(8,128)(2,1)S(1)} %get-tuple-element.46), channel_id=1, source_target_pairs={{0,240},{16,0},{32,16},{48,32},{64,48},{80,64},{96,80},{112,96},{1... | collective-permute-start | bytes 393224 | tf_op jit(solution)/shard_map/ppermute | solution.py:460
  46.0 4.3 %collective-permute-start.9 = (bf16[4,2,4,16,512]{4,3,2,1,0:T(8,128)(2,1)S(1)}, bf16[4,2,4,16,512]{4,3,2,1,0:T(8,128)(2,1)S(1)}, u32[]{:S(2)}, u32[]{:S(2)}) collective-permute-start(bf16[4,2,4,16,512]{4,3,2,1,0:T(8,128)(2,1)S(1)} %pad_maximum_fusion.1), channel_id=1, source_target_pairs={{0,8},{8,0},{1,9},{9,1},{2,10},{10,2},{3,11},{11,3},{4,12},{12,4},... | collective-permute-start | bytes 1572872 | tf_op jit(solution)/shard_map/ppermute | solution.py:450
  48.7 7.6 %collective-permute-start.10 = (f32[8,128]{1,0:T(8,128)S(1)}, f32[8,128]{1,0:T(8,128)S(1)}, u32[]{:S(2)}, u32[]{:S(2)}) collective-permute-start(f32[8,128]{1,0:T(8,128)S(1)} %get-tuple-element.27.own), channel_id=1, source_target_pairs={{0,8},{8,0},{1,9},{9,1},{2,10},{10,2},{3,11},{11,3},{4,12},{12,4},... | collective-permute-start | bytes 12296 | tf_op jit(solution)/shard_map/ppermute | solution.py:450
  50.2 33.9 %copy-start = (bf16[1024,256]{1,0:T(8,128)(2,1)S(1)}, bf16[1024,256]{1,0:T(8,128)(2,1)}, u32[]{:S(2)}) copy-start(bf16[1024,256]{1,0:T(8,128)(2,1)} %constant.32.clone.zl) | copy-start | bytes 1572868
  50.2 33.9 %copy-start.1 = (bf16[1024,256]{1,0:T(8,128)(2,1)S(1)}, bf16[1024,256]{1,0:T(8,128)(2,1)}, u32[]{:S(2)}) copy-start(bf16[1024,256]{1,0:T(8,128)(2,1)} %constant.31.clone.zh) | copy-start | bytes 1572868
  50.2 33.9 %copy-start.6 = (bf16[3,128,256]{2,1,0:T(8,128)(2,1)S(1)}, bf16[3,128,256]{2,1,0:T(8,128)(2,1)}, u32[]{:S(2)}) copy-start(bf16[3,128,256]{2,1,0:T(8,128)(2,1)} %constant.36.clone.tl) | copy-start | bytes 589828
  50.3 33.8 %copy-start.7 = (bf16[3,128,256]{2,1,0:T(8,128)(2,1)S(1)}, bf16[3,128,256]{2,1,0:T(8,128)(2,1)}, u32[]{:S(2)}) copy-start(bf16[3,128,256]{2,1,0:T(8,128)(2,1)} %constant.35.clone.th) | copy-start | bytes 589828
  50.3 33.8 %copy-start.8 = (bf16[3,256,128]{2,1,0:T(8,128)(2,1)S(1)}, bf16[3,256,128]{2,1,0:T(8,128)(2,1)}, u32[]{:S(2)}) copy-start(bf16[3,256,128]{2,1,0:T(8,128)(2,1)} %constant.34.clone.xl) | copy-start | bytes 589828
  50.3 33.8 %copy-start.9 = (bf16[3,256,128]{2,1,0:T(8,128)(2,1)S(1)}, bf16[3,256,128]{2,1,0:T(8,128)(2,1)}, u32[]{:S(2)}) copy-start(bf16[3,256,128]{2,1,0:T(8,128)(2,1)} %constant.33.clone.xh) | copy-start | bytes 589828
  50.3 33.8 %copy-start.10 = (f32[256,2]{1,0:T(8,128)S(1)}, f32[256,2]{1,0:T(8,128)}, u32[]{:S(2)}) copy-start(f32[256,2]{1,0:T(8,128)} %constant.37.clone.col) | copy-start | bytes 6148
  50.3 33.8 %copy-start.17 = (f32[8,256]{1,0:T(8,128)S(1)}, f32[8,256]{1,0:T(8,128)}, u32[]{:S(2)}) copy-start(f32[8,256]{1,0:T(8,128)} %constant.38.clone.row) | copy-start | bytes 24580
  50.3 33.8 %copy-start.23 = (f32[256]{0:T(256)S(1)}, f32[256]{0:T(256)}, u32[]{:S(2)}) copy-start(f32[256]{0:T(256)} %constant.30.clone.scale_y) | copy-start | bytes 3076
  55.9 1.3 %collective-permute-start.11 = (f32[1,128]{1,0:T(1,128)S(1)}, f32[1,128]{1,0:T(1,128)S(1)}, u32[]{:S(2)}, u32[]{:S(2)}) collective-permute-start(f32[1,128]{1,0:T(1,128)S(1)} %get-tuple-element.31.own.charge), channel_id=1, source_target_pairs={{0,8},{8,0},{1,9},{9,1},{2,10},{10,2},{3,11},{11,3},{4,12},{12,4},... | collective-permute-start | bytes 1544 | tf_op jit(solution)/shard_map/ppermute | solution.py:450
  114.6 3.6 %collective-permute-start.12 = (f32[8,128]{1,0:T(8,128)S(1)}, f32[8,128]{1,0:T(8,128)S(1)}, u32[]{:S(2)}, u32[]{:S(2)}) collective-permute-start(f32[8,128]{1,0:T(8,128)S(1)} %get-tuple-element.33), channel_id=1, source_target_pairs={{0,8},{8,0},{1,9},{9,1},{2,10},{10,2},{3,11},{11,3},{4,12},{12,4},... | collective-permute-start | bytes 12296 | tf_op jit(solution)/shard_map/ppermute | solution.py:450

commit v3 on v2

--- a/solution.py
+++ b/solution.py
@@ -78,6 +78,15 @@
             carry[row, ZPAD * third + 35 + left] = 1.0 - share
             carry[row, ZPAD * third + 36 + left] = share
     out["carry"] = carry.astype(BF16)
+    line = np.zeros((128, 128), np.float32)
+    move = np.zeros((128, 128), np.float32)
+    for third in range(3):
+        base = ZPAD * third
+        for point in range(35):
+            line[base + 35, base + point] = 1.0 - (point - 1) / 32.0
+            line[base + 39, base + point] = (point - 1) / 32.0
+        move[base + 35, base + 36] = move[base + 39, base + 38] = 1.0
+    out["lines"] = np.stack([-line, move - line]).astype(BF16)
     out["basis_z"] = np_halves(zed.reshape(1024, MESH))
     exx = np.zeros((3, MESH, 16, 8))
     for third in range(3):
@@ -119,7 +128,17 @@
     )
 
 
-def prep_kernel(feats, fraction, cells, octants, out, geometry_out):
+def prep_kernel(*refs):
+    sources, (out, geometry_out), local, signals = refs[:4], refs[4:6], refs[6:10], refs[10]
+    copies = [
+        pltpu.make_async_copy(source, target, signals.at[i])
+        for i, (source, target) in enumerate(zip(sources, local))
+    ]
+    for copy in copies:
+        copy.start()
+    for copy in copies:
+        copy.wait()
+    feats, fraction, cells, octants = local
     chosen = select_rows(octants)
     out[:, :512] = dot(chosen, feats[...]).astype(BF16)
     geometry = geometry_rows(cells, fraction)
@@ -341,6 +360,16 @@
     along_z = spread(weights_z, spots_z, ZPAD)
     down_x = spread(slopes_x, spots_x, 24)
     down_z = spread(slopes_z, spots_z, ZPAD)
+    point = lax.broadcasted_iota(jnp.int32, (ZPAD, 256), 0)
+    share = (point - 1).astype(F32) / 32.0
+
+    def with_line(az):
+        first = jnp.sum((1.0 - share) * az, axis=0, keepdims=True)
+        last = jnp.sum(share * az, axis=0, keepdims=True)
+        spare = jnp.where(point < 37, first, jnp.where(point == 37, 0.0, last))
+        return jnp.where(point < 35, az, spare)
+
+    along_z, down_z = with_line(along_z), with_line(down_z)
     for kind, (ax, az) in enumerate(
         ((along_x, along_z), (down_x, along_z), (along_x, down_z))
     ):
@@ -353,9 +382,10 @@
 def charges_kernel(own, other, weight_y, planes, carry, out, lines):
     charge = jnp.concatenate([own[...], other[...]], axis=1)
     charged = halves(weight_y[...] * charge)
+    used = lax.broadcasted_iota(jnp.int32, (1, 128), 1) % ZPAD < 35
     for group in range(7):
         rows = slice(128 * group, 128 * group + 128)
-        line = dot3(charged, (planes[0, rows, :], planes[1, rows, :]), NT)
+        line = jnp.where(used, dot3(charged, (planes[0, rows, :], planes[1, rows, :]), NT), 0.0)
         kept = line.astype(BF16).astype(F32)
         lines[:, group, :] = kept + dot((line - kept).astype(BF16), carry[...])
     lines[:, 7, :] = jnp.zeros((128, 128), F32)
@@ -363,7 +393,7 @@
 
 
 def waves_kernel(
-    scale_y, received, zh, zl, xh, xl, th, tl, col, row, out, coming, lhs,
+    scale_y, received, zh, zl, xh, xl, th, tl, col, row, lines, out, coming, lhs,
 ):
     for part in range(8):
         lanes = slice(part * 128, part * 128 + 128)
@@ -372,11 +402,11 @@
             moved = block if third == 0 else pltpu.roll(block, 128 - ZPAD * third, 1)
             coming[third * 128 : third * 128 + 128, lanes] = moved.astype(BF16)
     zed = (zh[...], zl[...])
-    lines = dot(coming[...], zed[0]) + dot(coming[...], zed[1])
+    rows = dot(coming[...], zed[0]) + dot(coming[...], zed[1])
     total = jnp.zeros((MESH, MESH), F32)
     for third in range(3):
         total += dot3(
-            (xh[third], xl[third]), halves(lines[third * 128 : third * 128 + 128, :])
+            (xh[third], xl[third]), halves(rows[third * 128 : third * 128 + 128, :])
         )
     number = lax.axis_index("gy") * 128 + lax.axis_index("gz") * 16 + lax.axis_index("gx")
     wave = jnp.where(number <= 128, number, number - 128)
@@ -390,19 +420,24 @@
         lhs[third * 128 : third * 128 + 128, :] = dot3(
             halves(dot3((th[third], tl[third]), scaled)), zed, NT
         )
+    spot = lax.broadcasted_iota(jnp.int32, (1, 128), 1) % ZPAD
+    spare = (spot >= 36) & (spot <= 38)
     for part in range(8):
         lanes = slice(part * 128, part * 128 + 128)
         block = lhs[0:128, lanes]
         for third in range(1, 3):
             block += pltpu.roll(lhs[third * 128 : third * 128 + 128, lanes], ZPAD * third, 1)
-        out[part] = block
+        high, low = halves(block)
+        left = jnp.where(spare, 0.0, block)
+        out[part] = (left + dot(high, lines[0]) + dot(low, lines[1])).astype(BF16)
 
 
 def forces_kernel(weight_y, slope_y, planes, returned, out_own, out_other):
-    flat = halves(jnp.concatenate([returned[:, group, :] for group in range(7)], axis=1))
+    values = returned[...].astype(F32)
+    flat = jnp.concatenate([values[:, group, :] for group in range(7)], axis=1).astype(BF16)
 
     def level(kind):
-        return dot3(flat, (planes[2 * kind], planes[2 * kind + 1]))
+        return dot(flat, planes[2 * kind]) + dot(flat, planes[2 * kind + 1])
 
     level_0 = level(0)
     along_y = weight_y[...]
@@ -479,9 +514,22 @@
     links = neighbours[0, 0, 0]
     heads = jnp.pad(jnp.transpose(readout), ((0, 6), (0, 0)))
 
-    outgoing, places = call(
-        prep_kernel, [((128, 640), BF16), ((8, 128), F32)], feats, part, cells, octants
-    )
+    outgoing, places = pl.pallas_call(
+        prep_kernel,
+        out_shape=[
+            jax.ShapeDtypeStruct((128, 640), BF16), jax.ShapeDtypeStruct((8, 128), F32)
+        ],
+        in_specs=[pl.BlockSpec(memory_space=pltpu.MemorySpace.HBM)] * 4,
+        out_specs=[VMEM] * 2,
+        scratch_shapes=[
+            pltpu.VMEM((128, 512), BF16),
+            pltpu.VMEM((3, 128), BF16),
+            pltpu.VMEM((1, 384), jnp.int32),
+            pltpu.VMEM((8, 14), jnp.int32),
+            pltpu.SemaphoreType.DMA((4,)),
+        ],
+        compiler_params=pltpu.CompilerParams(vmem_limit_bytes=8 << 20),
+    )(feats, part, cells, octants)
     near, far = ghosts(outgoing)
     weight_y, slope_y, planes = call(
         static_kernel,
@@ -530,9 +578,9 @@
     received = across(lines).reshape(8, 128, 128)
     (waves,) = call(
         waves_kernel,
-        [((8, 128, 128), F32)],
+        [((8, 128, 128), BF16)],
         table["scale_y"], received, *table["basis_z"], *table["basis_x"], *table["basis_xt"],
-        table["col"], table["row"],
+        table["col"], table["row"], table["lines"],
         scalars=(0,),
         scratch=[((384, 1024), BF16), ((384, 1024), F32)],
     )

time: 119 us -> 114 us (0.958)
  blocking collectives: 50.2 us -> 44.5 us
    all_to_all x2, blocking collectives: 50.2 us -> 44.5 us  [across(): lax.all_to_all(blocks, ('gz', 'gx'), split_axis=0, concat_axis=0, tiled=T...]
    pallas_call x8 -> x7, Pallas kernels: 19.6 us -> 19.1 us  [call(): pl.pallas_call(kernel, out_shape=[jax.ShapeDtypeStruct(s, d) for s, d in...]
    unnamed x54 -> x56, local copies, waits for them, and re-layouts: 3.11 us -> 3.12 us
where the time goes in v3:
time: 114 us; the launch traced here: 113 us
  blocking collectives  44.5 us (39%)
  starting transfers between devices  30.4 us (27%)
  Pallas kernels  19.7 us (17%)
  waiting for transfers between devices  14.2 us (12%)
  local copies, waits for them, and re-layouts  3.2 us (3%)
    all_to_all x2, blocking collectives, across(): lax.all_to_all(blocks, ('gz', 'gx'), split_axis=0, concat_axis=0, tiled=T...  44.5 us
    pallas_call x7, Pallas kernels, call(): pl.pallas_call(kernel, out_shape=[jax.ShapeDtypeStruct(s, d) for s, d in...  19.1 us
    ppermute x5, starting transfers between devices, partner(): return lax.ppermute(block, 'gy', [(0, 1), (1, 0)])  8.45 us
    ppermute x2, starting transfers between devices, ghosts(): after = lax.ppermute(x[:1], 'gx', ring('gx', -1))  8 us
    ppermute x2, starting transfers between devices, ghosts(): before = lax.ppermute(x[:, :, 1:], 'gz', ring('gz', 1))  6.93 us
    ppermute x2, waiting for transfers between devices, ghosts(): before = lax.ppermute(x[1:], 'gx', ring('gx', 1))  5.31 us
    ppermute x2, starting transfers between devices, ghosts(): after = lax.ppermute(x[:, :, :1], 'gz', ring('gz', -1))  4.94 us
    ppermute x5, waiting for transfers between devices, partner(): return lax.ppermute(block, 'gy', [(0, 1), (1, 0)])  3.8 us
  transfers between devices with their start and end apart: 13, of which 9 were waited for; matrix products, arithmetic and copies ran while one was open for 0% of the time, Pallas kernels for 6%

profile of v3, /device:TPU:1, one launch (start us, length us, event | category | flops | bytes accessed | tf_op | source)
XLA Modules:
  0.0 113.3 jit_solution(18206457965413760264)
XLA Ops:
  0.7 0.9 copy-done.2
  1.6 0.7 copy-done.15
  2.3 0.7 copy-done.19
  3.0 0.7 copy-done.22
  3.7 0.6 shard_map.247
  4.3 3.6 %collective-permute-start = (bf16[2,2,1,16,640]{4,3,2,1,0:T(8,128)(2,1)S(1)}, bf16[2,2,1,16,640]{4,3,2,1,0:T(8,128)(2,1)S(1)}, u32[]{:S(2)}, u32[]{:S(2)}) collective-permute-start(bf16[2,2,1,16,640]{4,3,2,1,0:T(8,128)(2,1)S(1)} %get-tuple-element.47), channel_id=1, source_target_pairs={{0,1},{1,2},{2,3},{3,4},{4,5},{5,6},{6,7},{7,0},{8,9},{9,10},{10,1... | collective-permute-start | bytes 245768 | tf_op jit(solution)/shard_map/ppermute | solution.py:491
  8.0 2.5 %collective-permute-start.1 = (bf16[2,2,1,16,640]{4,3,2,1,0:T(8,128)(2,1)S(1)}, bf16[2,2,1,16,640]{4,3,2,1,0:T(8,128)(2,1)S(1)}, u32[]{:S(2)}, u32[]{:S(2)}) collective-permute-start(bf16[2,2,1,16,640]{4,3,2,1,0:T(8,128)(2,1)S(1)} %get-tuple-element.48), channel_id=1, source_target_pairs={{0,7},{1,0},{2,1},{3,2},{4,3},{5,4},{6,5},{7,6},{8,15},{9,8},{10,9... | collective-permute-start | bytes 245768 | tf_op jit(solution)/shard_map/ppermute | solution.py:492
  10.5 1.7 %collective-permute-done = bf16[2,2,1,16,640]{4,3,2,1,0:T(8,128)(2,1)S(1)} collective-permute-done((bf16[2,2,1,16,640]{4,3,2,1,0:T(8,128)(2,1)S(1)}, bf16[2,2,1,16,640]{4,3,2,1,0:T(8,128)(2,1)S(1)}, u32[]{:S(2)}, u32[]{:S(2)}) %collective-permute-start) | collective-permute-done | bytes 81952 | tf_op jit(solution)/shard_map/ppermute | solution.py:491
  12.3 0.8 collective-permute-done.1
  13.2 2.0 %collective-permute-start.2 = (bf16[1,2,4,16,640]{4,3,2,1,0:T(8,128)(2,1)S(1)}, bf16[1,2,4,16,640]{4,3,2,1,0:T(8,128)(2,1)S(1)}, u32[]{:S(2)}, u32[]{:S(2)}) collective-permute-start(bf16[1,2,4,16,640]{4,3,2,1,0:T(8,128)(2,1)S(1)} %get-tuple-element.43), channel_id=1, source_target_pairs={{0,16},{16,32},{32,48},{48,64},{64,80},{80,96},{96,112},{112,128},... | collective-permute-start | bytes 491528 | tf_op jit(solution)/shard_map/ppermute | solution.py:494
  15.2 4.4 %collective-permute-start.3 = (bf16[1,2,4,16,640]{4,3,2,1,0:T(8,128)(2,1)S(1)}, bf16[1,2,4,16,640]{4,3,2,1,0:T(8,128)(2,1)S(1)}, u32[]{:S(2)}, u32[]{:S(2)}) collective-permute-start(bf16[1,2,4,16,640]{4,3,2,1,0:T(8,128)(2,1)S(1)} %get-tuple-element.44), channel_id=1, source_target_pairs={{0,240},{16,0},{32,16},{48,32},{64,48},{80,64},{96,80},{112,96},{1... | collective-permute-start | bytes 491528 | tf_op jit(solution)/shard_map/ppermute | solution.py:495
  19.6 3.0 %collective-permute-done.2 = bf16[1,2,4,16,640]{4,3,2,1,0:T(8,128)(2,1)S(1)} collective-permute-done((bf16[1,2,4,16,640]{4,3,2,1,0:T(8,128)(2,1)S(1)}, bf16[1,2,4,16,640]{4,3,2,1,0:T(8,128)(2,1)S(1)}, u32[]{:S(2)}, u32[]{:S(2)}) %collective-permute-start.2) | collective-permute-done | bytes 163872 | tf_op jit(solution)/shard_map/ppermute | solution.py:494
  22.6 0.1 pad_maximum_fusion
  22.7 2.2 %collective-permute-start.4 = (bf16[4,2,4,16,640]{4,3,2,1,0:T(8,128)(2,1)S(1)}, bf16[4,2,4,16,640]{4,3,2,1,0:T(8,128)(2,1)S(1)}, u32[]{:S(2)}, u32[]{:S(2)}) collective-permute-start(bf16[4,2,4,16,640]{4,3,2,1,0:T(8,128)(2,1)S(1)} %pad_maximum_fusion), channel_id=1, source_target_pairs={{0,8},{8,0},{1,9},{9,1},{2,10},{10,2},{3,11},{11,3},{4,12},{12,4},... | collective-permute-start | bytes 1966088 | tf_op jit(solution)/shard_map/ppermute | solution.py:485
  24.9 1.7 %collective-permute-done.4 = bf16[4,2,4,16,640]{4,3,2,1,0:T(8,128)(2,1)S(1)} collective-permute-done((bf16[4,2,4,16,640]{4,3,2,1,0:T(8,128)(2,1)S(1)}, bf16[4,2,4,16,640]{4,3,2,1,0:T(8,128)(2,1)S(1)}, u32[]{:S(2)}, u32[]{:S(2)}) %collective-permute-start.4) | collective-permute-done | bytes 655392 | tf_op jit(solution)/shard_map/ppermute | solution.py:485
  26.7 0.0 copy-start.11
  26.7 0.0 copy-start.12
  26.7 0.0 copy-start.14
  26.7 5.0 %shard_map.248 = (bf16[128,512]{1,0:T(8,128)(2,1)S(1)}, bf16[128,512]{1,0:T(8,128)(2,1)S(1)}, f32[48,128]{1,0:T(8,128)S(1)}, bf16[64,2048]{1,0:T(8,128)(2,1)S(1)}, s32[16,128]{1,0:T(8,128)S(1)}) custom-call(bf16[128,512]{1,0:T(8,128)(2,1)S(1)} %bitcast.30, bf16[512,640]{1,0:T(8,128)(2,1)S(1)} %bitcast.18, bf16[512,640]{1,0:T(8,128)(2,1)S(1)} %bitcast.28, ...), custom_call_target="tpu_custom_call" | custom-call | tf_op jit(solution)/shard_map/pallas_call | solution.py:469
  31.8 3.3 %collective-permute-start.5 = (bf16[2,2,1,16,512]{4,3,2,1,0:T(8,128)(2,1)S(1)}, bf16[2,2,1,16,512]{4,3,2,1,0:T(8,128)(2,1)S(1)}, u32[]{:S(2)}, u32[]{:S(2)}) collective-permute-start(bf16[2,2,1,16,512]{4,3,2,1,0:T(8,128)(2,1)S(1)} %get-tuple-element.49), channel_id=1, source_target_pairs={{0,1},{1,2},{2,3},{3,4},{4,5},{5,6},{6,7},{7,0},{8,9},{9,10},{10,1... | collective-permute-start | bytes 196616 | tf_op jit(solution)/shard_map/ppermute | solution.py:491
  35.1 2.4 %collective-permute-start.6 = (bf16[2,2,1,16,512]{4,3,2,1,0:T(8,128)(2,1)S(1)}, bf16[2,2,1,16,512]{4,3,2,1,0:T(8,128)(2,1)S(1)}, u32[]{:S(2)}, u32[]{:S(2)}) collective-permute-start(bf16[2,2,1,16,512]{4,3,2,1,0:T(8,128)(2,1)S(1)} %get-tuple-element.50), channel_id=1, source_target_pairs={{0,7},{1,0},{2,1},{3,2},{4,3},{5,4},{6,5},{7,6},{8,15},{9,8},{10,9... | collective-permute-start | bytes 196616 | tf_op jit(solution)/shard_map/ppermute | solution.py:492
  37.5 2.0 %collective-permute-done.5 = bf16[2,2,1,16,512]{4,3,2,1,0:T(8,128)(2,1)S(1)} collective-permute-done((bf16[2,2,1,16,512]{4,3,2,1,0:T(8,128)(2,1)S(1)}, bf16[2,2,1,16,512]{4,3,2,1,0:T(8,128)(2,1)S(1)}, u32[]{:S(2)}, u32[]{:S(2)}) %collective-permute-start.5) | collective-permute-done | bytes 65568 | tf_op jit(solution)/shard_map/ppermute | solution.py:491
  39.5 0.5 collective-permute-done.6
  40.0 0.1 collective-permute-start.7
  40.1 3.6 %collective-permute-start.8 = (bf16[1,2,4,16,512]{4,3,2,1,0:T(8,128)(2,1)S(1)}, bf16[1,2,4,16,512]{4,3,2,1,0:T(8,128)(2,1)S(1)}, u32[]{:S(2)}, u32[]{:S(2)}) collective-permute-start(bf16[1,2,4,16,512]{4,3,2,1,0:T(8,128)(2,1)S(1)} %get-tuple-element.46), channel_id=1, source_target_pairs={{0,240},{16,0},{32,16},{48,32},{64,48},{80,64},{96,80},{112,96},{1... | collective-permute-start | bytes 393224 | tf_op jit(solution)/shard_map/ppermute | solution.py:495
  43.7 2.4 %collective-permute-done.7 = bf16[1,2,4,16,512]{4,3,2,1,0:T(8,128)(2,1)S(1)} collective-permute-done((bf16[1,2,4,16,512]{4,3,2,1,0:T(8,128)(2,1)S(1)}, bf16[1,2,4,16,512]{4,3,2,1,0:T(8,128)(2,1)S(1)}, u32[]{:S(2)}, u32[]{:S(2)}) %collective-permute-start.7) | collective-permute-done | bytes 131104 | tf_op jit(solution)/shard_map/ppermute | solution.py:494
  46.0 0.1 pad_maximum_fusion.1
  46.1 2.8 %collective-permute-start.9 = (bf16[4,2,4,16,512]{4,3,2,1,0:T(8,128)(2,1)S(1)}, bf16[4,2,4,16,512]{4,3,2,1,0:T(8,128)(2,1)S(1)}, u32[]{:S(2)}, u32[]{:S(2)}) collective-permute-start(bf16[4,2,4,16,512]{4,3,2,1,0:T(8,128)(2,1)S(1)} %pad_maximum_fusion.1), channel_id=1, source_target_pairs={{0,8},{8,0},{1,9},{9,1},{2,10},{10,2},{3,11},{11,3},{4,12},{12,4},... | collective-permute-start | bytes 1572872 | tf_op jit(solution)/shard_map/ppermute | solution.py:485
  48.9 0.3 collective-permute-start.10
  49.2 1.2 %collective-permute-done.9 = bf16[4,2,4,16,512]{4,3,2,1,0:T(8,128)(2,1)S(1)} collective-permute-done((bf16[4,2,4,16,512]{4,3,2,1,0:T(8,128)(2,1)S(1)}, bf16[4,2,4,16,512]{4,3,2,1,0:T(8,128)(2,1)S(1)}, u32[]{:S(2)}, u32[]{:S(2)}) %collective-permute-start.9) | collective-permute-done | bytes 524320 | tf_op jit(solution)/shard_map/ppermute | solution.py:485
  50.4 0.0 copy-start.6
  50.4 0.0 copy-start.7
  50.5 0.0 copy-start.8
  50.5 0.0 copy-start.10
  50.5 0.0 copy-start.13
  50.5 0.0 copy-start.18
  50.5 0.0 copy-start.24
  50.5 5.5 %shard_map.249 = (bf16[128,512]{1,0:T(8,128)(2,1)}, f32[1,128]{1,0:T(1,128)S(1)}, f32[1,128]{1,0:T(1,128)S(1)}) custom-call(bf16[128,512]{1,0:T(8,128)(2,1)S(1)} %get-tuple-element.21.feats, bf16[512,512]{1,0:T(8,128)(2,1)S(1)} %bitcast.19, bf16[512,512]{1,0:T(8,128)(2,1)S(1)} %bitcast.31, s32[16,128]{1,0:T(8,128)S(1)} %get-tuple-element.23.rows, ...), custom_call_target="tpu_custom_call" | custom-call | tf_op jit(solution)/shard_map/pallas_call | solution.py:469
  56.1 0.4 collective-permute-start.11
  56.5 0.9 shard_map.250
  57.4 1.4 %shard_map.251 = bf16[128,8,128]{2,1,0:T(8,128)(2,1)S(1)} custom-call(f32[1,128]{1,0:T(1,128)S(1)} %get-tuple-element.31.own.charge, f32[1,128]{1,0:T(1,128)S(1)} %collective-permute-done.11.other, f32[128,256]{1,0:T(8,128)S(1)} %get-tuple-element.28.weight_y, bf16[6,896,256]{2,1,0:T(8,128)(2,1)S(1)} %get-tuple-element.30.planes, bf16[128,128]{1,0:T(8,128)(2,1)S(1)} %copy-done.14), custom_call_target="tpu_custom_call" | custom-call | tf_op jit(solution)/shard_map/pallas_call | solution.py:469
  58.8 25.4 %all_to_all.10 = bf16[128,8,128]{2,1,0:T(8,128)(2,1)S(1)} all-to-all(bf16[128,8,128]{2,1,0:T(8,128)(2,1)S(1)} %shard_map.251), channel_id=1, replica_groups=mesh['gx'=16,'gy'=2,'gz'=8] {'gz','gx'}, dimensions={0} | all-to-all | bytes 524288 | tf_op jit(solution)/shard_map/all_to_all | solution.py:501
  84.3 4.9 %shard_map.252 = bf16[8,128,128]{2,1,0:T(8,128)(2,1)S(1)} custom-call(f32[256]{0:T(256)S(1)} %copy-done.24, bf16[8,128,128]{2,1,0:T(8,128)(2,1)S(1)} %bitcast.26, bf16[1024,256]{1,0:T(8,128)(2,1)S(1)} %copy-done.5, bf16[1024,256]{1,0:T(8,128)(2,1)S(1)} %copy-done.4, bf16[3,256,128]{2,1,0:T(8,128)(2,1)S(1)} %copy-done.9, bf16[3,256,128]{2,1,0:T(8,128)(2,1)S(1)} %copy-done.8, ...), custom_call_target="tpu_custom_call" | custom-call | tf_op jit(solution)/shard_map/pallas_call | solution.py:469
  89.2 19.1 %all_to_all.11.returned = bf16[128,8,128]{2,1,0:T(8,128)(2,1)S(1)} all-to-all(bf16[128,8,128]{2,1,0:T(8,128)(2,1)S(1)} %bitcast.27), channel_id=1, replica_groups=mesh['gx'=16,'gy'=2,'gz'=8] {'gz','gx'}, dimensions={0} | all-to-all | bytes 524288 | tf_op jit(solution)/shard_map/all_to_all | solution.py:501
  108.3 0.7 shard_map.253
  109.1 2.8 %collective-permute-start.12 = (f32[8,128]{1,0:T(8,128)S(1)}, f32[8,128]{1,0:T(8,128)S(1)}, u32[]{:S(2)}, u32[]{:S(2)}) collective-permute-start(f32[8,128]{1,0:T(8,128)S(1)} %get-tuple-element.33), channel_id=1, source_target_pairs={{0,8},{8,0},{1,9},{9,1},{2,10},{10,2},{3,11},{11,3},{4,12},{12,4},... | collective-permute-start | bytes 12296 | tf_op jit(solution)/shard_map/ppermute | solution.py:485
  111.9 0.8 collective-permute-done.12.there
  112.7 0.6 shard_map.254
  (53 shorter events, 0.3 us)
Async XLA Ops:
  0.6 26.0 %copy-start.1 = (bf16[2,2,128,128]{3,2,1,0:T(8,128)(2,1)S(1)}, bf16[2,2,128,128]{3,2,1,0:T(8,128)(2,1)}, u32[]{:S(2)}) copy-start(bf16[2,2,128,128]{3,2,1,0:T(8,128)(2,1)} %mix_weight.3) | copy-start | bytes 393220
  0.6 26.0 %copy-start = (bf16[2,64,512]{2,1,0:T(8,128)(2,1)S(1)}, bf16[2,64,512]{2,1,0:T(8,128)(2,1)}, u32[]{:S(2)}) copy-start(bf16[2,64,512]{2,1,0:T(8,128)(2,1)} %radial_out.3) | copy-start | bytes 393220
  0.7 0.9 copy-start.2
  1.6 0.7 copy-start.15
  2.3 0.7 copy-start.19
  3.0 0.7 copy-start.22
  3.6 23.0 %copy-start.3 = (bf16[1,1,1,128,512]{4,3,2,1,0:T(8,128)(2,1)S(1)}, bf16[1,1,1,128,512]{4,3,2,1,0:T(8,128)(2,1)}, u32[]{:S(2)}) copy-start(bf16[1,1,1,128,512]{4,3,2,1,0:T(8,128)(2,1)} %param.24) | copy-start | bytes 393220
  3.6 23.0 %copy-start.16 = (s32[1,1,1,8,14]{4,3,2,1,0:T(8,128)S(1)}, s32[1,1,1,8,14]{4,3,2,1,0:T(8,128)}, u32[]{:S(2)}) copy-start(s32[1,1,1,8,14]{4,3,2,1,0:T(8,128)} %param.28) | copy-start | bytes 1348
  3.7 23.0 %copy-start.17 = (s32[1,1,1,16,128]{4,3,2,1,0:T(8,128)S(1)}, s32[1,1,1,16,128]{4,3,2,1,0:T(8,128)}, u32[]{:S(2)}) copy-start(s32[1,1,1,16,128]{4,3,2,1,0:T(8,128)} %param.29) | copy-start | bytes 24580
  3.7 23.0 %copy-start.20 = (s32[1,1,1,3,128]{4,2,3,1,0:T(1,128)S(1)}, s32[1,1,1,3,128]{4,2,3,1,0:T(1,128)}, u32[]{:S(2)}) copy-start(s32[1,1,1,3,128]{4,2,3,1,0:T(1,128)} %param.26) | copy-start | bytes 4612
  3.7 23.0 %copy-start.21 = (bf16[2,8,64]{2,1,0:T(8,128)(2,1)S(1)}, bf16[2,8,64]{2,1,0:T(8,128)(2,1)}, u32[]{:S(2)}) copy-start(bf16[2,8,64]{2,1,0:T(8,128)(2,1)} %radial_in.1) | copy-start | bytes 6148
  3.7 23.0 %copy-start.23 = (bf16[1,1,1,3,128]{4,3,2,1,0:T(4,128)(2,1)S(1)}, bf16[1,1,1,3,128]{4,3,2,1,0:T(4,128)(2,1)}, u32[]{:S(2)}) copy-start(bf16[1,1,1,3,128]{4,3,2,1,0:T(4,128)(2,1)} %param.25) | copy-start | bytes 2308
  4.3 7.9 %collective-permute-start = (bf16[2,2,1,16,640]{4,3,2,1,0:T(8,128)(2,1)S(1)}, bf16[2,2,1,16,640]{4,3,2,1,0:T(8,128)(2,1)S(1)}, u32[]{:S(2)}, u32[]{:S(2)}) collective-permute-start(bf16[2,2,1,16,640]{4,3,2,1,0:T(8,128)(2,1)S(1)} %get-tuple-element.47), channel_id=1, source_target_pairs={{0,1},{1,2},{2,3},{3,4},{4,5},{5,6},{6,7},{7,0},{8,9},{9,10},{10,1... | collective-permute-start | bytes 245768 | tf_op jit(solution)/shard_map/ppermute | solution.py:491
  8.0 5.1 %collective-permute-start.1 = (bf16[2,2,1,16,640]{4,3,2,1,0:T(8,128)(2,1)S(1)}, bf16[2,2,1,16,640]{4,3,2,1,0:T(8,128)(2,1)S(1)}, u32[]{:S(2)}, u32[]{:S(2)}) collective-permute-start(bf16[2,2,1,16,640]{4,3,2,1,0:T(8,128)(2,1)S(1)} %get-tuple-element.48), channel_id=1, source_target_pairs={{0,7},{1,0},{2,1},{3,2},{4,3},{5,4},{6,5},{7,6},{8,15},{9,8},{10,9... | collective-permute-start | bytes 245768 | tf_op jit(solution)/shard_map/ppermute | solution.py:492
  13.1 36.0 %copy-start.27 = (bf16[128,2]{0,1:T(2,128)(2,1)S(1)}, bf16[128,2]{0,1:T(2,128)(2,1)}, u32[]{:S(2)}) copy-start(bf16[128,2]{0,1:T(2,128)(2,1)} %param.33) | copy-start | bytes 1540
  13.2 37.3 %copy-start.25 = (f32[2,2]{1,0:T(2,128)S(1)}, f32[2,2]{1,0:T(2,128)}, u32[]{:S(2)}) copy-start(f32[2,2]{1,0:T(2,128)} %species_table.1) | copy-start | bytes 52
  13.2 37.3 %copy-start.26 = (s32[1,1,1,128]{3,2,1,0:T(1,128)S(1)}, s32[1,1,1,128]{3,2,1,0:T(1,128)}, u32[]{:S(2)}) copy-start(s32[1,1,1,128]{3,2,1,0:T(1,128)} %param.27) | copy-start | bytes 1540
  13.2 9.4 %collective-permute-start.2 = (bf16[1,2,4,16,640]{4,3,2,1,0:T(8,128)(2,1)S(1)}, bf16[1,2,4,16,640]{4,3,2,1,0:T(8,128)(2,1)S(1)}, u32[]{:S(2)}, u32[]{:S(2)}) collective-permute-start(bf16[1,2,4,16,640]{4,3,2,1,0:T(8,128)(2,1)S(1)} %get-tuple-element.43), channel_id=1, source_target_pairs={{0,16},{16,32},{32,48},{48,64},{64,80},{80,96},{96,112},{112,128},... | collective-permute-start | bytes 491528 | tf_op jit(solution)/shard_map/ppermute | solution.py:494
  15.2 7.4 %collective-permute-start.3 = (bf16[1,2,4,16,640]{4,3,2,1,0:T(8,128)(2,1)S(1)}, bf16[1,2,4,16,640]{4,3,2,1,0:T(8,128)(2,1)S(1)}, u32[]{:S(2)}, u32[]{:S(2)}) collective-permute-start(bf16[1,2,4,16,640]{4,3,2,1,0:T(8,128)(2,1)S(1)} %get-tuple-element.44), channel_id=1, source_target_pairs={{0,240},{16,0},{32,16},{48,32},{64,48},{80,64},{96,80},{112,96},{1... | collective-permute-start | bytes 491528 | tf_op jit(solution)/shard_map/ppermute | solution.py:495
  22.7 3.9 %collective-permute-start.4 = (bf16[4,2,4,16,640]{4,3,2,1,0:T(8,128)(2,1)S(1)}, bf16[4,2,4,16,640]{4,3,2,1,0:T(8,128)(2,1)S(1)}, u32[]{:S(2)}, u32[]{:S(2)}) collective-permute-start(bf16[4,2,4,16,640]{4,3,2,1,0:T(8,128)(2,1)S(1)} %pad_maximum_fusion), channel_id=1, source_target_pairs={{0,8},{8,0},{1,9},{9,1},{2,10},{10,2},{3,11},{11,3},{4,12},{12,4},... | collective-permute-start | bytes 1966088 | tf_op jit(solution)/shard_map/ppermute | solution.py:485
  26.7 29.8 %copy-start.11 = (bf16[256,256]{1,0:T(8,128)(2,1)S(1)}, bf16[256,256]{1,0:T(8,128)(2,1)}, u32[]{:S(2)}) copy-start(bf16[256,256]{1,0:T(8,128)(2,1)} %constant.30.clone.low) | copy-start | bytes 393220
  26.7 29.8 %copy-start.12 = (bf16[256,256]{1,0:T(8,128)(2,1)S(1)}, bf16[256,256]{1,0:T(8,128)(2,1)}, u32[]{:S(2)}) copy-start(bf16[256,256]{1,0:T(8,128)(2,1)} %constant.29.clone.high) | copy-start | bytes 393220
  26.7 30.7 %copy-start.14 = (bf16[128,128]{1,0:T(8,128)(2,1)S(1)}, bf16[128,128]{1,0:T(8,128)(2,1)}, u32[]{:S(2)}) copy-start(bf16[128,128]{1,0:T(8,128)(2,1)} %constant.31.clone.carry) | copy-start | bytes 98308
  31.8 7.7 %collective-permute-start.5 = (bf16[2,2,1,16,512]{4,3,2,1,0:T(8,128)(2,1)S(1)}, bf16[2,2,1,16,512]{4,3,2,1,0:T(8,128)(2,1)S(1)}, u32[]{:S(2)}, u32[]{:S(2)}) collective-permute-start(bf16[2,2,1,16,512]{4,3,2,1,0:T(8,128)(2,1)S(1)} %get-tuple-element.49), channel_id=1, source_target_pairs={{0,1},{1,2},{2,3},{3,4},{4,5},{5,6},{6,7},{7,0},{8,9},{9,10},{10,1... | collective-permute-start | bytes 196616 | tf_op jit(solution)/shard_map/ppermute | solution.py:491
  35.1 4.9 %collective-permute-start.6 = (bf16[2,2,1,16,512]{4,3,2,1,0:T(8,128)(2,1)S(1)}, bf16[2,2,1,16,512]{4,3,2,1,0:T(8,128)(2,1)S(1)}, u32[]{:S(2)}, u32[]{:S(2)}) collective-permute-start(bf16[2,2,1,16,512]{4,3,2,1,0:T(8,128)(2,1)S(1)} %get-tuple-element.50), channel_id=1, source_target_pairs={{0,7},{1,0},{2,1},{3,2},{4,3},{5,4},{6,5},{7,6},{8,15},{9,8},{10,9... | collective-permute-start | bytes 196616 | tf_op jit(solution)/shard_map/ppermute | solution.py:492
  40.0 6.0 %collective-permute-start.7 = (bf16[1,2,4,16,512]{4,3,2,1,0:T(8,128)(2,1)S(1)}, bf16[1,2,4,16,512]{4,3,2,1,0:T(8,128)(2,1)S(1)}, u32[]{:S(2)}, u32[]{:S(2)}) collective-permute-start(bf16[1,2,4,16,512]{4,3,2,1,0:T(8,128)(2,1)S(1)} %get-tuple-element.45), channel_id=1, source_target_pairs={{0,16},{16,32},{32,48},{48,64},{64,80},{80,96},{96,112},{112,128},... | collective-permute-start | bytes 393224 | tf_op jit(solution)/shard_map/ppermute | solution.py:494
  40.1 5.9 %collective-permute-start.8 = (bf16[1,2,4,16,512]{4,3,2,1,0:T(8,128)(2,1)S(1)}, bf16[1,2,4,16,512]{4,3,2,1,0:T(8,128)(2,1)S(1)}, u32[]{:S(2)}, u32[]{:S(2)}) collective-permute-start(bf16[1,2,4,16,512]{4,3,2,1,0:T(8,128)(2,1)S(1)} %get-tuple-element.46), channel_id=1, source_target_pairs={{0,240},{16,0},{32,16},{48,32},{64,48},{80,64},{96,80},{112,96},{1... | collective-permute-start | bytes 393224 | tf_op jit(solution)/shard_map/ppermute | solution.py:495
  46.1 4.3 %collective-permute-start.9 = (bf16[4,2,4,16,512]{4,3,2,1,0:T(8,128)(2,1)S(1)}, bf16[4,2,4,16,512]{4,3,2,1,0:T(8,128)(2,1)S(1)}, u32[]{:S(2)}, u32[]{:S(2)}) collective-permute-start(bf16[4,2,4,16,512]{4,3,2,1,0:T(8,128)(2,1)S(1)} %pad_maximum_fusion.1), channel_id=1, source_target_pairs={{0,8},{8,0},{1,9},{9,1},{2,10},{10,2},{3,11},{11,3},{4,12},{12,4},... | collective-permute-start | bytes 1572872 | tf_op jit(solution)/shard_map/ppermute | solution.py:485
  48.9 7.6 %collective-permute-start.10 = (f32[8,128]{1,0:T(8,128)S(1)}, f32[8,128]{1,0:T(8,128)S(1)}, u32[]{:S(2)}, u32[]{:S(2)}) collective-permute-start(f32[8,128]{1,0:T(8,128)S(1)} %get-tuple-element.27.own), channel_id=1, source_target_pairs={{0,8},{8,0},{1,9},{9,1},{2,10},{10,2},{3,11},{11,3},{4,12},{12,4},... | collective-permute-start | bytes 12296 | tf_op jit(solution)/shard_map/ppermute | solution.py:485
  50.4 33.8 %copy-start.4 = (bf16[1024,256]{1,0:T(8,128)(2,1)S(1)}, bf16[1024,256]{1,0:T(8,128)(2,1)}, u32[]{:S(2)}) copy-start(bf16[1024,256]{1,0:T(8,128)(2,1)} %constant.34.clone.zl) | copy-start | bytes 1572868
  50.4 33.8 %copy-start.5 = (bf16[1024,256]{1,0:T(8,128)(2,1)S(1)}, bf16[1024,256]{1,0:T(8,128)(2,1)}, u32[]{:S(2)}) copy-start(bf16[1024,256]{1,0:T(8,128)(2,1)} %constant.33.clone.zh) | copy-start | bytes 1572868
  50.4 33.8 %copy-start.6 = (bf16[3,128,256]{2,1,0:T(8,128)(2,1)S(1)}, bf16[3,128,256]{2,1,0:T(8,128)(2,1)}, u32[]{:S(2)}) copy-start(bf16[3,128,256]{2,1,0:T(8,128)(2,1)} %constant.38.clone.tl) | copy-start | bytes 589828
  50.4 33.8 %copy-start.7 = (bf16[3,128,256]{2,1,0:T(8,128)(2,1)S(1)}, bf16[3,128,256]{2,1,0:T(8,128)(2,1)}, u32[]{:S(2)}) copy-start(bf16[3,128,256]{2,1,0:T(8,128)(2,1)} %constant.37.clone.th) | copy-start | bytes 589828
  50.5 33.8 %copy-start.8 = (bf16[3,256,128]{2,1,0:T(8,128)(2,1)S(1)}, bf16[3,256,128]{2,1,0:T(8,128)(2,1)}, u32[]{:S(2)}) copy-start(bf16[3,256,128]{2,1,0:T(8,128)(2,1)} %constant.36.clone.xl) | copy-start | bytes 589828
  50.5 33.8 %copy-start.9 = (bf16[3,256,128]{2,1,0:T(8,128)(2,1)S(1)}, bf16[3,256,128]{2,1,0:T(8,128)(2,1)}, u32[]{:S(2)}) copy-start(bf16[3,256,128]{2,1,0:T(8,128)(2,1)} %constant.35.clone.xh) | copy-start | bytes 589828
  50.5 33.8 %copy-start.10 = (f32[256,2]{1,0:T(8,128)S(1)}, f32[256,2]{1,0:T(8,128)}, u32[]{:S(2)}) copy-start(f32[256,2]{1,0:T(8,128)} %constant.39.clone.col) | copy-start | bytes 6148
  50.5 33.8 %copy-start.13 = (bf16[2,128,128]{2,1,0:T(8,128)(2,1)S(1)}, bf16[2,128,128]{2,1,0:T(8,128)(2,1)}, u32[]{:S(2)}) copy-start(bf16[2,128,128]{2,1,0:T(8,128)(2,1)} %constant.41.clone.lines) | copy-start | bytes 196612
  50.5 33.8 %copy-start.18 = (f32[8,256]{1,0:T(8,128)S(1)}, f32[8,256]{1,0:T(8,128)}, u32[]{:S(2)}) copy-start(f32[8,256]{1,0:T(8,128)} %constant.40.clone.row) | copy-start | bytes 24580
  50.5 33.8 %copy-start.24 = (f32[256]{0:T(256)S(1)}, f32[256]{0:T(256)}, u32[]{:S(2)}) copy-start(f32[256]{0:T(256)} %constant.32.clone.scale_y) | copy-start | bytes 3076
  56.1 1.3 %collective-permute-start.11 = (f32[1,128]{1,0:T(1,128)S(1)}, f32[1,128]{1,0:T(1,128)S(1)}, u32[]{:S(2)}, u32[]{:S(2)}) collective-permute-start(f32[1,128]{1,0:T(1,128)S(1)} %get-tuple-element.31.own.charge), channel_id=1, source_target_pairs={{0,8},{8,0},{1,9},{9,1},{2,10},{10,2},{3,11},{11,3},{4,12},{12,4},... | collective-permute-start | bytes 1544 | tf_op jit(solution)/shard_map/ppermute | solution.py:485
  109.1 3.7 %collective-permute-start.12 = (f32[8,128]{1,0:T(8,128)S(1)}, f32[8,128]{1,0:T(8,128)S(1)}, u32[]{:S(2)}, u32[]{:S(2)}) collective-permute-start(f32[8,128]{1,0:T(8,128)S(1)} %get-tuple-element.33), channel_id=1, source_target_pairs={{0,8},{8,0},{1,9},{9,1},{2,10},{10,2},{3,11},{11,3},{4,12},{12,4},... | collective-permute-start | bytes 12296 | tf_op jit(solution)/shard_map/ppermute | solution.py:485

commit v4 on v3

--- a/solution.py
+++ b/solution.py
@@ -8,7 +8,7 @@
 from jax.experimental.pallas import tpu as pltpu
 from jax.sharding import PartitionSpec as P
 
-C = 128
+
 NB = 8
 HID = 64
 NEIGH = 16
@@ -87,7 +87,7 @@
             line[base + 39, base + point] = (point - 1) / 32.0
         move[base + 35, base + 36] = move[base + 39, base + 38] = 1.0
     out["lines"] = np.stack([-line, move - line]).astype(BF16)
-    out["basis_z"] = np_halves(zed.reshape(1024, MESH))
+    out["basis_z"] = np_halves(zed[:, :48].reshape(384, MESH))
     exx = np.zeros((3, MESH, 16, 8))
     for third in range(3):
         for part in range(16):
@@ -97,7 +97,6 @@
                     exx[third, :, part, group] = table[:, (part * BX + point - 1) % MESH]
     exx = exx.reshape(3, MESH, 128)
     out["basis_x"] = np_halves(exx)
-    out["basis_xt"] = np_halves(np.swapaxes(exx, 1, 2))
     out["col"] = np.stack([freq**2, factor], axis=1).astype(np.float32)
     row = np.zeros((8, MESH), np.float32)
     row[0], row[1] = freq**2, factor
@@ -194,17 +193,21 @@
 
 
 def gather_slots(rows, table, gathered, geometry=None):
-    for pair in range(NEIGH // 2):
-        wanted = jnp.concatenate(
-            [rows[2 * pair : 2 * pair + 1, :], rows[2 * pair + 1 : 2 * pair + 2, :]], axis=1
-        )
-        spots = lax.broadcasted_iota(jnp.int32, (1024, 256), 0)
-        one_hot = jnp.where(spots == wanted, 1.0, 0.0).astype(BF16)
-        found = dot(table[...], one_hot)
-        lanes = slice(pair * 256, pair * 256 + 256)
-        gathered[:, lanes] = found[:512].astype(BF16)
-        if geometry is not None:
-            geometry[:, lanes] = found[512:520]
+    def one_step(step, carry):
+        for pair in (2 * step, 2 * step + 1):
+            wanted = jnp.concatenate(
+                [rows[pl.ds(2 * pair, 1), :], rows[pl.ds(2 * pair + 1, 1), :]], axis=1
+            )
+            spots = lax.broadcasted_iota(jnp.int32, (1024, 256), 0)
+            one_hot = jnp.where(spots == wanted, 1.0, 0.0).astype(BF16)
+            found = dot(table[...], one_hot)
+            lanes = pl.ds(pl.multiple_of(pair * 256, 256), 256)
+            gathered[:, lanes] = found[:512].astype(BF16)
+            if geometry is not None:
+                geometry[:, lanes] = found[512:520]
+        return carry
+
+    lax.fori_loop(0, NEIGH // 4, one_step, 0)
 
 
 def silu(x):
@@ -212,9 +215,14 @@
 
 
 def messages(hidden, radial_out, radial, gathered, unit, message):
-    for pair in range(NEIGH // 2):
-        lanes = slice(pair * 256, pair * 256 + 256)
-        radial[:, lanes] = dot(radial_out, hidden[:, lanes], TN)
+    outward = transposed(radial_out)
+
+    def one_step(step, carry):
+        lanes = pl.ds(pl.multiple_of(step * 512, 512), 512)
+        radial[:, lanes] = dot(outward, hidden[:, lanes])
+        return carry
+
+    lax.fori_loop(0, NEIGH // 4, one_step, 0)
 
     def one_chunk(chunk, carry):
         start = pl.multiple_of(chunk * 32, 32)
@@ -253,13 +261,13 @@
 def first_kernel(
     feats, near, far, fraction, cells, octants, neighbours, radial_in, radial_out, mix_weight,
     new, outgoing, unit, hidden_next, rows_out,
-    table, gathered, geometry, radial, message,
+    table, gathered, geometry, radial, message, hidden,
 ):
     own = jnp.transpose(geometry_rows(cells, fraction)).astype(BF16)
     fill_table(table, feats, near, far, 528, own)
     rows, shifts = table_rows(neighbours[...])
     rows_out[...] = rows
-    gather_slots(rows, table, gathered, geometry)
+    gather_slots(rows_out, table, gathered, geometry)
     located = jnp.concatenate(cell_rows(cells), axis=0) + fraction[...].astype(F32)
     delta = []
     for d in range(3):
@@ -282,7 +290,7 @@
         away = distance[k : k + 1, :] - centres
         basis.append(jnp.exp(-(away * away)) * envelope[k : k + 1, :])
     basis = jnp.concatenate(basis, axis=1).astype(BF16)
-    hidden = silu(dot(radial_in[0], basis, TN)).astype(BF16)
+    hidden[...] = silu(dot(radial_in[0], basis, TN)).astype(BF16)
     hidden_next[...] = silu(dot(radial_in[1], basis, TN)).astype(BF16)
     messages(hidden, radial_out[0], radial, gathered, unit, message)
     mixed(feats, message, mix_weight, 0, new)
@@ -295,8 +303,8 @@
     table, gathered, radial, message,
 ):
     fill_table(table, feats, near, far, 512)
-    gather_slots(rows[...], table, gathered)
-    messages(hidden[...], radial_out[1], radial, gathered, unit, message)
+    gather_slots(rows, table, gathered)
+    messages(hidden, radial_out[1], radial, gathered, unit, message)
     mixed(feats, message, mix_weight, 1, new)
     heads = dot(readout[...], new[:, 0:128], NT)
     second = kinds[...] == 1
@@ -383,17 +391,21 @@
     charge = jnp.concatenate([own[...], other[...]], axis=1)
     charged = halves(weight_y[...] * charge)
     used = lax.broadcasted_iota(jnp.int32, (1, 128), 1) % ZPAD < 35
+    kept, lost = [], []
     for group in range(7):
         rows = slice(128 * group, 128 * group + 128)
         line = jnp.where(used, dot3(charged, (planes[0, rows, :], planes[1, rows, :]), NT), 0.0)
-        kept = line.astype(BF16).astype(F32)
-        lines[:, group, :] = kept + dot((line - kept).astype(BF16), carry[...])
+        kept.append(line.astype(BF16).astype(F32))
+        lost.append((line - kept[group]).astype(BF16))
+    carried = dot(jnp.concatenate(lost, axis=0), carry[...])
+    for group in range(7):
+        lines[:, group, :] = kept[group] + carried[128 * group : 128 * group + 128]
     lines[:, 7, :] = jnp.zeros((128, 128), F32)
     out[...] = lines[...].astype(BF16)
 
 
 def waves_kernel(
-    scale_y, received, zh, zl, xh, xl, th, tl, col, row, lines, out, coming, lhs,
+    scale_y, received, zh, zl, xh, xl, col, row, lines, out, coming, lhs, zed,
 ):
     for part in range(8):
         lanes = slice(part * 128, part * 128 + 128)
@@ -401,7 +413,10 @@
         for third in range(3):
             moved = block if third == 0 else pltpu.roll(block, 128 - ZPAD * third, 1)
             coming[third * 128 : third * 128 + 128, lanes] = moved.astype(BF16)
-    zed = (zh[...], zl[...])
+    for part in range(8):
+        for half, source in enumerate((zh, zl)):
+            zed[half, part * 128 : part * 128 + 48, :] = source[part * 48 : part * 48 + 48, :]
+            zed[half, part * 128 + 48 : part * 128 + 128, :] = jnp.zeros((80, MESH), BF16)
     rows = dot(coming[...], zed[0]) + dot(coming[...], zed[1])
     total = jnp.zeros((MESH, MESH), F32)
     for third in range(3):
@@ -418,7 +433,7 @@
     scaled = halves(total * kernel)
     for third in range(3):
         lhs[third * 128 : third * 128 + 128, :] = dot3(
-            halves(dot3((th[third], tl[third]), scaled)), zed, NT
+            halves(dot3((xh[third], xl[third]), scaled, TN)), (zed[0], zed[1]), NT
         )
     spot = lax.broadcasted_iota(jnp.int32, (1, 128), 1) % ZPAD
     spare = (spot >= 36) & (spot <= 38)
@@ -529,12 +544,16 @@
             pltpu.SemaphoreType.DMA((4,)),
         ],
         compiler_params=pltpu.CompilerParams(vmem_limit_bytes=8 << 20),
-    )(feats, part, cells, octants)
+    )(*[
+        pltpu.with_memory_space_constraint(x, pltpu.MemorySpace.HBM)
+        for x in (feats, part, cells, octants)
+    ])
     near, far = ghosts(outgoing)
+    others = partner(places)
     weight_y, slope_y, planes = call(
         static_kernel,
         [((128, 256), F32), ((128, 256), F32), ((6, 896, 256), BF16)],
-        places, partner(places), *table["basis_y"],
+        places, others, *table["basis_y"],
     )
     feats, outgoing, unit, hidden, rows = call(
         first_kernel,
@@ -552,6 +571,7 @@
             ((8, 2048), F32),
             ((512, 2048), F32),
             ((512, 128), BF16),
+            ((HID, 2048), BF16),
         ],
         limit=24,
     )
@@ -579,10 +599,10 @@
     (waves,) = call(
         waves_kernel,
         [((8, 128, 128), BF16)],
-        table["scale_y"], received, *table["basis_z"], *table["basis_x"], *table["basis_xt"],
+        table["scale_y"], received, *table["basis_z"], *table["basis_x"],
         table["col"], table["row"], table["lines"],
         scalars=(0,),
-        scratch=[((384, 1024), BF16), ((384, 1024), F32)],
+        scratch=[((384, 1024), BF16), ((384, 1024), F32), ((2, 1024, MESH), BF16)],
     )
     returned = across(waves.reshape(128, 8, 128))
     here, there = call(
@@ -603,6 +623,7 @@
 def solution(mesh):
     domain = P("gx", "gy", "gz", None, None)
     atoms = P("gx", "gy", "gz", None)
+
     return jax.shard_map(
         per_device,
         mesh=mesh,

time: 114 us -> 114 us (level)
  Pallas kernels: 19.7 us -> 23 us
  local copies, waits for them, and re-layouts: 3.2 us -> 0.2 us
    unnamed x56 -> x44, local copies, waits for them, and re-layouts: 3.12 us -> 0.12 us
    pallas_call x7, Pallas kernels: 19.1 us -> 21.6 us  [call(): pl.pallas_call(kernel, out_shape=[jax.ShapeDtypeStruct(s, d) for s, d in...]
  transfers between devices with their start and end apart: 13 -> 13, of which waited for: 9 -> 9; matrix products, arithmetic and copies ran while one was open for 0% -> 0% of each run, Pallas kernels for 6% -> 7%
where the time goes in v4:
time: 114 us
  blocking collectives  44.5 us (39%)
  starting transfers between devices  30.3 us (27%)
  Pallas kernels  23 us (20%)
  waiting for transfers between devices  14.4 us (13%)
    all_to_all x2, blocking collectives, across(): lax.all_to_all(blocks, ('gz', 'gx'), split_axis=0, concat_axis=0, tiled=T...  44.5 us
    pallas_call x7, Pallas kernels, call(): pl.pallas_call(kernel, out_shape=[jax.ShapeDtypeStruct(s, d) for s, d in...  21.6 us
    ppermute x5, starting transfers between devices, partner(): return lax.ppermute(block, 'gy', [(0, 1), (1, 0)])  8.28 us
    ppermute x2, starting transfers between devices, ghosts(): after = lax.ppermute(x[:1], 'gx', ring('gx', -1))  8 us
    ppermute x2, starting transfers between devices, ghosts(): before = lax.ppermute(x[:, :, 1:], 'gz', ring('gz', 1))  6.97 us
    ppermute x2, waiting for transfers between devices, ghosts(): before = lax.ppermute(x[1:], 'gx', ring('gx', 1))  5.3 us
    ppermute x2, starting transfers between devices, ghosts(): after = lax.ppermute(x[:, :, :1], 'gz', ring('gz', -1))  4.92 us
    ppermute x5, waiting for transfers between devices, partner(): return lax.ppermute(block, 'gy', [(0, 1), (1, 0)])  3.98 us
  transfers between devices with their start and end apart: 13, of which 9 were waited for; matrix products, arithmetic and copies ran while one was open for 0% of the time, Pallas kernels for 7%

profile of v4, /device:TPU:1, one launch (start us, length us, event | category | flops | bytes accessed | tf_op | source)
XLA Modules:
  0.0 113.6 jit_solution(16199883563197141916)
XLA Ops:
  0.7 1.4 %shard_map.229 = (bf16[128,640]{1,0:T(8,128)(2,1)S(1)}, f32[8,128]{1,0:T(8,128)S(1)}) custom-call(bf16[128,512]{1,0:T(8,128)(2,1)} %bitcast.29, bf16[3,128]{1,0:T(4,128)(2,1)} %bitcast.37, s32[1,384]{1,0:T(1,128)} %bitcast.35, s32[8,14]{1,0:T(8,128)} %bitcast.32), custom_call_target="tpu_custom_call" | custom-call | tf_op jit(solution)/shard_map/pallas_call | solution.py:532
  2.2 3.6 %collective-permute-start = (bf16[2,2,1,16,640]{4,3,2,1,0:T(8,128)(2,1)S(1)}, bf16[2,2,1,16,640]{4,3,2,1,0:T(8,128)(2,1)S(1)}, u32[]{:S(2)}, u32[]{:S(2)}) collective-permute-start(bf16[2,2,1,16,640]{4,3,2,1,0:T(8,128)(2,1)S(1)} %get-tuple-element.47), channel_id=1, source_target_pairs={{0,1},{1,2},{2,3},{3,4},{4,5},{5,6},{6,7},{7,0},{8,9},{9,10},{10,1... | collective-permute-start | bytes 245768 | tf_op jit(solution)/shard_map/ppermute | solution.py:506
  5.8 2.5 %collective-permute-start.1 = (bf16[2,2,1,16,640]{4,3,2,1,0:T(8,128)(2,1)S(1)}, bf16[2,2,1,16,640]{4,3,2,1,0:T(8,128)(2,1)S(1)}, u32[]{:S(2)}, u32[]{:S(2)}) collective-permute-start(bf16[2,2,1,16,640]{4,3,2,1,0:T(8,128)(2,1)S(1)} %get-tuple-element.48), channel_id=1, source_target_pairs={{0,7},{1,0},{2,1},{3,2},{4,3},{5,4},{6,5},{7,6},{8,15},{9,8},{10,9... | collective-permute-start | bytes 245768 | tf_op jit(solution)/shard_map/ppermute | solution.py:507
  8.4 1.7 %collective-permute-done = bf16[2,2,1,16,640]{4,3,2,1,0:T(8,128)(2,1)S(1)} collective-permute-done((bf16[2,2,1,16,640]{4,3,2,1,0:T(8,128)(2,1)S(1)}, bf16[2,2,1,16,640]{4,3,2,1,0:T(8,128)(2,1)S(1)}, u32[]{:S(2)}, u32[]{:S(2)}) %collective-permute-start) | collective-permute-done | bytes 81952 | tf_op jit(solution)/shard_map/ppermute | solution.py:506
  10.1 0.8 collective-permute-done.1
  11.0 0.0 copy-start.21
  11.0 0.0 copy-start.18
  11.0 0.0 copy-start.20
  11.0 2.0 %collective-permute-start.2 = (bf16[1,2,4,16,640]{4,3,2,1,0:T(8,128)(2,1)S(1)}, bf16[1,2,4,16,640]{4,3,2,1,0:T(8,128)(2,1)S(1)}, u32[]{:S(2)}, u32[]{:S(2)}) collective-permute-start(bf16[1,2,4,16,640]{4,3,2,1,0:T(8,128)(2,1)S(1)} %get-tuple-element.43), channel_id=1, source_target_pairs={{0,16},{16,32},{32,48},{48,64},{64,80},{80,96},{96,112},{112,128},... | collective-permute-start | bytes 491528 | tf_op jit(solution)/shard_map/ppermute | solution.py:509
  13.0 4.4 %collective-permute-start.3 = (bf16[1,2,4,16,640]{4,3,2,1,0:T(8,128)(2,1)S(1)}, bf16[1,2,4,16,640]{4,3,2,1,0:T(8,128)(2,1)S(1)}, u32[]{:S(2)}, u32[]{:S(2)}) collective-permute-start(bf16[1,2,4,16,640]{4,3,2,1,0:T(8,128)(2,1)S(1)} %get-tuple-element.44), channel_id=1, source_target_pairs={{0,240},{16,0},{32,16},{48,32},{64,48},{80,64},{96,80},{112,96},{1... | collective-permute-start | bytes 491528 | tf_op jit(solution)/shard_map/ppermute | solution.py:510
  17.5 3.0 %collective-permute-done.2 = bf16[1,2,4,16,640]{4,3,2,1,0:T(8,128)(2,1)S(1)} collective-permute-done((bf16[1,2,4,16,640]{4,3,2,1,0:T(8,128)(2,1)S(1)}, bf16[1,2,4,16,640]{4,3,2,1,0:T(8,128)(2,1)S(1)}, u32[]{:S(2)}, u32[]{:S(2)}) %collective-permute-start.2) | collective-permute-done | bytes 163872 | tf_op jit(solution)/shard_map/ppermute | solution.py:509
  20.4 0.0 collective-permute-done.3
  20.4 0.1 pad_maximum_fusion
  20.5 2.2 %collective-permute-start.4 = (bf16[4,2,4,16,640]{4,3,2,1,0:T(8,128)(2,1)S(1)}, bf16[4,2,4,16,640]{4,3,2,1,0:T(8,128)(2,1)S(1)}, u32[]{:S(2)}, u32[]{:S(2)}) collective-permute-start(bf16[4,2,4,16,640]{4,3,2,1,0:T(8,128)(2,1)S(1)} %pad_maximum_fusion), channel_id=1, source_target_pairs={{0,8},{8,0},{1,9},{9,1},{2,10},{10,2},{3,11},{11,3},{4,12},{12,4},... | collective-permute-start | bytes 1966088 | tf_op jit(solution)/shard_map/ppermute | solution.py:500
  22.7 1.7 %collective-permute-done.4 = bf16[4,2,4,16,640]{4,3,2,1,0:T(8,128)(2,1)S(1)} collective-permute-done((bf16[4,2,4,16,640]{4,3,2,1,0:T(8,128)(2,1)S(1)}, bf16[4,2,4,16,640]{4,3,2,1,0:T(8,128)(2,1)S(1)}, u32[]{:S(2)}, u32[]{:S(2)}) %collective-permute-start.4) | collective-permute-done | bytes 655392 | tf_op jit(solution)/shard_map/ppermute | solution.py:500
  24.5 0.0 copy-start.7
  24.5 0.0 copy-start.8
  24.5 0.0 copy-start.11
  24.6 6.5 %shard_map.230 = (bf16[128,512]{1,0:T(8,128)(2,1)S(1)}, bf16[128,512]{1,0:T(8,128)(2,1)S(1)}, f32[48,128]{1,0:T(8,128)S(1)}, bf16[64,2048]{1,0:T(8,128)(2,1)S(1)}, s32[16,128]{1,0:T(8,128)S(1)}) custom-call(bf16[128,512]{1,0:T(8,128)(2,1)S(1)} %bitcast.30, bf16[512,640]{1,0:T(8,128)(2,1)S(1)} %bitcast.18, bf16[512,640]{1,0:T(8,128)(2,1)S(1)} %bitcast.28, ...), custom_call_target="tpu_custom_call" | custom-call | tf_op jit(solution)/shard_map/pallas_call | solution.py:484
  31.1 3.3 %collective-permute-start.5 = (bf16[2,2,1,16,512]{4,3,2,1,0:T(8,128)(2,1)S(1)}, bf16[2,2,1,16,512]{4,3,2,1,0:T(8,128)(2,1)S(1)}, u32[]{:S(2)}, u32[]{:S(2)}) collective-permute-start(bf16[2,2,1,16,512]{4,3,2,1,0:T(8,128)(2,1)S(1)} %get-tuple-element.49), channel_id=1, source_target_pairs={{0,1},{1,2},{2,3},{3,4},{4,5},{5,6},{6,7},{7,0},{8,9},{9,10},{10,1... | collective-permute-start | bytes 196616 | tf_op jit(solution)/shard_map/ppermute | solution.py:506
  34.4 2.4 %collective-permute-start.6 = (bf16[2,2,1,16,512]{4,3,2,1,0:T(8,128)(2,1)S(1)}, bf16[2,2,1,16,512]{4,3,2,1,0:T(8,128)(2,1)S(1)}, u32[]{:S(2)}, u32[]{:S(2)}) collective-permute-start(bf16[2,2,1,16,512]{4,3,2,1,0:T(8,128)(2,1)S(1)} %get-tuple-element.50), channel_id=1, source_target_pairs={{0,7},{1,0},{2,1},{3,2},{4,3},{5,4},{6,5},{7,6},{8,15},{9,8},{10,9... | collective-permute-start | bytes 196616 | tf_op jit(solution)/shard_map/ppermute | solution.py:507
  36.8 2.0 %collective-permute-done.5 = bf16[2,2,1,16,512]{4,3,2,1,0:T(8,128)(2,1)S(1)} collective-permute-done((bf16[2,2,1,16,512]{4,3,2,1,0:T(8,128)(2,1)S(1)}, bf16[2,2,1,16,512]{4,3,2,1,0:T(8,128)(2,1)S(1)}, u32[]{:S(2)}, u32[]{:S(2)}) %collective-permute-start.5) | collective-permute-done | bytes 65568 | tf_op jit(solution)/shard_map/ppermute | solution.py:506
  38.8 0.5 collective-permute-done.6
  39.4 0.1 collective-permute-start.7
  39.5 3.6 %collective-permute-start.8 = (bf16[1,2,4,16,512]{4,3,2,1,0:T(8,128)(2,1)S(1)}, bf16[1,2,4,16,512]{4,3,2,1,0:T(8,128)(2,1)S(1)}, u32[]{:S(2)}, u32[]{:S(2)}) collective-permute-start(bf16[1,2,4,16,512]{4,3,2,1,0:T(8,128)(2,1)S(1)} %get-tuple-element.46), channel_id=1, source_target_pairs={{0,240},{16,0},{32,16},{48,32},{64,48},{80,64},{96,80},{112,96},{1... | collective-permute-start | bytes 393224 | tf_op jit(solution)/shard_map/ppermute | solution.py:510
  43.1 2.4 %collective-permute-done.7 = bf16[1,2,4,16,512]{4,3,2,1,0:T(8,128)(2,1)S(1)} collective-permute-done((bf16[1,2,4,16,512]{4,3,2,1,0:T(8,128)(2,1)S(1)}, bf16[1,2,4,16,512]{4,3,2,1,0:T(8,128)(2,1)S(1)}, u32[]{:S(2)}, u32[]{:S(2)}) %collective-permute-start.7) | collective-permute-done | bytes 131104 | tf_op jit(solution)/shard_map/ppermute | solution.py:509
  45.4 0.1 pad_maximum_fusion.1
  45.5 2.8 %collective-permute-start.9 = (bf16[4,2,4,16,512]{4,3,2,1,0:T(8,128)(2,1)S(1)}, bf16[4,2,4,16,512]{4,3,2,1,0:T(8,128)(2,1)S(1)}, u32[]{:S(2)}, u32[]{:S(2)}) collective-permute-start(bf16[4,2,4,16,512]{4,3,2,1,0:T(8,128)(2,1)S(1)} %pad_maximum_fusion.1), channel_id=1, source_target_pairs={{0,8},{8,0},{1,9},{9,1},{2,10},{10,2},{3,11},{11,3},{4,12},{12,4},... | collective-permute-start | bytes 1572872 | tf_op jit(solution)/shard_map/ppermute | solution.py:500
  48.3 0.1 collective-permute-start.10
  48.4 1.4 %collective-permute-done.9 = bf16[4,2,4,16,512]{4,3,2,1,0:T(8,128)(2,1)S(1)} collective-permute-done((bf16[4,2,4,16,512]{4,3,2,1,0:T(8,128)(2,1)S(1)}, bf16[4,2,4,16,512]{4,3,2,1,0:T(8,128)(2,1)S(1)}, u32[]{:S(2)}, u32[]{:S(2)}) %collective-permute-start.9) | collective-permute-done | bytes 524320 | tf_op jit(solution)/shard_map/ppermute | solution.py:500
  49.8 0.0 copy-start.5
  49.8 0.0 copy-start.6
  49.8 0.0 copy-start.9
  49.8 0.0 copy-start.10
  49.9 0.0 copy-start.14
  49.9 0.0 copy-start.19
  49.9 7.0 %shard_map.231 = (bf16[128,512]{1,0:T(8,128)(2,1)}, f32[1,128]{1,0:T(1,128)S(1)}, f32[1,128]{1,0:T(1,128)S(1)}) custom-call(bf16[128,512]{1,0:T(8,128)(2,1)S(1)} %get-tuple-element.21.feats, bf16[512,512]{1,0:T(8,128)(2,1)S(1)} %bitcast.19, bf16[512,512]{1,0:T(8,128)(2,1)S(1)} %bitcast.31, s32[16,128]{1,0:T(8,128)S(1)} %get-tuple-element.23.rows, ...), custom_call_target="tpu_custom_call" | custom-call | tf_op jit(solution)/shard_map/pallas_call | solution.py:484
  56.9 0.4 collective-permute-start.11
  57.3 0.9 shard_map.232
  58.3 0.0 collective-permute-done.11.other
  58.3 0.8 shard_map.233
  59.1 25.4 %all_to_all.10 = bf16[128,8,128]{2,1,0:T(8,128)(2,1)S(1)} all-to-all(bf16[128,8,128]{2,1,0:T(8,128)(2,1)S(1)} %shard_map.233), channel_id=1, replica_groups=mesh['gx'=16,'gy'=2,'gz'=8] {'gz','gx'}, dimensions={0} | all-to-all | bytes 524288 | tf_op jit(solution)/shard_map/all_to_all | solution.py:516
  84.6 4.9 %shard_map.234 = bf16[8,128,128]{2,1,0:T(8,128)(2,1)S(1)} custom-call(f32[256]{0:T(256)S(1)} %copy-done.19, bf16[8,128,128]{2,1,0:T(8,128)(2,1)S(1)} %bitcast.26, bf16[384,256]{1,0:T(8,128)(2,1)S(1)} %copy-done.6, bf16[384,256]{1,0:T(8,128)(2,1)S(1)} %copy-done.5, bf16[3,256,128]{2,1,0:T(8,128)(2,1)S(1)} %copy-done.4, bf16[3,256,128]{2,1,0:T(8,128)(2,1)S(1)} %copy-done.3, ...), custom_call_target="tpu_custom_call" | custom-call | tf_op jit(solution)/shard_map/pallas_call | solution.py:484
  89.5 19.1 %all_to_all.11.returned = bf16[128,8,128]{2,1,0:T(8,128)(2,1)S(1)} all-to-all(bf16[128,8,128]{2,1,0:T(8,128)(2,1)S(1)} %bitcast.27), channel_id=1, replica_groups=mesh['gx'=16,'gy'=2,'gz'=8] {'gz','gx'}, dimensions={0} | all-to-all | bytes 524288 | tf_op jit(solution)/shard_map/all_to_all | solution.py:516
  108.6 0.7 shard_map.235
  109.3 2.8 %collective-permute-start.12 = (f32[8,128]{1,0:T(8,128)S(1)}, f32[8,128]{1,0:T(8,128)S(1)}, u32[]{:S(2)}, u32[]{:S(2)}) collective-permute-start(f32[8,128]{1,0:T(8,128)S(1)} %get-tuple-element.33), channel_id=1, source_target_pairs={{0,8},{8,0},{1,9},{9,1},{2,10},{10,2},{3,11},{11,3},{4,12},{12,4},... | collective-permute-start | bytes 12296 | tf_op jit(solution)/shard_map/ppermute | solution.py:500
  112.2 0.8 collective-permute-done.12.there
  113.0 0.6 shard_map.236
  (41 shorter events, 0.2 us)
Async XLA Ops:
  0.6 23.8 %copy-start.12 = (s32[1,1,1,8,14]{4,3,2,1,0:T(8,128)S(1)}, s32[1,1,1,8,14]{4,3,2,1,0:T(8,128)}, u32[]{:S(2)}) copy-start(s32[1,1,1,8,14]{4,3,2,1,0:T(8,128)} %param.26) | copy-start | bytes 1348
  0.6 23.8 %copy-start.15 = (s32[1,1,1,3,128]{4,2,3,1,0:T(1,128)S(1)}, s32[1,1,1,3,128]{4,2,3,1,0:T(1,128)}, u32[]{:S(2)}) copy-start(s32[1,1,1,3,128]{4,2,3,1,0:T(1,128)} %param.24) | copy-start | bytes 4612
  0.7 23.8 %copy-start.17 = (bf16[1,1,1,3,128]{4,3,2,1,0:T(4,128)(2,1)S(1)}, bf16[1,1,1,3,128]{4,3,2,1,0:T(4,128)(2,1)}, u32[]{:S(2)}) copy-start(bf16[1,1,1,3,128]{4,3,2,1,0:T(4,128)(2,1)} %param.23) | copy-start | bytes 2308
  0.7 23.8 %copy-start.2 = (bf16[1,1,1,128,512]{4,3,2,1,0:T(8,128)(2,1)S(1)}, bf16[1,1,1,128,512]{4,3,2,1,0:T(8,128)(2,1)}, u32[]{:S(2)}) copy-start(bf16[1,1,1,128,512]{4,3,2,1,0:T(8,128)(2,1)} %param.22) | copy-start | bytes 393220
  0.7 23.8 %copy-start.1 = (bf16[2,2,128,128]{3,2,1,0:T(8,128)(2,1)S(1)}, bf16[2,2,128,128]{3,2,1,0:T(8,128)(2,1)}, u32[]{:S(2)}) copy-start(bf16[2,2,128,128]{3,2,1,0:T(8,128)(2,1)} %mix_weight.3) | copy-start | bytes 393220
  0.7 23.8 %copy-start = (bf16[2,64,512]{2,1,0:T(8,128)(2,1)S(1)}, bf16[2,64,512]{2,1,0:T(8,128)(2,1)}, u32[]{:S(2)}) copy-start(bf16[2,64,512]{2,1,0:T(8,128)(2,1)} %radial_out.3) | copy-start | bytes 393220
  0.7 23.8 %copy-start.16 = (bf16[2,8,64]{2,1,0:T(8,128)(2,1)S(1)}, bf16[2,8,64]{2,1,0:T(8,128)(2,1)}, u32[]{:S(2)}) copy-start(bf16[2,8,64]{2,1,0:T(8,128)(2,1)} %radial_in.1) | copy-start | bytes 6148
  0.7 23.8 %copy-start.13 = (s32[1,1,1,16,128]{4,3,2,1,0:T(8,128)S(1)}, s32[1,1,1,16,128]{4,3,2,1,0:T(8,128)}, u32[]{:S(2)}) copy-start(s32[1,1,1,16,128]{4,3,2,1,0:T(8,128)} %param.27) | copy-start | bytes 24580
  2.2 7.9 %collective-permute-start = (bf16[2,2,1,16,640]{4,3,2,1,0:T(8,128)(2,1)S(1)}, bf16[2,2,1,16,640]{4,3,2,1,0:T(8,128)(2,1)S(1)}, u32[]{:S(2)}, u32[]{:S(2)}) collective-permute-start(bf16[2,2,1,16,640]{4,3,2,1,0:T(8,128)(2,1)S(1)} %get-tuple-element.47), channel_id=1, source_target_pairs={{0,1},{1,2},{2,3},{3,4},{4,5},{5,6},{6,7},{7,0},{8,9},{9,10},{10,1... | collective-permute-start | bytes 245768 | tf_op jit(solution)/shard_map/ppermute | solution.py:506
  5.8 5.1 %collective-permute-start.1 = (bf16[2,2,1,16,640]{4,3,2,1,0:T(8,128)(2,1)S(1)}, bf16[2,2,1,16,640]{4,3,2,1,0:T(8,128)(2,1)S(1)}, u32[]{:S(2)}, u32[]{:S(2)}) collective-permute-start(bf16[2,2,1,16,640]{4,3,2,1,0:T(8,128)(2,1)S(1)} %get-tuple-element.48), channel_id=1, source_target_pairs={{0,7},{1,0},{2,1},{3,2},{4,3},{5,4},{6,5},{7,6},{8,15},{9,8},{10,9... | collective-permute-start | bytes 245768 | tf_op jit(solution)/shard_map/ppermute | solution.py:507
  11.0 37.4 %copy-start.21 = (bf16[128,2]{0,1:T(2,128)(2,1)S(1)}, bf16[128,2]{0,1:T(2,128)(2,1)}, u32[]{:S(2)}) copy-start(bf16[128,2]{0,1:T(2,128)(2,1)} %param.31) | copy-start | bytes 1540
  11.0 38.8 %copy-start.18 = (f32[2,2]{1,0:T(2,128)S(1)}, f32[2,2]{1,0:T(2,128)}, u32[]{:S(2)}) copy-start(f32[2,2]{1,0:T(2,128)} %species_table.1) | copy-start | bytes 52
  11.0 38.8 %copy-start.20 = (s32[1,1,1,128]{3,2,1,0:T(1,128)S(1)}, s32[1,1,1,128]{3,2,1,0:T(1,128)}, u32[]{:S(2)}) copy-start(s32[1,1,1,128]{3,2,1,0:T(1,128)} %param.25) | copy-start | bytes 1540
  11.0 9.4 %collective-permute-start.2 = (bf16[1,2,4,16,640]{4,3,2,1,0:T(8,128)(2,1)S(1)}, bf16[1,2,4,16,640]{4,3,2,1,0:T(8,128)(2,1)S(1)}, u32[]{:S(2)}, u32[]{:S(2)}) collective-permute-start(bf16[1,2,4,16,640]{4,3,2,1,0:T(8,128)(2,1)S(1)} %get-tuple-element.43), channel_id=1, source_target_pairs={{0,16},{16,32},{32,48},{48,64},{64,80},{80,96},{96,112},{112,128},... | collective-permute-start | bytes 491528 | tf_op jit(solution)/shard_map/ppermute | solution.py:509
  13.0 7.4 %collective-permute-start.3 = (bf16[1,2,4,16,640]{4,3,2,1,0:T(8,128)(2,1)S(1)}, bf16[1,2,4,16,640]{4,3,2,1,0:T(8,128)(2,1)S(1)}, u32[]{:S(2)}, u32[]{:S(2)}) collective-permute-start(bf16[1,2,4,16,640]{4,3,2,1,0:T(8,128)(2,1)S(1)} %get-tuple-element.44), channel_id=1, source_target_pairs={{0,240},{16,0},{32,16},{48,32},{64,48},{80,64},{96,80},{112,96},{1... | collective-permute-start | bytes 491528 | tf_op jit(solution)/shard_map/ppermute | solution.py:510
  20.5 3.9 %collective-permute-start.4 = (bf16[4,2,4,16,640]{4,3,2,1,0:T(8,128)(2,1)S(1)}, bf16[4,2,4,16,640]{4,3,2,1,0:T(8,128)(2,1)S(1)}, u32[]{:S(2)}, u32[]{:S(2)}) collective-permute-start(bf16[4,2,4,16,640]{4,3,2,1,0:T(8,128)(2,1)S(1)} %pad_maximum_fusion), channel_id=1, source_target_pairs={{0,8},{8,0},{1,9},{9,1},{2,10},{10,2},{3,11},{11,3},{4,12},{12,4},... | collective-permute-start | bytes 1966088 | tf_op jit(solution)/shard_map/ppermute | solution.py:500
  24.5 32.8 %copy-start.7 = (bf16[256,256]{1,0:T(8,128)(2,1)S(1)}, bf16[256,256]{1,0:T(8,128)(2,1)}, u32[]{:S(2)}) copy-start(bf16[256,256]{1,0:T(8,128)(2,1)} %constant.26.clone.low) | copy-start | bytes 393220
  24.5 32.8 %copy-start.8 = (bf16[256,256]{1,0:T(8,128)(2,1)S(1)}, bf16[256,256]{1,0:T(8,128)(2,1)}, u32[]{:S(2)}) copy-start(bf16[256,256]{1,0:T(8,128)(2,1)} %constant.25.clone.high) | copy-start | bytes 393220
  24.5 33.8 %copy-start.11 = (bf16[128,128]{1,0:T(8,128)(2,1)S(1)}, bf16[128,128]{1,0:T(8,128)(2,1)}, u32[]{:S(2)}) copy-start(bf16[128,128]{1,0:T(8,128)(2,1)} %constant.27.clone.carry) | copy-start | bytes 98308
  31.1 7.7 %collective-permute-start.5 = (bf16[2,2,1,16,512]{4,3,2,1,0:T(8,128)(2,1)S(1)}, bf16[2,2,1,16,512]{4,3,2,1,0:T(8,128)(2,1)S(1)}, u32[]{:S(2)}, u32[]{:S(2)}) collective-permute-start(bf16[2,2,1,16,512]{4,3,2,1,0:T(8,128)(2,1)S(1)} %get-tuple-element.49), channel_id=1, source_target_pairs={{0,1},{1,2},{2,3},{3,4},{4,5},{5,6},{6,7},{7,0},{8,9},{9,10},{10,1... | collective-permute-start | bytes 196616 | tf_op jit(solution)/shard_map/ppermute | solution.py:506
  34.4 4.9 %collective-permute-start.6 = (bf16[2,2,1,16,512]{4,3,2,1,0:T(8,128)(2,1)S(1)}, bf16[2,2,1,16,512]{4,3,2,1,0:T(8,128)(2,1)S(1)}, u32[]{:S(2)}, u32[]{:S(2)}) collective-permute-start(bf16[2,2,1,16,512]{4,3,2,1,0:T(8,128)(2,1)S(1)} %get-tuple-element.50), channel_id=1, source_target_pairs={{0,7},{1,0},{2,1},{3,2},{4,3},{5,4},{6,5},{7,6},{8,15},{9,8},{10,9... | collective-permute-start | bytes 196616 | tf_op jit(solution)/shard_map/ppermute | solution.py:507
  39.4 6.0 %collective-permute-start.7 = (bf16[1,2,4,16,512]{4,3,2,1,0:T(8,128)(2,1)S(1)}, bf16[1,2,4,16,512]{4,3,2,1,0:T(8,128)(2,1)S(1)}, u32[]{:S(2)}, u32[]{:S(2)}) collective-permute-start(bf16[1,2,4,16,512]{4,3,2,1,0:T(8,128)(2,1)S(1)} %get-tuple-element.45), channel_id=1, source_target_pairs={{0,16},{16,32},{32,48},{48,64},{64,80},{80,96},{96,112},{112,128},... | collective-permute-start | bytes 393224 | tf_op jit(solution)/shard_map/ppermute | solution.py:509
  39.5 5.9 %collective-permute-start.8 = (bf16[1,2,4,16,512]{4,3,2,1,0:T(8,128)(2,1)S(1)}, bf16[1,2,4,16,512]{4,3,2,1,0:T(8,128)(2,1)S(1)}, u32[]{:S(2)}, u32[]{:S(2)}) collective-permute-start(bf16[1,2,4,16,512]{4,3,2,1,0:T(8,128)(2,1)S(1)} %get-tuple-element.46), channel_id=1, source_target_pairs={{0,240},{16,0},{32,16},{48,32},{64,48},{80,64},{96,80},{112,96},{1... | collective-permute-start | bytes 393224 | tf_op jit(solution)/shard_map/ppermute | solution.py:510
  45.5 4.3 %collective-permute-start.9 = (bf16[4,2,4,16,512]{4,3,2,1,0:T(8,128)(2,1)S(1)}, bf16[4,2,4,16,512]{4,3,2,1,0:T(8,128)(2,1)S(1)}, u32[]{:S(2)}, u32[]{:S(2)}) collective-permute-start(bf16[4,2,4,16,512]{4,3,2,1,0:T(8,128)(2,1)S(1)} %pad_maximum_fusion.1), channel_id=1, source_target_pairs={{0,8},{8,0},{1,9},{9,1},{2,10},{10,2},{3,11},{11,3},{4,12},{12,4},... | collective-permute-start | bytes 1572872 | tf_op jit(solution)/shard_map/ppermute | solution.py:500
  48.3 9.1 %collective-permute-start.10 = (f32[8,128]{1,0:T(8,128)S(1)}, f32[8,128]{1,0:T(8,128)S(1)}, u32[]{:S(2)}, u32[]{:S(2)}) collective-permute-start(f32[8,128]{1,0:T(8,128)S(1)} %get-tuple-element.27.own), channel_id=1, source_target_pairs={{0,8},{8,0},{1,9},{9,1},{2,10},{10,2},{3,11},{11,3},{4,12},{12,4},... | collective-permute-start | bytes 12296 | tf_op jit(solution)/shard_map/ppermute | solution.py:500
  49.8 34.7 %copy-start.3 = (bf16[3,256,128]{2,1,0:T(8,128)(2,1)S(1)}, bf16[3,256,128]{2,1,0:T(8,128)(2,1)}, u32[]{:S(2)}) copy-start(bf16[3,256,128]{2,1,0:T(8,128)(2,1)} %constant.32.clone.xl) | copy-start | bytes 589828
  49.8 34.7 %copy-start.4 = (bf16[3,256,128]{2,1,0:T(8,128)(2,1)S(1)}, bf16[3,256,128]{2,1,0:T(8,128)(2,1)}, u32[]{:S(2)}) copy-start(bf16[3,256,128]{2,1,0:T(8,128)(2,1)} %constant.31.clone.xh) | copy-start | bytes 589828
  49.8 34.7 %copy-start.5 = (bf16[384,256]{1,0:T(8,128)(2,1)S(1)}, bf16[384,256]{1,0:T(8,128)(2,1)}, u32[]{:S(2)}) copy-start(bf16[384,256]{1,0:T(8,128)(2,1)} %constant.30.clone.zl) | copy-start | bytes 589828
  49.8 34.7 %copy-start.6 = (bf16[384,256]{1,0:T(8,128)(2,1)S(1)}, bf16[384,256]{1,0:T(8,128)(2,1)}, u32[]{:S(2)}) copy-start(bf16[384,256]{1,0:T(8,128)(2,1)} %constant.29.clone.zh) | copy-start | bytes 589828
  49.8 34.7 %copy-start.9 = (f32[256,2]{1,0:T(8,128)S(1)}, f32[256,2]{1,0:T(8,128)}, u32[]{:S(2)}) copy-start(f32[256,2]{1,0:T(8,128)} %constant.33.clone.col) | copy-start | bytes 6148
  49.8 34.7 %copy-start.10 = (bf16[2,128,128]{2,1,0:T(8,128)(2,1)S(1)}, bf16[2,128,128]{2,1,0:T(8,128)(2,1)}, u32[]{:S(2)}) copy-start(bf16[2,128,128]{2,1,0:T(8,128)(2,1)} %constant.35.clone.lines) | copy-start | bytes 196612
  49.9 34.7 %copy-start.14 = (f32[8,256]{1,0:T(8,128)S(1)}, f32[8,256]{1,0:T(8,128)}, u32[]{:S(2)}) copy-start(f32[8,256]{1,0:T(8,128)} %constant.34.clone.row) | copy-start | bytes 24580
  49.9 34.7 %copy-start.19 = (f32[256]{0:T(256)S(1)}, f32[256]{0:T(256)}, u32[]{:S(2)}) copy-start(f32[256]{0:T(256)} %constant.28.clone.scale_y) | copy-start | bytes 3076
  56.9 1.4 %collective-permute-start.11 = (f32[1,128]{1,0:T(1,128)S(1)}, f32[1,128]{1,0:T(1,128)S(1)}, u32[]{:S(2)}, u32[]{:S(2)}) collective-permute-start(f32[1,128]{1,0:T(1,128)S(1)} %get-tuple-element.31.own.charge), channel_id=1, source_target_pairs={{0,8},{8,0},{1,9},{9,1},{2,10},{10,2},{3,11},{11,3},{4,12},{12,4},... | collective-permute-start | bytes 1544 | tf_op jit(solution)/shard_map/ppermute | solution.py:500
  109.3 3.7 %collective-permute-start.12 = (f32[8,128]{1,0:T(8,128)S(1)}, f32[8,128]{1,0:T(8,128)S(1)}, u32[]{:S(2)}, u32[]{:S(2)}) collective-permute-start(f32[8,128]{1,0:T(8,128)S(1)} %get-tuple-element.33), channel_id=1, source_target_pairs={{0,8},{8,0},{1,9},{9,1},{2,10},{10,2},{3,11},{11,3},{4,12},{12,4},... | collective-permute-start | bytes 12296 | tf_op jit(solution)/shard_map/ppermute | solution.py:500

commit v5 on v3

--- a/solution.py
+++ b/solution.py
@@ -8,7 +8,7 @@
 from jax.experimental.pallas import tpu as pltpu
 from jax.sharding import PartitionSpec as P
 
-C = 128
+
 NB = 8
 HID = 64
 NEIGH = 16
@@ -212,9 +212,10 @@
 
 
 def messages(hidden, radial_out, radial, gathered, unit, message):
+    outward = transposed(radial_out)
     for pair in range(NEIGH // 2):
         lanes = slice(pair * 256, pair * 256 + 256)
-        radial[:, lanes] = dot(radial_out, hidden[:, lanes], TN)
+        radial[:, lanes] = dot(outward, hidden[:, lanes])
 
     def one_chunk(chunk, carry):
         start = pl.multiple_of(chunk * 32, 32)
@@ -383,11 +384,15 @@
     charge = jnp.concatenate([own[...], other[...]], axis=1)
     charged = halves(weight_y[...] * charge)
     used = lax.broadcasted_iota(jnp.int32, (1, 128), 1) % ZPAD < 35
+    kept, lost = [], []
     for group in range(7):
         rows = slice(128 * group, 128 * group + 128)
         line = jnp.where(used, dot3(charged, (planes[0, rows, :], planes[1, rows, :]), NT), 0.0)
-        kept = line.astype(BF16).astype(F32)
-        lines[:, group, :] = kept + dot((line - kept).astype(BF16), carry[...])
+        kept.append(line.astype(BF16).astype(F32))
+        lost.append((line - kept[group]).astype(BF16))
+    carried = dot(jnp.concatenate(lost, axis=0), carry[...])
+    for group in range(7):
+        lines[:, group, :] = kept[group] + carried[128 * group : 128 * group + 128]
     lines[:, 7, :] = jnp.zeros((128, 128), F32)
     out[...] = lines[...].astype(BF16)
 
@@ -529,12 +534,16 @@
             pltpu.SemaphoreType.DMA((4,)),
         ],
         compiler_params=pltpu.CompilerParams(vmem_limit_bytes=8 << 20),
-    )(feats, part, cells, octants)
+    )(*[
+        pltpu.with_memory_space_constraint(x, pltpu.MemorySpace.HBM)
+        for x in (feats, part, cells, octants)
+    ])
     near, far = ghosts(outgoing)
+    others = partner(places)
     weight_y, slope_y, planes = call(
         static_kernel,
         [((128, 256), F32), ((128, 256), F32), ((6, 896, 256), BF16)],
-        places, partner(places), *table["basis_y"],
+        places, others, *table["basis_y"],
     )
     feats, outgoing, unit, hidden, rows = call(
         first_kernel,
@@ -603,6 +612,7 @@
 def solution(mesh):
     domain = P("gx", "gy", "gz", None, None)
     atoms = P("gx", "gy", "gz", None)
+
     return jax.shard_map(
         per_device,
         mesh=mesh,

time: 114 us -> 111 us (0.974)
  local copies, waits for them, and re-layouts: 3.2 us -> 0.22 us
    unnamed x56 -> x48, local copies, waits for them, and re-layouts: 3.12 us -> 0.14 us
where the time goes in v5:
time: 111 us
  blocking collectives  44.5 us (40%)
  starting transfers between devices  30.4 us (27%)
  Pallas kernels  19.9 us (18%)
  waiting for transfers between devices  14.2 us (13%)
    all_to_all x2, blocking collectives, across(): lax.all_to_all(blocks, ('gz', 'gx'), split_axis=0, concat_axis=0, tiled=T...  44.5 us
    pallas_call x7, Pallas kernels, call(): pl.pallas_call(kernel, out_shape=[jax.ShapeDtypeStruct(s, d) for s, d in...  18.5 us
    ppermute x5, starting transfers between devices, partner(): return lax.ppermute(block, 'gy', [(0, 1), (1, 0)])  8.41 us
    ppermute x2, starting transfers between devices, ghosts(): after = lax.ppermute(x[:1], 'gx', ring('gx', -1))  8 us
    ppermute x2, starting transfers between devices, ghosts(): before = lax.ppermute(x[:, :, 1:], 'gz', ring('gz', 1))  6.94 us
    ppermute x2, waiting for transfers between devices, ghosts(): before = lax.ppermute(x[1:], 'gx', ring('gx', 1))  5.3 us
    ppermute x2, starting transfers between devices, ghosts(): after = lax.ppermute(x[:, :, :1], 'gz', ring('gz', -1))  4.94 us
    ppermute x5, waiting for transfers between devices, partner(): return lax.ppermute(block, 'gy', [(0, 1), (1, 0)])  3.8 us
  transfers between devices with their start and end apart: 13, of which 9 were waited for; matrix products, arithmetic and copies ran while one was open for 0% of the time, Pallas kernels for 6%

profile of v5, /device:TPU:1, one launch (start us, length us, event | category | flops | bytes accessed | tf_op | source)
XLA Modules:
  0.0 110.6 jit_solution(4899196027462737518)
XLA Ops:
  0.7 1.4 %shard_map.247 = (bf16[128,640]{1,0:T(8,128)(2,1)S(1)}, f32[8,128]{1,0:T(8,128)S(1)}) custom-call(bf16[128,512]{1,0:T(8,128)(2,1)} %bitcast.29, bf16[3,128]{1,0:T(4,128)(2,1)} %bitcast.37, s32[1,384]{1,0:T(1,128)} %bitcast.35, s32[8,14]{1,0:T(8,128)} %bitcast.32), custom_call_target="tpu_custom_call" | custom-call | tf_op jit(solution)/shard_map/pallas_call | solution.py:522
  2.2 3.6 %collective-permute-start = (bf16[2,2,1,16,640]{4,3,2,1,0:T(8,128)(2,1)S(1)}, bf16[2,2,1,16,640]{4,3,2,1,0:T(8,128)(2,1)S(1)}, u32[]{:S(2)}, u32[]{:S(2)}) collective-permute-start(bf16[2,2,1,16,640]{4,3,2,1,0:T(8,128)(2,1)S(1)} %get-tuple-element.47), channel_id=1, source_target_pairs={{0,1},{1,2},{2,3},{3,4},{4,5},{5,6},{6,7},{7,0},{8,9},{9,10},{10,1... | collective-permute-start | bytes 245768 | tf_op jit(solution)/shard_map/ppermute | solution.py:496
  5.8 2.5 %collective-permute-start.1 = (bf16[2,2,1,16,640]{4,3,2,1,0:T(8,128)(2,1)S(1)}, bf16[2,2,1,16,640]{4,3,2,1,0:T(8,128)(2,1)S(1)}, u32[]{:S(2)}, u32[]{:S(2)}) collective-permute-start(bf16[2,2,1,16,640]{4,3,2,1,0:T(8,128)(2,1)S(1)} %get-tuple-element.48), channel_id=1, source_target_pairs={{0,7},{1,0},{2,1},{3,2},{4,3},{5,4},{6,5},{7,6},{8,15},{9,8},{10,9... | collective-permute-start | bytes 245768 | tf_op jit(solution)/shard_map/ppermute | solution.py:497
  8.4 1.7 %collective-permute-done = bf16[2,2,1,16,640]{4,3,2,1,0:T(8,128)(2,1)S(1)} collective-permute-done((bf16[2,2,1,16,640]{4,3,2,1,0:T(8,128)(2,1)S(1)}, bf16[2,2,1,16,640]{4,3,2,1,0:T(8,128)(2,1)S(1)}, u32[]{:S(2)}, u32[]{:S(2)}) %collective-permute-start) | collective-permute-done | bytes 81952 | tf_op jit(solution)/shard_map/ppermute | solution.py:496
  10.1 0.8 collective-permute-done.1
  11.0 0.0 copy-start.23
  11.0 0.0 copy-start.21
  11.0 0.0 copy-start.22
  11.0 2.0 %collective-permute-start.2 = (bf16[1,2,4,16,640]{4,3,2,1,0:T(8,128)(2,1)S(1)}, bf16[1,2,4,16,640]{4,3,2,1,0:T(8,128)(2,1)S(1)}, u32[]{:S(2)}, u32[]{:S(2)}) collective-permute-start(bf16[1,2,4,16,640]{4,3,2,1,0:T(8,128)(2,1)S(1)} %get-tuple-element.43), channel_id=1, source_target_pairs={{0,16},{16,32},{32,48},{48,64},{64,80},{80,96},{96,112},{112,128},... | collective-permute-start | bytes 491528 | tf_op jit(solution)/shard_map/ppermute | solution.py:499
  13.0 4.4 %collective-permute-start.3 = (bf16[1,2,4,16,640]{4,3,2,1,0:T(8,128)(2,1)S(1)}, bf16[1,2,4,16,640]{4,3,2,1,0:T(8,128)(2,1)S(1)}, u32[]{:S(2)}, u32[]{:S(2)}) collective-permute-start(bf16[1,2,4,16,640]{4,3,2,1,0:T(8,128)(2,1)S(1)} %get-tuple-element.44), channel_id=1, source_target_pairs={{0,240},{16,0},{32,16},{48,32},{64,48},{80,64},{96,80},{112,96},{1... | collective-permute-start | bytes 491528 | tf_op jit(solution)/shard_map/ppermute | solution.py:500
  17.5 3.0 %collective-permute-done.2 = bf16[1,2,4,16,640]{4,3,2,1,0:T(8,128)(2,1)S(1)} collective-permute-done((bf16[1,2,4,16,640]{4,3,2,1,0:T(8,128)(2,1)S(1)}, bf16[1,2,4,16,640]{4,3,2,1,0:T(8,128)(2,1)S(1)}, u32[]{:S(2)}, u32[]{:S(2)}) %collective-permute-start.2) | collective-permute-done | bytes 163872 | tf_op jit(solution)/shard_map/ppermute | solution.py:499
  20.4 0.1 pad_maximum_fusion
  20.5 2.2 %collective-permute-start.4 = (bf16[4,2,4,16,640]{4,3,2,1,0:T(8,128)(2,1)S(1)}, bf16[4,2,4,16,640]{4,3,2,1,0:T(8,128)(2,1)S(1)}, u32[]{:S(2)}, u32[]{:S(2)}) collective-permute-start(bf16[4,2,4,16,640]{4,3,2,1,0:T(8,128)(2,1)S(1)} %pad_maximum_fusion), channel_id=1, source_target_pairs={{0,8},{8,0},{1,9},{9,1},{2,10},{10,2},{3,11},{11,3},{4,12},{12,4},... | collective-permute-start | bytes 1966088 | tf_op jit(solution)/shard_map/ppermute | solution.py:490
  22.7 1.7 %collective-permute-done.4 = bf16[4,2,4,16,640]{4,3,2,1,0:T(8,128)(2,1)S(1)} collective-permute-done((bf16[4,2,4,16,640]{4,3,2,1,0:T(8,128)(2,1)S(1)}, bf16[4,2,4,16,640]{4,3,2,1,0:T(8,128)(2,1)S(1)}, u32[]{:S(2)}, u32[]{:S(2)}) %collective-permute-start.4) | collective-permute-done | bytes 655392 | tf_op jit(solution)/shard_map/ppermute | solution.py:490
  24.5 0.0 copy-start.10
  24.5 0.0 copy-start.11
  24.5 0.0 copy-start.13
  24.6 5.0 %shard_map.248 = (bf16[128,512]{1,0:T(8,128)(2,1)S(1)}, bf16[128,512]{1,0:T(8,128)(2,1)S(1)}, f32[48,128]{1,0:T(8,128)S(1)}, bf16[64,2048]{1,0:T(8,128)(2,1)S(1)}, s32[16,128]{1,0:T(8,128)S(1)}) custom-call(bf16[128,512]{1,0:T(8,128)(2,1)S(1)} %bitcast.30, bf16[512,640]{1,0:T(8,128)(2,1)S(1)} %bitcast.18, bf16[512,640]{1,0:T(8,128)(2,1)S(1)} %bitcast.28, ...), custom_call_target="tpu_custom_call" | custom-call | tf_op jit(solution)/shard_map/pallas_call | solution.py:474
  29.6 3.3 %collective-permute-start.5 = (bf16[2,2,1,16,512]{4,3,2,1,0:T(8,128)(2,1)S(1)}, bf16[2,2,1,16,512]{4,3,2,1,0:T(8,128)(2,1)S(1)}, u32[]{:S(2)}, u32[]{:S(2)}) collective-permute-start(bf16[2,2,1,16,512]{4,3,2,1,0:T(8,128)(2,1)S(1)} %get-tuple-element.49), channel_id=1, source_target_pairs={{0,1},{1,2},{2,3},{3,4},{4,5},{5,6},{6,7},{7,0},{8,9},{9,10},{10,1... | collective-permute-start | bytes 196616 | tf_op jit(solution)/shard_map/ppermute | solution.py:496
  32.9 2.4 %collective-permute-start.6 = (bf16[2,2,1,16,512]{4,3,2,1,0:T(8,128)(2,1)S(1)}, bf16[2,2,1,16,512]{4,3,2,1,0:T(8,128)(2,1)S(1)}, u32[]{:S(2)}, u32[]{:S(2)}) collective-permute-start(bf16[2,2,1,16,512]{4,3,2,1,0:T(8,128)(2,1)S(1)} %get-tuple-element.50), channel_id=1, source_target_pairs={{0,7},{1,0},{2,1},{3,2},{4,3},{5,4},{6,5},{7,6},{8,15},{9,8},{10,9... | collective-permute-start | bytes 196616 | tf_op jit(solution)/shard_map/ppermute | solution.py:497
  35.3 2.0 %collective-permute-done.5 = bf16[2,2,1,16,512]{4,3,2,1,0:T(8,128)(2,1)S(1)} collective-permute-done((bf16[2,2,1,16,512]{4,3,2,1,0:T(8,128)(2,1)S(1)}, bf16[2,2,1,16,512]{4,3,2,1,0:T(8,128)(2,1)S(1)}, u32[]{:S(2)}, u32[]{:S(2)}) %collective-permute-start.5) | collective-permute-done | bytes 65568 | tf_op jit(solution)/shard_map/ppermute | solution.py:496
  37.3 0.5 collective-permute-done.6
  37.9 0.1 collective-permute-start.7
  38.0 3.6 %collective-permute-start.8 = (bf16[1,2,4,16,512]{4,3,2,1,0:T(8,128)(2,1)S(1)}, bf16[1,2,4,16,512]{4,3,2,1,0:T(8,128)(2,1)S(1)}, u32[]{:S(2)}, u32[]{:S(2)}) collective-permute-start(bf16[1,2,4,16,512]{4,3,2,1,0:T(8,128)(2,1)S(1)} %get-tuple-element.46), channel_id=1, source_target_pairs={{0,240},{16,0},{32,16},{48,32},{64,48},{80,64},{96,80},{112,96},{1... | collective-permute-start | bytes 393224 | tf_op jit(solution)/shard_map/ppermute | solution.py:500
  41.5 2.4 %collective-permute-done.7 = bf16[1,2,4,16,512]{4,3,2,1,0:T(8,128)(2,1)S(1)} collective-permute-done((bf16[1,2,4,16,512]{4,3,2,1,0:T(8,128)(2,1)S(1)}, bf16[1,2,4,16,512]{4,3,2,1,0:T(8,128)(2,1)S(1)}, u32[]{:S(2)}, u32[]{:S(2)}) %collective-permute-start.7) | collective-permute-done | bytes 131104 | tf_op jit(solution)/shard_map/ppermute | solution.py:499
  43.9 0.1 pad_maximum_fusion.1
  44.0 2.7 %collective-permute-start.9 = (bf16[4,2,4,16,512]{4,3,2,1,0:T(8,128)(2,1)S(1)}, bf16[4,2,4,16,512]{4,3,2,1,0:T(8,128)(2,1)S(1)}, u32[]{:S(2)}, u32[]{:S(2)}) collective-permute-start(bf16[4,2,4,16,512]{4,3,2,1,0:T(8,128)(2,1)S(1)} %pad_maximum_fusion.1), channel_id=1, source_target_pairs={{0,8},{8,0},{1,9},{9,1},{2,10},{10,2},{3,11},{11,3},{4,12},{12,4},... | collective-permute-start | bytes 1572872 | tf_op jit(solution)/shard_map/ppermute | solution.py:490
  46.7 0.3 collective-permute-start.10
  47.0 1.2 %collective-permute-done.9 = bf16[4,2,4,16,512]{4,3,2,1,0:T(8,128)(2,1)S(1)} collective-permute-done((bf16[4,2,4,16,512]{4,3,2,1,0:T(8,128)(2,1)S(1)}, bf16[4,2,4,16,512]{4,3,2,1,0:T(8,128)(2,1)S(1)}, u32[]{:S(2)}, u32[]{:S(2)}) %collective-permute-start.9) | collective-permute-done | bytes 524320 | tf_op jit(solution)/shard_map/ppermute | solution.py:490
  48.2 0.0 copy-start.5
  48.2 0.0 copy-start.6
  48.2 0.0 copy-start.7
  48.3 0.0 copy-start.8
  48.3 0.0 copy-start.9
  48.3 0.0 copy-start.12
  48.3 0.0 copy-start.16
  48.3 0.0 copy-start.20
  48.3 5.5 %shard_map.249 = (bf16[128,512]{1,0:T(8,128)(2,1)}, f32[1,128]{1,0:T(1,128)S(1)}, f32[1,128]{1,0:T(1,128)S(1)}) custom-call(bf16[128,512]{1,0:T(8,128)(2,1)S(1)} %get-tuple-element.21.feats, bf16[512,512]{1,0:T(8,128)(2,1)S(1)} %bitcast.19, bf16[512,512]{1,0:T(8,128)(2,1)S(1)} %bitcast.31, s32[16,128]{1,0:T(8,128)S(1)} %get-tuple-element.23.rows, ...), custom_call_target="tpu_custom_call" | custom-call | tf_op jit(solution)/shard_map/pallas_call | solution.py:474
  53.9 0.4 collective-permute-start.11
  54.3 0.9 shard_map.250
  55.2 0.8 shard_map.251
  56.0 25.4 %all_to_all.10 = bf16[128,8,128]{2,1,0:T(8,128)(2,1)S(1)} all-to-all(bf16[128,8,128]{2,1,0:T(8,128)(2,1)S(1)} %shard_map.251), channel_id=1, replica_groups=mesh['gx'=16,'gy'=2,'gz'=8] {'gz','gx'}, dimensions={0} | all-to-all | bytes 524288 | tf_op jit(solution)/shard_map/all_to_all | solution.py:506
  81.5 4.9 %shard_map.252 = bf16[8,128,128]{2,1,0:T(8,128)(2,1)S(1)} custom-call(f32[256]{0:T(256)S(1)} %copy-done.20, bf16[8,128,128]{2,1,0:T(8,128)(2,1)S(1)} %bitcast.26, bf16[1024,256]{1,0:T(8,128)(2,1)S(1)} %copy-done.4, bf16[1024,256]{1,0:T(8,128)(2,1)S(1)} %copy-done.3, bf16[3,256,128]{2,1,0:T(8,128)(2,1)S(1)} %copy-done.8, bf16[3,256,128]{2,1,0:T(8,128)(2,1)S(1)} %copy-done.7, ...), custom_call_target="tpu_custom_call" | custom-call | tf_op jit(solution)/shard_map/pallas_call | solution.py:474
  86.4 19.1 %all_to_all.11.returned = bf16[128,8,128]{2,1,0:T(8,128)(2,1)S(1)} all-to-all(bf16[128,8,128]{2,1,0:T(8,128)(2,1)S(1)} %bitcast.27), channel_id=1, replica_groups=mesh['gx'=16,'gy'=2,'gz'=8] {'gz','gx'}, dimensions={0} | all-to-all | bytes 524288 | tf_op jit(solution)/shard_map/all_to_all | solution.py:506
  105.6 0.7 shard_map.253
  106.3 2.8 %collective-permute-start.12 = (f32[8,128]{1,0:T(8,128)S(1)}, f32[8,128]{1,0:T(8,128)S(1)}, u32[]{:S(2)}, u32[]{:S(2)}) collective-permute-start(f32[8,128]{1,0:T(8,128)S(1)} %get-tuple-element.33), channel_id=1, source_target_pairs={{0,8},{8,0},{1,9},{9,1},{2,10},{10,2},{3,11},{11,3},{4,12},{12,4},... | collective-permute-start | bytes 12296 | tf_op jit(solution)/shard_map/ppermute | solution.py:490
  109.2 0.8 collective-permute-done.12.there
  110.0 0.6 shard_map.254
  (45 shorter events, 0.2 us)
Async XLA Ops:
  0.6 23.8 %copy-start.14 = (s32[1,1,1,8,14]{4,3,2,1,0:T(8,128)S(1)}, s32[1,1,1,8,14]{4,3,2,1,0:T(8,128)}, u32[]{:S(2)}) copy-start(s32[1,1,1,8,14]{4,3,2,1,0:T(8,128)} %param.28) | copy-start | bytes 1348
  0.6 23.8 %copy-start.17 = (s32[1,1,1,3,128]{4,2,3,1,0:T(1,128)S(1)}, s32[1,1,1,3,128]{4,2,3,1,0:T(1,128)}, u32[]{:S(2)}) copy-start(s32[1,1,1,3,128]{4,2,3,1,0:T(1,128)} %param.26) | copy-start | bytes 4612
  0.7 23.8 %copy-start.19 = (bf16[1,1,1,3,128]{4,3,2,1,0:T(4,128)(2,1)S(1)}, bf16[1,1,1,3,128]{4,3,2,1,0:T(4,128)(2,1)}, u32[]{:S(2)}) copy-start(bf16[1,1,1,3,128]{4,3,2,1,0:T(4,128)(2,1)} %param.25) | copy-start | bytes 2308
  0.7 23.8 %copy-start.2 = (bf16[1,1,1,128,512]{4,3,2,1,0:T(8,128)(2,1)S(1)}, bf16[1,1,1,128,512]{4,3,2,1,0:T(8,128)(2,1)}, u32[]{:S(2)}) copy-start(bf16[1,1,1,128,512]{4,3,2,1,0:T(8,128)(2,1)} %param.24) | copy-start | bytes 393220
  0.7 23.8 %copy-start.1 = (bf16[2,2,128,128]{3,2,1,0:T(8,128)(2,1)S(1)}, bf16[2,2,128,128]{3,2,1,0:T(8,128)(2,1)}, u32[]{:S(2)}) copy-start(bf16[2,2,128,128]{3,2,1,0:T(8,128)(2,1)} %mix_weight.3) | copy-start | bytes 393220
  0.7 23.8 %copy-start = (bf16[2,64,512]{2,1,0:T(8,128)(2,1)S(1)}, bf16[2,64,512]{2,1,0:T(8,128)(2,1)}, u32[]{:S(2)}) copy-start(bf16[2,64,512]{2,1,0:T(8,128)(2,1)} %radial_out.3) | copy-start | bytes 393220
  0.7 23.8 %copy-start.18 = (bf16[2,8,64]{2,1,0:T(8,128)(2,1)S(1)}, bf16[2,8,64]{2,1,0:T(8,128)(2,1)}, u32[]{:S(2)}) copy-start(bf16[2,8,64]{2,1,0:T(8,128)(2,1)} %radial_in.1) | copy-start | bytes 6148
  0.7 23.8 %copy-start.15 = (s32[1,1,1,16,128]{4,3,2,1,0:T(8,128)S(1)}, s32[1,1,1,16,128]{4,3,2,1,0:T(8,128)}, u32[]{:S(2)}) copy-start(s32[1,1,1,16,128]{4,3,2,1,0:T(8,128)} %param.29) | copy-start | bytes 24580
  2.2 7.9 %collective-permute-start = (bf16[2,2,1,16,640]{4,3,2,1,0:T(8,128)(2,1)S(1)}, bf16[2,2,1,16,640]{4,3,2,1,0:T(8,128)(2,1)S(1)}, u32[]{:S(2)}, u32[]{:S(2)}) collective-permute-start(bf16[2,2,1,16,640]{4,3,2,1,0:T(8,128)(2,1)S(1)} %get-tuple-element.47), channel_id=1, source_target_pairs={{0,1},{1,2},{2,3},{3,4},{4,5},{5,6},{6,7},{7,0},{8,9},{9,10},{10,1... | collective-permute-start | bytes 245768 | tf_op jit(solution)/shard_map/ppermute | solution.py:496
  5.8 5.1 %collective-permute-start.1 = (bf16[2,2,1,16,640]{4,3,2,1,0:T(8,128)(2,1)S(1)}, bf16[2,2,1,16,640]{4,3,2,1,0:T(8,128)(2,1)S(1)}, u32[]{:S(2)}, u32[]{:S(2)}) collective-permute-start(bf16[2,2,1,16,640]{4,3,2,1,0:T(8,128)(2,1)S(1)} %get-tuple-element.48), channel_id=1, source_target_pairs={{0,7},{1,0},{2,1},{3,2},{4,3},{5,4},{6,5},{7,6},{8,15},{9,8},{10,9... | collective-permute-start | bytes 245768 | tf_op jit(solution)/shard_map/ppermute | solution.py:497
  11.0 36.0 %copy-start.23 = (bf16[128,2]{0,1:T(2,128)(2,1)S(1)}, bf16[128,2]{0,1:T(2,128)(2,1)}, u32[]{:S(2)}) copy-start(bf16[128,2]{0,1:T(2,128)(2,1)} %param.33) | copy-start | bytes 1540
  11.0 37.2 %copy-start.21 = (f32[2,2]{1,0:T(2,128)S(1)}, f32[2,2]{1,0:T(2,128)}, u32[]{:S(2)}) copy-start(f32[2,2]{1,0:T(2,128)} %species_table.1) | copy-start | bytes 52
  11.0 37.2 %copy-start.22 = (s32[1,1,1,128]{3,2,1,0:T(1,128)S(1)}, s32[1,1,1,128]{3,2,1,0:T(1,128)}, u32[]{:S(2)}) copy-start(s32[1,1,1,128]{3,2,1,0:T(1,128)} %param.27) | copy-start | bytes 1540
  11.0 9.4 %collective-permute-start.2 = (bf16[1,2,4,16,640]{4,3,2,1,0:T(8,128)(2,1)S(1)}, bf16[1,2,4,16,640]{4,3,2,1,0:T(8,128)(2,1)S(1)}, u32[]{:S(2)}, u32[]{:S(2)}) collective-permute-start(bf16[1,2,4,16,640]{4,3,2,1,0:T(8,128)(2,1)S(1)} %get-tuple-element.43), channel_id=1, source_target_pairs={{0,16},{16,32},{32,48},{48,64},{64,80},{80,96},{96,112},{112,128},... | collective-permute-start | bytes 491528 | tf_op jit(solution)/shard_map/ppermute | solution.py:499
  13.0 7.4 %collective-permute-start.3 = (bf16[1,2,4,16,640]{4,3,2,1,0:T(8,128)(2,1)S(1)}, bf16[1,2,4,16,640]{4,3,2,1,0:T(8,128)(2,1)S(1)}, u32[]{:S(2)}, u32[]{:S(2)}) collective-permute-start(bf16[1,2,4,16,640]{4,3,2,1,0:T(8,128)(2,1)S(1)} %get-tuple-element.44), channel_id=1, source_target_pairs={{0,240},{16,0},{32,16},{48,32},{64,48},{80,64},{96,80},{112,96},{1... | collective-permute-start | bytes 491528 | tf_op jit(solution)/shard_map/ppermute | solution.py:500
  20.5 3.9 %collective-permute-start.4 = (bf16[4,2,4,16,640]{4,3,2,1,0:T(8,128)(2,1)S(1)}, bf16[4,2,4,16,640]{4,3,2,1,0:T(8,128)(2,1)S(1)}, u32[]{:S(2)}, u32[]{:S(2)}) collective-permute-start(bf16[4,2,4,16,640]{4,3,2,1,0:T(8,128)(2,1)S(1)} %pad_maximum_fusion), channel_id=1, source_target_pairs={{0,8},{8,0},{1,9},{9,1},{2,10},{10,2},{3,11},{11,3},{4,12},{12,4},... | collective-permute-start | bytes 1966088 | tf_op jit(solution)/shard_map/ppermute | solution.py:490
  24.5 29.7 %copy-start.10 = (bf16[256,256]{1,0:T(8,128)(2,1)S(1)}, bf16[256,256]{1,0:T(8,128)(2,1)}, u32[]{:S(2)}) copy-start(bf16[256,256]{1,0:T(8,128)(2,1)} %constant.30.clone.low) | copy-start | bytes 393220
  24.5 29.7 %copy-start.11 = (bf16[256,256]{1,0:T(8,128)(2,1)S(1)}, bf16[256,256]{1,0:T(8,128)(2,1)}, u32[]{:S(2)}) copy-start(bf16[256,256]{1,0:T(8,128)(2,1)} %constant.29.clone.high) | copy-start | bytes 393220
  24.5 30.7 %copy-start.13 = (bf16[128,128]{1,0:T(8,128)(2,1)S(1)}, bf16[128,128]{1,0:T(8,128)(2,1)}, u32[]{:S(2)}) copy-start(bf16[128,128]{1,0:T(8,128)(2,1)} %constant.31.clone.carry) | copy-start | bytes 98308
  29.6 7.7 %collective-permute-start.5 = (bf16[2,2,1,16,512]{4,3,2,1,0:T(8,128)(2,1)S(1)}, bf16[2,2,1,16,512]{4,3,2,1,0:T(8,128)(2,1)S(1)}, u32[]{:S(2)}, u32[]{:S(2)}) collective-permute-start(bf16[2,2,1,16,512]{4,3,2,1,0:T(8,128)(2,1)S(1)} %get-tuple-element.49), channel_id=1, source_target_pairs={{0,1},{1,2},{2,3},{3,4},{4,5},{5,6},{6,7},{7,0},{8,9},{9,10},{10,1... | collective-permute-start | bytes 196616 | tf_op jit(solution)/shard_map/ppermute | solution.py:496
  32.9 4.9 %collective-permute-start.6 = (bf16[2,2,1,16,512]{4,3,2,1,0:T(8,128)(2,1)S(1)}, bf16[2,2,1,16,512]{4,3,2,1,0:T(8,128)(2,1)S(1)}, u32[]{:S(2)}, u32[]{:S(2)}) collective-permute-start(bf16[2,2,1,16,512]{4,3,2,1,0:T(8,128)(2,1)S(1)} %get-tuple-element.50), channel_id=1, source_target_pairs={{0,7},{1,0},{2,1},{3,2},{4,3},{5,4},{6,5},{7,6},{8,15},{9,8},{10,9... | collective-permute-start | bytes 196616 | tf_op jit(solution)/shard_map/ppermute | solution.py:497
  37.9 6.0 %collective-permute-start.7 = (bf16[1,2,4,16,512]{4,3,2,1,0:T(8,128)(2,1)S(1)}, bf16[1,2,4,16,512]{4,3,2,1,0:T(8,128)(2,1)S(1)}, u32[]{:S(2)}, u32[]{:S(2)}) collective-permute-start(bf16[1,2,4,16,512]{4,3,2,1,0:T(8,128)(2,1)S(1)} %get-tuple-element.45), channel_id=1, source_target_pairs={{0,16},{16,32},{32,48},{48,64},{64,80},{80,96},{96,112},{112,128},... | collective-permute-start | bytes 393224 | tf_op jit(solution)/shard_map/ppermute | solution.py:499
  38.0 5.9 %collective-permute-start.8 = (bf16[1,2,4,16,512]{4,3,2,1,0:T(8,128)(2,1)S(1)}, bf16[1,2,4,16,512]{4,3,2,1,0:T(8,128)(2,1)S(1)}, u32[]{:S(2)}, u32[]{:S(2)}) collective-permute-start(bf16[1,2,4,16,512]{4,3,2,1,0:T(8,128)(2,1)S(1)} %get-tuple-element.46), channel_id=1, source_target_pairs={{0,240},{16,0},{32,16},{48,32},{64,48},{80,64},{96,80},{112,96},{1... | collective-permute-start | bytes 393224 | tf_op jit(solution)/shard_map/ppermute | solution.py:500
  44.0 4.2 %collective-permute-start.9 = (bf16[4,2,4,16,512]{4,3,2,1,0:T(8,128)(2,1)S(1)}, bf16[4,2,4,16,512]{4,3,2,1,0:T(8,128)(2,1)S(1)}, u32[]{:S(2)}, u32[]{:S(2)}) collective-permute-start(bf16[4,2,4,16,512]{4,3,2,1,0:T(8,128)(2,1)S(1)} %pad_maximum_fusion.1), channel_id=1, source_target_pairs={{0,8},{8,0},{1,9},{9,1},{2,10},{10,2},{3,11},{11,3},{4,12},{12,4},... | collective-permute-start | bytes 1572872 | tf_op jit(solution)/shard_map/ppermute | solution.py:490
  46.7 7.6 %collective-permute-start.10 = (f32[8,128]{1,0:T(8,128)S(1)}, f32[8,128]{1,0:T(8,128)S(1)}, u32[]{:S(2)}, u32[]{:S(2)}) collective-permute-start(f32[8,128]{1,0:T(8,128)S(1)} %get-tuple-element.27.own), channel_id=1, source_target_pairs={{0,8},{8,0},{1,9},{9,1},{2,10},{10,2},{3,11},{11,3},{4,12},{12,4},... | collective-permute-start | bytes 12296 | tf_op jit(solution)/shard_map/ppermute | solution.py:490
  48.2 33.2 %copy-start.3 = (bf16[1024,256]{1,0:T(8,128)(2,1)S(1)}, bf16[1024,256]{1,0:T(8,128)(2,1)}, u32[]{:S(2)}) copy-start(bf16[1024,256]{1,0:T(8,128)(2,1)} %constant.34.clone.zl) | copy-start | bytes 1572868
  48.2 33.2 %copy-start.4 = (bf16[1024,256]{1,0:T(8,128)(2,1)S(1)}, bf16[1024,256]{1,0:T(8,128)(2,1)}, u32[]{:S(2)}) copy-start(bf16[1024,256]{1,0:T(8,128)(2,1)} %constant.33.clone.zh) | copy-start | bytes 1572868
  48.2 33.2 %copy-start.5 = (bf16[3,128,256]{2,1,0:T(8,128)(2,1)S(1)}, bf16[3,128,256]{2,1,0:T(8,128)(2,1)}, u32[]{:S(2)}) copy-start(bf16[3,128,256]{2,1,0:T(8,128)(2,1)} %constant.38.clone.tl) | copy-start | bytes 589828
  48.2 33.2 %copy-start.6 = (bf16[3,128,256]{2,1,0:T(8,128)(2,1)S(1)}, bf16[3,128,256]{2,1,0:T(8,128)(2,1)}, u32[]{:S(2)}) copy-start(bf16[3,128,256]{2,1,0:T(8,128)(2,1)} %constant.37.clone.th) | copy-start | bytes 589828
  48.2 33.2 %copy-start.7 = (bf16[3,256,128]{2,1,0:T(8,128)(2,1)S(1)}, bf16[3,256,128]{2,1,0:T(8,128)(2,1)}, u32[]{:S(2)}) copy-start(bf16[3,256,128]{2,1,0:T(8,128)(2,1)} %constant.36.clone.xl) | copy-start | bytes 589828
  48.3 33.2 %copy-start.8 = (bf16[3,256,128]{2,1,0:T(8,128)(2,1)S(1)}, bf16[3,256,128]{2,1,0:T(8,128)(2,1)}, u32[]{:S(2)}) copy-start(bf16[3,256,128]{2,1,0:T(8,128)(2,1)} %constant.35.clone.xh) | copy-start | bytes 589828
  48.3 33.2 %copy-start.9 = (f32[256,2]{1,0:T(8,128)S(1)}, f32[256,2]{1,0:T(8,128)}, u32[]{:S(2)}) copy-start(f32[256,2]{1,0:T(8,128)} %constant.39.clone.col) | copy-start | bytes 6148
  48.3 33.2 %copy-start.12 = (bf16[2,128,128]{2,1,0:T(8,128)(2,1)S(1)}, bf16[2,128,128]{2,1,0:T(8,128)(2,1)}, u32[]{:S(2)}) copy-start(bf16[2,128,128]{2,1,0:T(8,128)(2,1)} %constant.41.clone.lines) | copy-start | bytes 196612
  48.3 33.2 %copy-start.16 = (f32[8,256]{1,0:T(8,128)S(1)}, f32[8,256]{1,0:T(8,128)}, u32[]{:S(2)}) copy-start(f32[8,256]{1,0:T(8,128)} %constant.40.clone.row) | copy-start | bytes 24580
  48.3 33.2 %copy-start.20 = (f32[256]{0:T(256)S(1)}, f32[256]{0:T(256)}, u32[]{:S(2)}) copy-start(f32[256]{0:T(256)} %constant.32.clone.scale_y) | copy-start | bytes 3076
  53.9 1.3 %collective-permute-start.11 = (f32[1,128]{1,0:T(1,128)S(1)}, f32[1,128]{1,0:T(1,128)S(1)}, u32[]{:S(2)}, u32[]{:S(2)}) collective-permute-start(f32[1,128]{1,0:T(1,128)S(1)} %get-tuple-element.31.own.charge), channel_id=1, source_target_pairs={{0,8},{8,0},{1,9},{9,1},{2,10},{10,2},{3,11},{11,3},{4,12},{12,4},... | collective-permute-start | bytes 1544 | tf_op jit(solution)/shard_map/ppermute | solution.py:490
  106.3 3.7 %collective-permute-start.12 = (f32[8,128]{1,0:T(8,128)S(1)}, f32[8,128]{1,0:T(8,128)S(1)}, u32[]{:S(2)}, u32[]{:S(2)}) collective-permute-start(f32[8,128]{1,0:T(8,128)S(1)} %get-tuple-element.33), channel_id=1, source_target_pairs={{0,8},{8,0},{1,9},{9,1},{2,10},{10,2},{3,11},{11,3},{4,12},{12,4},... | collective-permute-start | bytes 12296 | tf_op jit(solution)/shard_map/ppermute | solution.py:490
